TPU v7x, 128 devices: a whole 4x4x4 slice. The times are simulated.
128 devices in a mesh: dp: 1, yz: 16 (over z, y), x: 8 (over x, core).
Axes of the slice: x: 4, y: 4, z: 4, core: 2. Of those that a mesh axis runs over, the one named last changes fastest.
Arguments:
- x_in: bfloat16 [8192, 2816], P('dp', ('x', 'yz'))
- ln_gain: bfloat16 [2816], P(('x', 'yz'))
- w_qkv: bfloat16 [2816, 3072], P('x', 'yz')
- w_gate: bfloat16 [2816, 11264], P('x', 'yz')
- w_up: bfloat16 [2816, 11264], P('x', 'yz')
- w_attn_out: bfloat16 [2816, 2816], P('yz', 'x')
- w_mlp_out: bfloat16 [11264, 2816], P('yz', 'x')
- k_cache: bfloat16 [8192, 128, 128], P(('dp', 'x', 'yz'))
- v_cache: bfloat16 [8192, 128, 128], P(('dp', 'x', 'yz'))
- ctx_len: int32 [8192], P(('dp', 'x', 'yz'))
Outputs:
- output 1: bfloat16 [8192, 2816], P('dp', ('x', 'yz'))
- output 2: bfloat16 [8192, 128, 128], P(('dp', 'x', 'yz'))
- output 3: bfloat16 [8192, 128, 128], P(('dp', 'x', 'yz'))
All inputs are finite; a program needn't handle non-finite values.
Results may differ from a plain program's by a relative error of at most 0.00711414.
Values are sent between devices in bfloat16 or wider.
A program may use at most 1 GiB of HBM per device.

v0:
```python
import jax
import jax.numpy as jnp
from jax import lax
from jax.sharding import PartitionSpec as P


def apply_rope(vecs, positions):
    half_dim = vecs.shape[-1] // 2
    inv_freq = 10000.0 ** (-jnp.arange(half_dim, dtype=jnp.float32) / half_dim)
    angles = positions.astype(jnp.float32)[..., None] * inv_freq
    cos_t = jnp.cos(angles)
    sin_t = jnp.sin(angles)
    first_half = vecs[..., :half_dim]
    second_half = vecs[..., half_dim:]
    return jnp.concatenate([first_half * cos_t - second_half * sin_t, second_half * cos_t + first_half * sin_t], axis=-1)


def attend_local(q_rot, k_all, v_all, ctx_len):
    head_dim = q_rot.shape[-1]
    positions = jnp.arange(k_all.shape[1])
    scores = jnp.einsum("bhd,btd->bht", q_rot, k_all, preferred_element_type=jnp.float32) * head_dim ** -0.5
    visible = (positions[None, :] <= ctx_len[:, None])[:, None, :]
    scores = jnp.where(visible, scores, -1e30)
    attn_probs = jax.nn.softmax(scores, axis=-1).astype(jnp.bfloat16)
    return jnp.einsum("bht,btd->bhd", attn_probs, v_all, preferred_element_type=jnp.float32).astype(jnp.bfloat16)


def solution(mesh):
    x_size = mesh.shape["x"]
    yz_size = mesh.shape["yz"]
    both_axes = ("x", "yz")
    row_spec = P("dp", both_axes)
    in_w_spec = P("x", "yz")
    out_w_spec = P("yz", "x")
    cache_spec = P(("dp", "x", "yz"), None, None)
    len_spec = P(("dp", "x", "yz"))

    def local_layer(x_loc, gain_loc, wqkv_loc, wgate_loc, wup_loc, wao_loc, wmo_loc, kc_loc, vc_loc, len_loc):
        d_model = x_loc.shape[1] * x_size * yz_size
        head_dim = kc_loc.shape[2]
        dev_rows = kc_loc.shape[0]
        attn_cols = wao_loc.shape[0] * yz_size
        num_heads = attn_cols // head_dim
        x_f32 = x_loc.astype(jnp.float32)
        row_stats = jnp.stack([jnp.sum(x_f32, axis=1), jnp.sum(x_f32 * x_f32, axis=1)], axis=1)
        row_stats = lax.psum(row_stats, both_axes)
        row_mean = row_stats[:, 0:1] / d_model
        row_var = row_stats[:, 1:2] / d_model - row_mean * row_mean
        normed = ((x_f32 - row_mean) * lax.rsqrt(row_var + 1e-6) * gain_loc.astype(jnp.float32)).astype(jnp.bfloat16)
        normed_rows = lax.all_gather(normed, "yz", axis=1, tiled=True)
        qkv_part = jnp.dot(normed_rows, wqkv_loc, preferred_element_type=jnp.float32)
        gate_part = jnp.dot(normed_rows, wgate_loc, preferred_element_type=jnp.float32)
        up_part = jnp.dot(normed_rows, wup_loc, preferred_element_type=jnp.float32)
        qkv_rows = lax.psum_scatter(qkv_part, "x", scatter_dimension=0, tiled=True).astype(jnp.bfloat16)
        gate_rows = lax.psum_scatter(gate_part, "x", scatter_dimension=0, tiled=True).astype(jnp.bfloat16)
        up_rows = lax.psum_scatter(up_part, "x", scatter_dimension=0, tiled=True).astype(jnp.bfloat16)
        mlp_rows = (jax.nn.silu(gate_rows.astype(jnp.float32)) * up_rows.astype(jnp.float32)).astype(jnp.bfloat16)
        qkv_dev = lax.all_to_all(qkv_rows, "yz", 0, 1, tiled=True)
        q_heads = qkv_dev[:, :attn_cols].reshape(dev_rows, num_heads, head_dim)
        k_new = qkv_dev[:, attn_cols:attn_cols + head_dim]
        v_new = qkv_dev[:, attn_cols + head_dim:]
        q_rot = apply_rope(q_heads.astype(jnp.float32), len_loc[:, None]).astype(jnp.bfloat16)
        k_rot = apply_rope(k_new.astype(jnp.float32), len_loc).astype(jnp.bfloat16)
        new_slot = (jnp.arange(kc_loc.shape[1])[None, :] == len_loc[:, None])[:, :, None]
        k_all = jnp.where(new_slot, k_rot[:, None, :], kc_loc)
        v_all = jnp.where(new_slot, v_new[:, None, :], vc_loc)
        attn_dev = attend_local(q_rot, k_all, v_all, len_loc).reshape(dev_rows, attn_cols)
        attn_rows = lax.all_to_all(attn_dev, "yz", 1, 0, tiled=True)
        attn_full = lax.all_gather(attn_rows, "x", axis=0, tiled=True)
        mlp_full = lax.all_gather(mlp_rows, "x", axis=0, tiled=True)
        z_part = jnp.dot(attn_full, wao_loc, preferred_element_type=jnp.float32) + jnp.dot(mlp_full, wmo_loc, preferred_element_type=jnp.float32)
        z_loc = lax.psum_scatter(z_part, "yz", scatter_dimension=1, tiled=True)
        y_loc = (x_f32 + z_loc).astype(jnp.bfloat16)
        return y_loc, k_all, v_all

    in_specs = (row_spec, P(both_axes), in_w_spec, in_w_spec, in_w_spec, out_w_spec, out_w_spec, cache_spec, cache_spec, len_spec)
    out_specs = (row_spec, cache_spec, cache_spec)
    return jax.shard_map(local_layer, mesh=mesh, in_specs=in_specs, out_specs=out_specs, check_vma=False)
```

profile of v0, /device:TPU:1, one launch (start us, length us, event | category | flops | bytes accessed | tf_op | source)
XLA Modules:
  0.0 931.6 jit_solution(11359693497538059027)
XLA Ops:
  7.2 0.0 all-reduce.4.cloned.1.call-start
  7.2 1.3 convert_reduce_fusion
  8.5 0.7 pad_maximum_fusion
  9.2 0.0 all-reduce.4.cloned.1.call-update
  9.2 0.0 all-gather.9.cloned.1.call-start
  9.3 0.7 convert_element_type.57
  9.9 152.2 %all-reduce.4.cloned.1.call-done = f32[8192,2]{0,1:T(2,128)} async-done(((f32[8192,2]{0,1:T(2,128)}), f32[8192,2]{0,1:T(2,128)}) %all-reduce.4.cloned.1.call-update) | async-done | bytes 65552 | tf_op jit(solution)/shard_map/psum | solution.py:46
  162.2 1.0 slice_multiply_fusion.1
  163.2 1.9 fusion.15
  165.1 0.0 all-gather.9.cloned.1.call-update
  165.1 0.0 reduce-scatter.10.cloned.1.call-start
  165.1 59.5 %all-gather.9.cloned.1.call-done = bf16[16,22,8192]{2,1,0:T(8,128)(2,1)} async-done(((bf16[1,22,8192]{2,1,0:T(8,128)(2,1)}), bf16[16,22,8192]{2,1,0:T(8,128)(2,1)}) %all-gather.9.cloned.1.call-update) | async-done | bytes 5767184 | tf_op jit(solution)/shard_map/all_gather | solution.py:50
  224.6 6.4 reshape.143
  231.0 13.8 %fusion.25 = f32[8192,704]{0,1:T(8,128)} fusion(bf16[352,8192]{1,0:T(8,128)(2,1)} %reshape.143, bf16[352,704]{1,0:T(8,128)(2,1)S(1)} %copy-done), kind=kOutput, calls=%fused_computation.52 | convolution fusion | flops 4060086272 | bytes 29331456 | tf_op jit(solution)/shard_map/dot_general | solution.py:53
  244.7 0.0 reduce-scatter.10.cloned.1.call-update
  244.8 0.0 reduce-scatter.8.cloned.1.call-start
  244.8 1.0 copy-done.4
  245.8 13.7 %fusion.24 = f32[8192,704]{0,1:T(8,128)} fusion(bf16[352,8192]{1,0:T(8,128)(2,1)} %reshape.143, bf16[352,704]{1,0:T(8,128)(2,1)S(1)} %copy-done.4), kind=kOutput, calls=%fused_computation.51 | convolution fusion | flops 4060086272 | bytes 29331456 | tf_op jit(solution)/shard_map/dot_general | solution.py:52
  259.5 0.0 reduce-scatter.8.cloned.1.call-update
  259.5 0.0 reduce-scatter.6.cloned.1.call-start
  259.6 0.8 copy-done.5
  260.4 7.0 fusion.27
  267.4 0.0 reduce-scatter.6.cloned.1.call-update
  267.5 0.0 all-gather.7.cloned.1.call-start
  267.5 98.3 %reduce-scatter.10.cloned.1.call-done = f32[1024,704]{0,1:T(8,128)} async-done(((f32[8192,704]{0,1:T(8,128)}), f32[1024,704]{0,1:T(8,128)}) %reduce-scatter.10.cloned.1.call-update) | async-done | bytes 2883600 | tf_op jit(solution)/shard_map/reduce_scatter | solution.py:56
  365.8 123.5 %reduce-scatter.8.cloned.1.call-done = f32[1024,704]{0,1:T(8,128)} async-done(((f32[8192,704]{0,1:T(8,128)}), f32[1024,704]{0,1:T(8,128)}) %reduce-scatter.8.cloned.1.call-update) | async-done | bytes 2883600 | tf_op jit(solution)/shard_map/reduce_scatter | solution.py:55
  489.3 4.7 fusion.6
  494.1 39.8 %reduce-scatter.6.cloned.1.call-done = f32[1024,192]{0,1:T(8,128)} async-done(((f32[8192,192]{0,1:T(8,128)}), f32[1024,192]{0,1:T(8,128)}) %reduce-scatter.6.cloned.1.call-update) | async-done | bytes 786448 | tf_op jit(solution)/shard_map/reduce_scatter | solution.py:54
  533.9 1.2 convert_element_type.59
  535.0 1.0 copy.16
  536.0 6.7 all-to-all-start
  542.7 0.2 all-gather.5.cloned.1.call-start
  543.0 0.1 iota_compare_fusion.1
  543.1 9.8 %all-to-all-done = bf16[16,64,192]{2,1,0:T(8,128)(2,1)S(1)} async-done(((bf16[16,64,192]{2,1,0:T(8,128)(2,1)}), bf16[16,64,192]{2,1,0:T(8,128)(2,1)S(1)}, u32[]{:S(2)}, u32[]{:S(2)}) %all-to-all-start) | async-done | bytes 393248 | tf_op jit(solution)/shard_map/all_to_all | solution.py:58
  552.9 0.3 copy.17
  553.2 0.5 all_to_all.31
  553.8 0.1 reshape.141
  554.0 0.2 multiply_cosine_fusion
  554.2 0.1 pad_maximum_fusion.1
  554.2 0.4 subtract_convert_fusion
  554.6 4.8 broadcast_select_fusion.1
  559.4 1.2 fusion.9
  560.6 0.5 fusion.23
  561.1 5.1 convolution_convert_fusion
  566.2 1.9 all_to_all.32
  568.1 0.2 copy.18
  568.3 13.7 %all_to_all.38 = bf16[64,16,176]{2,0,1:T(8,128)(2,1)} all-to-all(bf16[64,16,176]{2,0,1:T(8,128)(2,1)S(1)} %copy.18), channel_id=1, replica_groups=mesh['dp'=1,'yz'=16,'x'=8] {'yz'}, dimensions={1} | all-to-all | bytes 720896 | tf_op jit(solution)/shard_map/all_to_all | solution.py:68
  582.0 0.0 all-gather.5.cloned.1.call-update
  582.0 16.8 %all-gather.7.cloned.1.call-done = bf16[8192,704]{0,1:T(8,128)(2,1)} async-done(((bf16[1024,704]{0,1:T(8,128)(2,1)}), bf16[8192,704]{0,1:T(8,128)(2,1)}) %all-gather.7.cloned.1.call-update) | async-done | bytes 11534352 | tf_op jit(solution)/shard_map/all_gather | solution.py:70
  598.8 13.3 %fusion.26 = f32[8192,352]{0,1:T(8,128)} fusion(bf16[8192,704]{0,1:T(8,128)(2,1)} %all-gather.7.cloned.1.call-done, bf16[704,352]{1,0:T(8,128)(2,1)} %param.16), kind=kOutput, calls=%fused_computation.53 | convolution fusion | flops 4060086272 | bytes 23564288 | tf_op jit(solution)/shard_map/dot_general | solution.py:71
  612.1 20.6 %all-gather.5.cloned.1.call-done = bf16[8192,176]{1,0:T(8,128)(2,1)} async-done(((bf16[1024,176]{1,0:T(8,128)(2,1)}), bf16[8192,176]{1,0:T(8,128)(2,1)}) %all-gather.5.cloned.1.call-update) | async-done | bytes 2883600 | tf_op jit(solution)/shard_map/all_gather | solution.py:69
  632.7 11.5 %convolution_add_fusion = f32[8192,352]{0,1:T(8,128)} fusion(f32[8192,352]{0,1:T(8,128)} %fusion.26, bf16[8192,176]{1,0:T(8,128)(2,1)} %all-gather.5.cloned.1.call-done, bf16[176,352]{1,0:T(8,128)(2,1)S(1)} %copy-done.6), kind=kOutput, calls=%fused_computation.1 | convolution fusion | flops 1017905152 | bytes 26076160 | tf_op jit(solution)/shard_map/dot_general | solution.py:71
  644.2 144.6 %fusion = f32[8192,32]{0,1:T(8,128)S(1)} fusion(f32[8192,352]{0,1:T(8,128)} %convolution_add_fusion), kind=kCustom, calls=%all-reduce-scatter | all-reduce-scatter fusion | flops 4194305 | bytes 12583424
  788.8 1.4 collective-permute-start.3
  790.2 5.0 collective-permute-start.2
  795.1 3.3 collective-permute-start.1
  798.4 2.7 collective-permute-start
  801.2 1.0 slice.45
  802.1 2.8 collective-permute-start.4
  804.9 0.6 dynamic-slice.4
  806.2 50.5 %collective-permute-done.4 = f32[8192,22]{0,1:T(8,128)} collective-permute-done((f32[8192,22]{0,1:T(8,128)}, f32[8192,22]{0,1:T(8,128)}, u32[]{:S(2)}, u32[]{:S(2)}) %collective-permute-start.4) | collective-permute-done | bytes 720928
  856.6 36.3 %collective-permute-done.3 = f32[8192,32]{0,1:T(8,128)S(1)} collective-permute-done((f32[8192,32]{0,1:T(8,128)S(1)}, f32[8192,32]{0,1:T(8,128)S(1)}, u32[]{:S(2)}, u32[]{:S(2)}) %collective-permute-start.3) | collective-permute-done | bytes 1048608
  892.9 29.8 %concatenate.14 = f32[8192,182]{0,1:T(8,128)} concatenate(f32[8192,22]{0,1:T(8,128)} %collective-permute-done.4, f32[8192,32]{0,1:T(8,128)S(1)} %collective-permute-done.3, f32[8192,32]{0,1:T(8,128)} %collective-permute-done.2, f32[8192,32]{0,1:T(8,128)} %collective-permute-done.1, f32[8192,32]{0,1:T(8,128)} %collective-permute-done, f32[8192,32]{0,1:T(8,128)S(1)} %fusion), dimensions={1} | concatenate | bytes 11927552
  922.7 2.1 fusion.14
  (24 shorter events, 0.1 us)
Async XLA Ops:
  7.2 223.8 %copy-start = (bf16[352,704]{1,0:T(8,128)(2,1)S(1)}, bf16[352,704]{1,0:T(8,128)(2,1)}, u32[]{:S(2)}) copy-start(bf16[352,704]{1,0:T(8,128)(2,1)} %param.14) | copy-start | bytes 1486852
  7.2 155.0 %all-reduce.4.cloned.1.call-start = ((), (), s32[]{:S(2)}) async-start(), calls=%async_computation.5 | async-start | bytes 131072 | tf_op jit(solution)/shard_map/psum | solution.py:46
  9.2 215.4 %all-gather.9.cloned.1.call-start = ((), (), s32[]{:S(2)}) async-start(), calls=%async_computation.11 | async-start | bytes 6684672 | tf_op jit(solution)/shard_map/all_gather | solution.py:50
  165.1 200.7 %reduce-scatter.10.cloned.1.call-start = ((), (), s32[]{:S(2)}) async-start(), calls=%async_computation.9 | async-start | bytes 25952256 | tf_op jit(solution)/shard_map/reduce_scatter | solution.py:56
  244.7 1.0 copy-start.4
  244.8 244.6 %reduce-scatter.8.cloned.1.call-start = ((), (), s32[]{:S(2)}) async-start(), calls=%async_computation.8 | async-start | bytes 25952256 | tf_op jit(solution)/shard_map/reduce_scatter | solution.py:55
  259.5 0.9 copy-start.5
  259.5 274.4 %reduce-scatter.6.cloned.1.call-start = ((), (), s32[]{:S(2)}) async-start(), calls=%async_computation.6 | async-start | bytes 7077888 | tf_op jit(solution)/shard_map/reduce_scatter | solution.py:54
  267.5 275.5 %copy-start.7 = (s32[64]{0:T(128)S(1)}, s32[64]{0:T(128)}, u32[]{:S(2)}) copy-start(s32[64]{0:T(128)} %param.19) | copy-start | bytes 772
  267.5 331.4 %all-gather.7.cloned.1.call-start = ((), (), s32[]{:S(2)}) async-start(), calls=%async_computation.10 | async-start | bytes 12976128 | tf_op jit(solution)/shard_map/all_gather | solution.py:70
  536.0 16.9 %all-to-all-start = ((bf16[16,64,192]{2,1,0:T(8,128)(2,1)}), bf16[16,64,192]{2,1,0:T(8,128)(2,1)S(1)}, u32[]{:S(2)}, u32[]{:S(2)}) async-start(bf16[16,64,192]{2,1,0:T(8,128)(2,1)} %bitcast.6), calls=%async_computation.1 | async-start | bytes 1048576 | tf_op jit(solution)/shard_map/all_to_all | solution.py:58
  542.7 90.0 %all-gather.5.cloned.1.call-start = ((), (), s32[]{:S(2)}) async-start(), calls=%async_computation.7 | async-start | bytes 4718592 | tf_op jit(solution)/shard_map/all_gather | solution.py:69
  559.4 6.9 copy-start.2
  582.0 50.7 %copy-start.6 = (bf16[176,352]{1,0:T(8,128)(2,1)S(1)}, bf16[176,352]{1,0:T(8,128)(2,1)}, u32[]{:S(2)}) copy-start(bf16[176,352]{1,0:T(8,128)(2,1)} %param.15) | copy-start | bytes 371716
  644.2 160.7 %copy-start.8 = (u32[128]{0:T(128)S(1)}, u32[128]{0:T(128)}, u32[]{:S(2)}) copy-start(u32[128]{0:T(128)} %constant.30) | copy-start | bytes 1540
  788.8 104.1 %collective-permute-start.3 = (f32[8192,32]{0,1:T(8,128)S(1)}, f32[8192,32]{0,1:T(8,128)S(1)}, u32[]{:S(2)}, u32[]{:S(2)}) collective-permute-start(f32[8192,32]{0,1:T(8,128)S(1)} %fusion), channel_id=1, source_target_pairs={{0,32},{8,40},{16,48},{24,56},{32,64},{40,72},{48,80},{56,88},{64,... | collective-permute-start | bytes 3145736
  790.2 102.7 %collective-permute-start.2 = (f32[8192,32]{0,1:T(8,128)S(1)}, f32[8192,32]{0,1:T(8,128)}, u32[]{:S(2)}, u32[]{:S(2)}) collective-permute-start(f32[8192,32]{0,1:T(8,128)S(1)} %fusion), channel_id=1, source_target_pairs={{0,24},{8,32},{16,40},{24,48},{32,56},{40,64},{48,72},{56,80},{64,... | collective-permute-start | bytes 3145736
  795.1 97.8 %collective-permute-start.1 = (f32[8192,32]{0,1:T(8,128)S(1)}, f32[8192,32]{0,1:T(8,128)}, u32[]{:S(2)}, u32[]{:S(2)}) collective-permute-start(f32[8192,32]{0,1:T(8,128)S(1)} %fusion), channel_id=1, source_target_pairs={{0,16},{8,24},{16,32},{24,40},{32,48},{40,56},{48,64},{56,72},{64,... | collective-permute-start | bytes 3145736
  798.4 94.5 %collective-permute-start = (f32[8192,32]{0,1:T(8,128)S(1)}, f32[8192,32]{0,1:T(8,128)}, u32[]{:S(2)}, u32[]{:S(2)}) collective-permute-start(f32[8192,32]{0,1:T(8,128)S(1)} %fusion), channel_id=1, source_target_pairs={{0,8},{8,16},{16,24},{24,32},{32,40},{40,48},{48,56},{56,64},{64,7... | collective-permute-start | bytes 3145736
  802.1 54.5 %collective-permute-start.4 = (f32[8192,22]{0,1:T(8,128)}, f32[8192,22]{0,1:T(8,128)}, u32[]{:S(2)}, u32[]{:S(2)}) collective-permute-start(f32[8192,22]{0,1:T(8,128)} %slice.45), channel_id=1, source_target_pairs={{0,40},{8,48},{16,56},{24,64},{32,72},{40,80},{48,88},{56,96},{64,... | collective-permute-start | bytes 2162696
  806.1 118.7 %copy-start.1 = (bf16[352,704]{1,0:T(8,128)(2,1)S(1)}, bf16[352,704]{1,0:T(8,128)(2,1)}, u32[]{:S(2)}) copy-start(bf16[352,704]{1,0:T(8,128)(2,1)} %param.14) | copy-start | bytes 1486852
  806.1 116.6 %copy-start.3 = (bf16[8192,22]{0,1:T(8,128)(2,1)S(1)}, bf16[8192,22]{0,1:T(8,128)(2,1)}, u32[]{:S(2)}) copy-start(bf16[8192,22]{0,1:T(8,128)(2,1)} %param.10) | copy-start | bytes 1081348
Sparse Core Ops, SparseCore 0:
  13.3 148.8 all-reduce.3
  165.2 59.3 all-gather.8
  244.9 120.8 reduce-scatter.9
  368.1 121.1 reduce-scatter.7
  491.6 42.2 reduce-scatter.5
  535.4 63.3 all-gather.6
  600.5 32.1 all-gather.4
where the time goes:
time: 936 us; the launch traced here: 932 us
  waiting for transfers between devices  607 us (65%)
  blocking collectives  158 us (17%)
  matrix products  65.6 us (7%)
  local copies, waits for them, and re-layouts  43.5 us (5%)
  starting transfers between devices  22.3 us (2%)
  other arithmetic  19.5 us (2%)
  between operations  15 us (2%)
    psum x1, waiting for transfers between devices, local_layer(): row_stats = lax.psum(row_stats, both_axes)  152 us
    unnamed x1, blocking collectives  145 us
    reduce_scatter x1, waiting for transfers between devices, local_layer(): lax.psum_scatter(gate_part, 'x', scatter_dimension=0, tiled=True)  124 us
    reduce_scatter x1, waiting for transfers between devices, local_layer(): lax.psum_scatter(up_part, 'x', scatter_dimension=0, tiled=True)  98.3 us
    unnamed x12, waiting for transfers between devices  86.9 us
    all_gather x1, waiting for transfers between devices, local_layer(): normed_rows = lax.all_gather(normed, 'yz', axis=1, tiled=True)  59.5 us
    reduce_scatter x1, waiting for transfers between devices, local_layer(): lax.psum_scatter(qkv_part, 'x', scatter_dimension=0, tiled=True)  39.8 us
    unnamed x22, local copies, waits for them, and re-layouts  39.6 us
  transfers between devices with their start and end apart: 13, of which 10 were waited for; matrix products, arithmetic and copies ran while one was open for 6% of the time, Pallas kernels for 0%

commit v1 on v0

v1 whole, which is shorter than its diff:
```python
import jax
import jax.numpy as jnp
from jax import lax
from jax.sharding import PartitionSpec as P


def apply_rope(vecs, positions):
    half_dim = vecs.shape[-1] // 2
    inv_freq = 10000.0 ** (-jnp.arange(half_dim, dtype=jnp.float32) / half_dim)
    angles = positions.astype(jnp.float32)[..., None] * inv_freq
    cos_t = jnp.cos(angles)
    sin_t = jnp.sin(angles)
    first_half = vecs[..., :half_dim]
    second_half = vecs[..., half_dim:]
    return jnp.concatenate([first_half * cos_t - second_half * sin_t, second_half * cos_t + first_half * sin_t], axis=-1)


def attend_local(q_rot, k_all, v_all, ctx_len):
    head_dim = q_rot.shape[-1]
    positions = jnp.arange(k_all.shape[1])
    scores = jnp.einsum("bhd,btd->bht", q_rot, k_all, preferred_element_type=jnp.float32) * head_dim ** -0.5
    visible = (positions[None, :] <= ctx_len[:, None])[:, None, :]
    scores = jnp.where(visible, scores, -1e30)
    attn_probs = jax.nn.softmax(scores, axis=-1).astype(jnp.bfloat16)
    return jnp.einsum("bht,btd->bhd", attn_probs, v_all, preferred_element_type=jnp.float32).astype(jnp.bfloat16)


def solution(mesh):
    xs = mesh.shape["x"]
    yzs = mesh.shape["yz"]
    both_axes = ("x", "yz")
    row_spec = P("dp", both_axes)
    in_w_spec = P("x", "yz")
    out_w_spec = P("yz", "x")
    cache_spec = P(("dp", "x", "yz"), None, None)
    len_spec = P(("dp", "x", "yz"))

    def local_layer(x_loc, gain_loc, wqkv_loc, wgate_loc, wup_loc, wao_loc, wmo_loc, kc_loc, vc_loc, len_loc):
        n_rows, grp = x_loc.shape
        pad = -grp % 8
        gp = grp + pad
        d_model = grp * xs * yzs
        head_dim = kc_loc.shape[2]
        dev_rows = kc_loc.shape[0]
        rows = n_rows // xs
        attn_cols = wao_loc.shape[0] * yzs
        num_heads = attn_cols // head_dim
        f32, bf16 = jnp.float32, jnp.bfloat16

        w1_loc = jnp.concatenate([wqkv_loc, wgate_loc, wup_loc], axis=1)
        n1 = w1_loc.shape[1]
        w1_loc = jnp.pad(w1_loc.reshape(yzs, grp, n1), ((0, 0), (0, pad), (0, 0))).reshape(yzs * gp, n1)
        w1 = lax.all_gather(w1_loc, "x", axis=0, tiled=True)
        w2_loc = jnp.concatenate([wao_loc, wmo_loc], axis=0).T
        n2 = w2_loc.shape[1]
        w2_loc = jnp.pad(w2_loc.reshape(yzs, grp, n2), ((0, 0), (0, pad), (0, 0))).reshape(yzs * gp, n2)
        w2 = lax.all_gather(w2_loc, "x", axis=0, tiled=False)

        x_t = x_loc.T.reshape(grp, xs, rows).transpose(1, 0, 2)
        gain_row = jnp.broadcast_to(jnp.pad(gain_loc, (0, rows - grp)).reshape(1, 1, rows), (xs, 1, rows))
        x_pad = jnp.concatenate([x_t, gain_row, jnp.zeros((xs, pad - 1, rows), bf16)], axis=1)
        x_mine = lax.all_to_all(x_pad, "x", 0, 0, tiled=True)
        x_all = lax.all_gather(x_mine, "yz", axis=0, tiled=False)
        gain = x_all[:, :, grp, :grp].astype(f32)[..., None]
        x_f32 = x_all[:, :, :grp, :].astype(f32)
        row_mean = jnp.sum(x_f32, axis=(0, 1, 2), keepdims=True) / d_model
        row_var = jnp.sum(x_f32 * x_f32, axis=(0, 1, 2), keepdims=True) / d_model - row_mean * row_mean
        normed = ((x_f32 - row_mean) * lax.rsqrt(row_var + 1e-6) * gain).astype(bf16)
        normed = jnp.pad(normed, ((0, 0), (0, 0), (0, pad), (0, 0))).transpose(1, 0, 2, 3).reshape(xs * yzs * gp, rows)

        c_q = wqkv_loc.shape[1]
        c_f = wgate_loc.shape[1]
        cd = (((0,), (0,)), ((), ()))
        qkv = lax.dot_general(normed, w1[:, :c_q], cd, preferred_element_type=f32).astype(bf16)
        gate = lax.dot_general(w1[:, c_q:c_q + c_f], normed, cd, preferred_element_type=f32).astype(bf16)
        up = lax.dot_general(w1[:, c_q + c_f:], normed, cd, preferred_element_type=f32).astype(bf16)
        mlp_t = (jax.nn.silu(gate.astype(f32)) * up.astype(f32)).astype(bf16)

        qkv_dev = lax.all_to_all(qkv, "yz", 0, 1, tiled=True)
        q_heads = qkv_dev[:, :attn_cols].reshape(dev_rows, num_heads, head_dim)
        k_new = qkv_dev[:, attn_cols:attn_cols + head_dim]
        v_new = qkv_dev[:, attn_cols + head_dim:]
        q_rot = apply_rope(q_heads.astype(f32), len_loc[:, None]).astype(bf16)
        k_rot = apply_rope(k_new.astype(f32), len_loc).astype(bf16)
        new_slot = (jnp.arange(kc_loc.shape[1])[None, :] == len_loc[:, None])[:, :, None]
        k_all = jnp.where(new_slot, k_rot[:, None, :], kc_loc)
        v_all = jnp.where(new_slot, v_new[:, None, :], vc_loc)
        attn_dev = attend_local(q_rot, k_all, v_all, len_loc).reshape(dev_rows, attn_cols)
        attn_rows = lax.all_to_all(attn_dev, "yz", 1, 0, tiled=True)

        w2_p = w2.reshape(xs, yzs, gp, n2).transpose(1, 0, 2, 3).reshape(yzs * xs * gp, n2)
        c_a = wao_loc.shape[0]
        z_part = jnp.dot(w2_p[:, c_a:], mlp_t, preferred_element_type=f32)
        z_part = z_part + lax.dot_general(w2_p[:, :c_a], attn_rows, (((1,), (1,)), ((), ())), preferred_element_type=f32)
        z_loc = lax.psum_scatter(z_part, "yz", scatter_dimension=0, tiled=True)
        z_loc = z_loc.reshape(xs, gp, rows)
        y_mine = (x_mine.astype(f32) + z_loc).astype(bf16)
        y_back = lax.all_to_all(y_mine, "x", 0, 0, tiled=True)
        y_loc = y_back[:, :grp].transpose(1, 0, 2).reshape(grp, n_rows).T
        return y_loc, k_all, v_all

    in_specs = (row_spec, P(both_axes), in_w_spec, in_w_spec, in_w_spec, out_w_spec, out_w_spec, cache_spec, cache_spec, len_spec)
    out_specs = (row_spec, cache_spec, cache_spec)
    return jax.shard_map(local_layer, mesh=mesh, in_specs=in_specs, out_specs=out_specs, check_vma=False)
```

time: 936 us -> 367 us (0.39)
  waiting for transfers between devices: 607 us -> 214 us
  blocking collectives: 158 us -> 27.7 us
  local copies, waits for them, and re-layouts: 43.5 us -> 29 us
  matrix products: 65.6 us -> 51.7 us
    reduce_scatter x3 -> x1, waiting for transfers between devices: 262 us -> 93.8 us  [local_layer(): z_loc = lax.psum_scatter(z_part, 'yz', scatter_dimension=0, tiled=True)]
    psum x1 -> x0, waiting for transfers between devices: 152 us -> none  [local_layer(): row_stats = lax.psum(row_stats, both_axes)]
    unnamed x1 -> x0, blocking collectives: 145 us -> none
    unnamed x12 -> x4, waiting for transfers between devices: 86.9 us -> 0.07 us
    unnamed x22 -> x26, local copies, waits for them, and re-layouts: 39.6 us -> 1.41 us
    all_gather x3, waiting for transfers between devices: 96.9 us -> 120 us  [the longest x1 48.9 us: local_layer(): x_all = lax.all_gather(x_mine, 'yz', axis=0, tiled=False)]
    unnamed x5 -> x0, starting transfers between devices: 15.1 us -> none
    all_to_all x1 -> x2, blocking collectives: 13.7 us -> 27.7 us  [the longest x1 14 us: local_layer(): y_back = lax.all_to_all(y_mine, 'x', 0, 0, tiled=True)]
  transfers between devices with their start and end apart: 13 -> 6, of which waited for: 10 -> 5; matrix products, arithmetic and copies ran while one was open for 6% -> 16% of each run, Pallas kernels for 0% -> 0%
where the time goes in v1:
time: 367 us; the launch traced here: 366 us
  waiting for transfers between devices  214 us (58%)
  matrix products  51.7 us (14%)
  local copies, waits for them, and re-layouts  29 us (8%)
  blocking collectives  27.7 us (8%)
  other arithmetic  15.5 us (4%)
  between operations  14.1 us (4%)
  starting transfers between devices  13.6 us (4%)
    reduce_scatter x1, waiting for transfers between devices, local_layer(): z_loc = lax.psum_scatter(z_part, 'yz', scatter_dimension=0, tiled=True)  93.8 us
    all_gather x1, waiting for transfers between devices, local_layer(): x_all = lax.all_gather(x_mine, 'yz', axis=0, tiled=False)  48.9 us
    all_gather x1, waiting for transfers between devices, local_layer(): w1 = lax.all_gather(w1_loc, 'x', axis=0, tiled=True)  48.1 us
    all_gather x1, waiting for transfers between devices, local_layer(): w2 = lax.all_gather(w2_loc, 'x', axis=0, tiled=False)  22.9 us
    all_to_all x1, blocking collectives, local_layer(): y_back = lax.all_to_all(y_mine, 'x', 0, 0, tiled=True)  14 us
    all_to_all x1, blocking collectives, local_layer(): x_mine = lax.all_to_all(x_pad, 'x', 0, 0, tiled=True)  13.6 us
    dot_general x1, matrix products, local_layer(): lax.dot_general(w2_p[:, :c_a], attn_rows, (((1,), (1,)), ((), ())), prefe...  11.4 us
    dot_general x1, matrix products, local_layer(): z_part = jnp.dot(w2_p[:, c_a:], mlp_t, preferred_element_type=f32)  10.6 us
  transfers between devices with their start and end apart: 6, of which 5 were waited for; matrix products, arithmetic and copies ran while one was open for 16% of the time, Pallas kernels for 0%

profile of v1, /device:TPU:1, one launch (start us, length us, event | category | flops | bytes accessed | tf_op | source)
XLA Modules:
  0.0 365.9 jit_solution(6727647873827587108)
XLA Ops:
  7.2 0.0 all-gather.5.cloned.1.call-start
  7.2 1.2 maximum_bitcast_fusion
  8.4 0.3 copy.52
  8.8 0.0 copy-start.6
  8.8 0.0 copy-start.3
  8.8 0.0 copy-start.4
  8.8 0.2 reshape.197
  9.0 0.1 pad.17
  9.1 1.1 copy.53
  10.2 0.0 all-gather.5.cloned.1.call-update
  10.2 0.0 all-gather.9.cloned.1.call-start
  10.3 0.2 copy.62
  10.5 0.1 pad.28.clone
  10.6 0.1 maximum_maximum_fusion
  10.7 0.2 copy.51
  11.0 13.6 %all_to_all.48 = bf16[8,24,1024]{2,1,0:T(8,128)(2,1)} all-to-all(bf16[8,24,1024]{2,1,0:T(8,128)(2,1)S(1)} %copy.51), channel_id=1, replica_groups=mesh['dp'=1,'yz'=16,'x'=8] {'x'}, dimensions={0} | all-to-all | bytes 786432 | tf_op jit(solution)/shard_map/all_to_all | solution.py:62
  24.6 0.0 all-gather.9.cloned.1.call-update
  24.6 0.0 all-gather.7.cloned.1.call-start
  24.7 0.1 copy.56
  24.9 1.3 concatenate.23
  26.2 0.4 reshape.200
  26.6 1.1 pad.18
  27.7 0.0 all-gather.7.cloned.1.call-update
  27.8 0.1 iota_compare_fusion.1
  27.9 22.9 %all-gather.5.cloned.1.call-done = bf16[8,384,880]{1,2,0:T(8,128)(2,1)} async-done(((bf16[1,384,880]{1,2,0:T(8,128)(2,1)}), bf16[8,384,880]{1,2,0:T(8,128)(2,1)}) %all-gather.5.cloned.1.call-update) | async-done | bytes 5406736 | tf_op jit(solution)/shard_map/all_gather | solution.py:57
  50.8 8.2 %copy.54 = bf16[8,384,880]{2,1,0:T(8,128)(2,1)} copy(bf16[8,384,880]{1,2,0:T(8,128)(2,1)} %all-gather.5.cloned.1.call-done) | data formatting | bytes 10813440 | tf_op jit(solution)/shard_map/all_gather | solution.py:57
  58.9 5.6 %copy.55 = bf16[16,8,24,880]{3,2,1,0:T(8,128)(2,1)} copy(bf16[16,8,24,880]{3,2,0,1:T(8,128)(2,1)} %bitcast.45) | data formatting | bytes 10813440 | tf_op jit(solution)/shard_map/transpose | solution.py:91
  64.6 48.9 %all-gather.9.cloned.1.call-done = bf16[128,24,1024]{2,1,0:T(8,128)(2,1)} async-done(((bf16[8,24,1024]{2,1,0:T(8,128)(2,1)}), bf16[128,24,1024]{2,1,0:T(8,128)(2,1)}) %all-gather.9.cloned.1.call-update) | async-done | bytes 6291472 | tf_op jit(solution)/shard_map/all_gather | solution.py:63
  113.4 4.9 %convert_reduce_fusion = (f32[1024]{0:T(1024)S(1)}, f32[1024]{0:T(1024)S(1)}) fusion(bf16[16,8,24,1024]{3,2,1,0:T(8,128)(2,1)} %bitcast.42), kind=kLoop, calls=%fused_computation.3 | loop fusion | flops 11532288 | bytes 5775360 | tf_op jit(solution)/shard_map/reduce_sum | solution.py:66
  118.3 0.1 slice_convert_fusion.1
  118.4 2.0 fusion.3
  120.4 1.4 pad_bitcast_fusion
  121.8 3.3 copy.57
  125.1 48.1 %all-gather.7.cloned.1.call-done = bf16[3072,1600]{1,0:T(8,128)(2,1)} async-done(((bf16[384,1600]{1,0:T(8,128)(2,1)}), bf16[3072,1600]{1,0:T(8,128)(2,1)}) %all-gather.7.cloned.1.call-update) | async-done | bytes 9830416 | tf_op jit(solution)/shard_map/all_gather | solution.py:53
  173.2 4.6 %fusion.30 = bf16[1024,192]{0,1:T(8,128)(2,1)S(1)} fusion(bf16[3072,1024]{1,0:T(8,128)(2,1)} %bitcast.48, bf16[3072,1600]{1,0:T(8,128)(2,1)} %all-gather.7.cloned.1.call-done), kind=kOutput, calls=%fused_computation.34 | convolution fusion | flops 1208156160 | bytes 8257536 | tf_op jit(solution)/shard_map/dot_general | solution.py:74
  177.9 1.0 copy.58
  178.9 6.8 %all-to-all-start.1 = ((bf16[16,64,192]{2,1,0:T(8,128)(2,1)}), bf16[16,64,192]{2,1,0:T(8,128)(2,1)S(1)}, u32[]{:S(2)}, u32[]{:S(2)}) async-start(bf16[16,64,192]{2,1,0:T(8,128)(2,1)} %bitcast.12), calls=%async_computation.1 | async-start | bytes 1048576 | tf_op jit(solution)/shard_map/all_to_all | solution.py:79
  185.7 0.0 slice-start.1
  185.7 9.0 %fusion.21 = bf16[704,1024]{1,0:T(8,128)(2,1)S(1)} fusion(bf16[3072,1024]{1,0:T(8,128)(2,1)} %bitcast.49, bf16[3072,1600]{1,0:T(8,128)(2,1)} %all-gather.7.cloned.1.call-done), kind=kOutput, calls=%fused_computation.26 | convolution fusion | flops 4429905920 | bytes 12451840 | tf_op jit(solution)/shard_map/dot_general | solution.py:76
  194.8 10.4 %fusion.15 = bf16[704,1024]{1,0:T(8,128)(2,1)} fusion(bf16[704,1024]{1,0:T(8,128)(2,1)S(1)} %fusion.21, bf16[3072,1024]{1,0:T(8,128)(2,1)S(1)} %bitcast.52, bf16[3072,1600]{1,0:T(8,128)(2,1)} %all-gather.7.cloned.1.call-done), kind=kOutput, calls=%fused_computation.22 | convolution fusion | flops 4435673088 | bytes 13893632 | tf_op jit(solution)/shard_map/dot_general | solution.py:75
  205.2 0.0 all-to-all-done.1
  205.2 0.3 copy.59
  205.5 0.5 all_to_all.38
  206.1 0.1 reshape.206
  206.2 0.2 multiply_cosine_fusion
  206.4 0.1 pad_maximum_fusion
  206.5 0.4 subtract_convert_fusion
  206.9 4.8 %broadcast_select_fusion.1 = (bf16[64,128,128]{2,1,0:T(8,128)(2,1)S(1)}, bf16[64,128,128]{2,1,0:T(8,128)(2,1)}) fusion(bf16[64,128,128]{2,1,0:T(8,128)(2,1)} %param.17, pred[64,128]{1,0:T(8,128)(4,1)S(1)} %get-tuple-element.20, bf16[64,128]{1,0:T(8,128)(2,1)S(1)} %pad_maximum_fusion, bf16[64,128,128]{2,1,0:T(8,128)(2,1)} %param.18, ...), kind=kLoop, calls=%fused_computation.24 | loop fusion | flops 2097152 | bytes 8429568 | tf_op jit(solution)/shard_map/jit(_where)/select_n | solution.py:86
  211.6 1.2 fusion.29
  212.9 0.5 fusion.39
  213.4 4.4 %convolution_convert_fusion = bf16[64,22,128]{2,1,0:T(8,128)(2,1)S(1)} fusion(bf16[64,128,128]{2,1,0:T(8,128)(2,1)} %get-tuple-element.12, f32[64,22]{1,0:T(8,128)S(1)} %fusion.39, f32[64,22,128]{2,1,0:T(8,128)S(1)} %fusion.29), kind=kOutput, calls=%fused_computation.35 | convolution fusion | flops 46859776 | bytes 3184128 | tf_op jit(solution)/shard_map/bht,btd->bhd/dot_general | solution.py:25
  217.8 1.1 all_to_all.39
  218.8 1.0 copy.60
  219.8 6.6 %all-to-all-start.2 = ((bf16[64,16,176]{2,0,1:T(8,128)(2,1)}), bf16[64,16,176]{2,0,1:T(8,128)(2,1)S(1)}, u32[]{:S(2)}, u32[]{:S(2)}) async-start(bf16[64,16,176]{2,0,1:T(8,128)(2,1)} %copy.60), calls=%async_computation.2 | async-start | bytes 1048576 | tf_op jit(solution)/shard_map/all_to_all | solution.py:89
  226.5 0.0 reduce-scatter.2.cloned.1.call-start
  226.5 10.6 %fusion.9 = f32[3072,1024]{1,0:T(8,128)} fusion(bf16[704,1024]{1,0:T(8,128)(2,1)} %fusion.15, bf16[3072,880]{1,0:T(8,128)(2,1)} %bitcast.46), kind=kOutput, calls=%fused_computation.14 | convolution fusion | flops 4429185024 | bytes 18743296 | tf_op jit(solution)/shard_map/dot_general | solution.py:93
  237.1 0.5 all-to-all-done.2
  237.6 11.4 %convolution_add_fusion = f32[3072,1024]{1,0:T(8,128)} fusion(f32[3072,1024]{1,0:T(8,128)} %fusion.9, bf16[1024,176]{1,0:T(8,128)(2,1)S(1)} %bitcast.55, bf16[3072,880]{1,0:T(8,128)(2,1)} %bitcast.47), kind=kOutput, calls=%fused_computation.8 | convolution fusion | flops 1110441984 | bytes 27099136 | tf_op jit(solution)/shard_map/dot_general | solution.py:94
  249.0 0.0 reduce-scatter.2.cloned.1.call-update
  249.0 93.8 %reduce-scatter.2.cloned.1.call-done = f32[192,1024]{1,0:T(8,128)} async-done(((f32[3072,1024]{1,0:T(8,128)}), f32[192,1024]{1,0:T(8,128)}) %reduce-scatter.2.cloned.1.call-update) | async-done | bytes 786448 | tf_op jit(solution)/shard_map/reduce_scatter | solution.py:95
  342.8 1.2 add_convert_fusion
  344.0 14.0 %all_to_all.49 = bf16[8,24,1024]{2,1,0:T(8,128)(2,1)S(1)} all-to-all(bf16[8,24,1024]{2,1,0:T(8,128)(2,1)S(1)} %add_convert_fusion), channel_id=1, replica_groups=mesh['dp'=1,'yz'=16,'x'=8] {'x'}, dimensions={0} | all-to-all | bytes 786432 | tf_op jit(solution)/shard_map/all_to_all | solution.py:98
  358.1 0.2 copy.61
  358.4 1.0 copy.63
  (29 shorter events, 0.2 us)
Async XLA Ops:
  7.2 3.1 copy-start.5
  7.2 3.3 copy-start.8
  7.2 43.6 %all-gather.5.cloned.1.call-start = ((), (), s32[]{:S(2)}) async-start(), calls=%async_computation.5 | async-start | bytes 6082560 | tf_op jit(solution)/shard_map/all_gather | solution.py:57
  8.8 15.9 %copy-start.6 = (bf16[352,192]{0,1:T(8,128)(2,1)S(1)}, bf16[352,192]{0,1:T(8,128)(2,1)}, u32[]{:S(2)}) copy-start(bf16[352,192]{0,1:T(8,128)(2,1)} %param.12) | copy-start | bytes 405508
  8.8 16.1 %copy-start.3 = (bf16[352,704]{1,0:T(8,128)(2,1)S(1)}, bf16[352,704]{1,0:T(8,128)(2,1)}, u32[]{:S(2)}) copy-start(bf16[352,704]{1,0:T(8,128)(2,1)} %param.13) | copy-start | bytes 1486852
  8.8 16.1 %copy-start.4 = (bf16[352,704]{1,0:T(8,128)(2,1)S(1)}, bf16[352,704]{1,0:T(8,128)(2,1)}, u32[]{:S(2)}) copy-start(bf16[352,704]{1,0:T(8,128)(2,1)} %param.14) | copy-start | bytes 1486852
  10.2 103.2 %all-gather.9.cloned.1.call-start = ((), (), s32[]{:S(2)}) async-start(), calls=%async_computation.8 | async-start | bytes 6684672 | tf_op jit(solution)/shard_map/all_gather | solution.py:63
  24.6 3.2 copy-start.7
  24.6 148.6 %all-gather.7.cloned.1.call-start = ((), (), s32[]{:S(2)}) async-start(), calls=%async_computation.6 | async-start | bytes 11501568 | tf_op jit(solution)/shard_map/all_gather | solution.py:53
  113.4 4.9 %copy-start = (bf16[128,24,1024]{2,1,0:T(8,128)(2,1)S(1)}, bf16[128,24,1024]{2,1,0:T(8,128)(2,1)}, u32[]{:S(2)}) copy-start(bf16[128,24,1024]{2,1,0:T(8,128)(2,1)} %all-gather.9.cloned.1.call-done) | copy-start | bytes 18874372
  178.9 15.9 %slice-start = ((s8[6291456]{0:T(1024)(128)(4,1)}), s8[2097152]{0:T(1024)(128)(4,1)S(1)}, s32[]{:S(2)}) async-start(s8[6291456]{0:T(1024)(128)(4,1)} %bitcast.50), calls=%async_computation.9 | async-start | bytes 4194304
  178.9 26.3 %all-to-all-start.1 = ((bf16[16,64,192]{2,1,0:T(8,128)(2,1)}), bf16[16,64,192]{2,1,0:T(8,128)(2,1)S(1)}, u32[]{:S(2)}, u32[]{:S(2)}) async-start(bf16[16,64,192]{2,1,0:T(8,128)(2,1)} %bitcast.12), calls=%async_computation.1 | async-start | bytes 1048576 | tf_op jit(solution)/shard_map/all_to_all | solution.py:79
  185.7 9.1 %slice-start.1 = ((s8[6291456]{0:T(1024)(128)(4,1)}), s8[4194304]{0:T(1024)(128)(4,1)S(1)}, s32[]{:S(2)}) async-start(s8[6291456]{0:T(1024)(128)(4,1)} %bitcast.50), calls=%async_computation.10 | async-start | bytes 8388608
  211.6 7.2 %copy-start.1 = (bf16[64,128,128]{2,1,0:T(8,128)(2,1)}, bf16[64,128,128]{2,1,0:T(8,128)(2,1)S(1)}, u32[]{:S(2)}) copy-start(bf16[64,128,128]{2,1,0:T(8,128)(2,1)S(1)} %get-tuple-element.11) | copy-start | bytes 6291460
  219.8 17.8 %all-to-all-start.2 = ((bf16[64,16,176]{2,0,1:T(8,128)(2,1)}), bf16[64,16,176]{2,0,1:T(8,128)(2,1)S(1)}, u32[]{:S(2)}, u32[]{:S(2)}) async-start(bf16[64,16,176]{2,0,1:T(8,128)(2,1)} %copy.60), calls=%async_computation.2 | async-start | bytes 1048576 | tf_op jit(solution)/shard_map/all_to_all | solution.py:89
  226.5 116.4 %reduce-scatter.2.cloned.1.call-start = ((), (), s32[]{:S(2)}) async-start(), calls=%async_computation.7 | async-start | bytes 13369344 | tf_op jit(solution)/shard_map/reduce_scatter | solution.py:95
  249.0 93.8 %copy-start.2 = (bf16[8,24,1024]{2,1,0:T(8,128)(2,1)S(1)}, bf16[8,24,1024]{2,1,0:T(8,128)(2,1)}, u32[]{:S(2)}) copy-start(bf16[8,24,1024]{2,1,0:T(8,128)(2,1)} %all_to_all.48) | copy-start | bytes 1179652
Sparse Core Ops, SparseCore 0:
  10.3 40.3 all-gather.4
  52.9 60.4 all-gather.8
  115.7 57.4 all-gather.6
  249.2 93.6 reduce-scatter.1

commit v2 on v1

--- a/solution.py
+++ b/solution.py
@@ -1,7 +1,15 @@
+import functools
+
 import jax
 import jax.numpy as jnp
 from jax import lax
+from jax.experimental import pallas as pl
+from jax.experimental.pallas import tpu as pltpu
 from jax.sharding import PartitionSpec as P
+
+MESH = pl.DeviceIdType.MESH
+RING = 4
+VMEM_LIMIT = 62 * 1024 * 1024
 
 
 def apply_rope(vecs, positions):
@@ -23,6 +31,322 @@
     scores = jnp.where(visible, scores, -1e30)
     attn_probs = jax.nn.softmax(scores, axis=-1).astype(jnp.bfloat16)
     return jnp.einsum("bht,btd->bhd", attn_probs, v_all, preferred_element_type=jnp.float32).astype(jnp.bfloat16)
+
+
+class Where:
+    def __init__(self, xs):
+        self.xs = xs
+        self.dp = lax.axis_index("dp")
+        self.x = lax.axis_index("x")
+        self.j = lax.axis_index("yz")
+        self.zz = self.j // RING
+        self.yy = self.j % RING
+        self.chip = self.x // 2
+        self.core = self.x % 2
+
+    def block(self, dz, dy):
+        return ((self.zz + dz) % RING) * RING + (self.yy + dy) % RING
+
+    def on_yz(self, j):
+        return (self.dp, j, self.x)
+
+    def on_x(self, x):
+        return (self.dp, self.j, x)
+
+    def axis_block(self, first, df, dg):
+        return self.block(df, dg) if first == "z" else self.block(dg, df)
+
+    def step(self, first, axis, d):
+        return self.on_yz(self.axis_block(first, d, 0) if axis == 0 else self.axis_block(first, 0, d))
+
+    def x_of(self, dc):
+        return ((self.chip + dc) % RING) * 2 + self.core
+
+    def x_other(self, dc):
+        return ((self.chip + dc) % RING) * 2 + (1 - self.core)
+
+    def greet(self):
+        barrier = pltpu.get_barrier_semaphore()
+        peers = [self.on_x((self.x + d) % self.xs) for d in range(1, self.xs)]
+        peers += [self.on_yz(self.block(*d)) for d in ((1, 0), (3, 0), (0, 1), (0, 3))]
+        for peer in peers:
+            pl.semaphore_signal(barrier, inc=1, device_id=peer, device_id_type=MESH)
+        pl.semaphore_wait(barrier, len(peers))
+
+
+def remote(src, dst, send, recv, peer):
+    return pltpu.make_async_remote_copy(src_ref=src, dst_ref=dst, send_sem=send, recv_sem=recv, device_id=peer, device_id_type=MESH)
+
+
+def gather_kernel(xs, x_ref, w_ref, xg_ref, wg_ref, loc_sem, xsend, xrecv, gsend, grecv, wsend, wrecv):
+    at = Where(xs)
+    half = xs // 2
+    quarter = half // 2
+    at.greet()
+    started = []
+
+    def send(src, dst, sems, idx, peer):
+        copy = remote(src, dst, sems[0].at[idx], sems[1].at[idx], peer)
+        copy.start()
+        started.append(copy)
+
+    def arrived(region, sems, idx):
+        remote(region, region, sems[0].at[idx], sems[1].at[idx], at.on_yz(at.block(0, 1))).wait_recv()
+
+    xsem, wsem = (xsend, xrecv), (wsend, wrecv)
+    own_x = pltpu.make_async_copy(x_ref.at[at.x], xg_ref.at[at.x, at.j], loc_sem.at[0])
+    own_x.start()
+    for d in range(1, xs):
+        to = (at.x + d) % xs
+        send(x_ref.at[to], xg_ref.at[at.x, at.j], xsem, d - 1, at.on_x(to))
+    own_w = pltpu.make_async_copy(w_ref, wg_ref.at[at.x], loc_sem.at[1])
+    own_w.start()
+    send(w_ref, wg_ref.at[at.x], wsem, 0, at.on_x(at.x_of(1)))
+    send(w_ref, wg_ref.at[at.x], wsem, 1, at.on_x(at.x_of(3)))
+    send(w_ref, wg_ref.at[at.x], wsem, 2, at.on_x(at.x_other(0)))
+    own_x.wait()
+    for d in range(1, xs):
+        arrived(xg_ref.at[(at.x + xs - d) % xs, at.j], xsem, d - 1)
+
+    order = ("y", "z")
+
+    def region(h, df, dg, lo=0, n=half):
+        return xg_ref.at[pl.ds(h * half + lo, n), at.axis_block(order[h], df, dg)]
+
+    def gsend_block(h, df, dg, axis, d, slot, lo=0, n=half):
+        r = region(h, df, dg, lo, n)
+        send(r, r, (gsend.at[h], grecv.at[h]), slot, at.step(order[h], axis, d))
+
+    def garrived(h, df, dg, slot, lo=0, n=half):
+        arrived(region(h, df, dg, lo, n), (gsend.at[h], grecv.at[h]), slot)
+
+    for h in range(2):
+        gsend_block(h, 0, 0, 0, 1, 0)
+        gsend_block(h, 0, 0, 0, 3, 1)
+        gsend_block(h, 0, 0, 1, 1, 4)
+        gsend_block(h, 0, 0, 1, 3, 8)
+    for h in range(2):
+        garrived(h, 3, 0, 0)
+        gsend_block(h, 3, 0, 0, 1, 2, 0, quarter)
+        garrived(h, 1, 0, 1)
+        gsend_block(h, 1, 0, 0, 3, 3, quarter, quarter)
+        gsend_block(h, 3, 0, 1, 1, 4 + 3)
+        gsend_block(h, 3, 0, 1, 3, 8 + 3)
+        gsend_block(h, 1, 0, 1, 1, 4 + 1)
+        gsend_block(h, 1, 0, 1, 3, 8 + 1)
+    for h in range(2):
+        garrived(h, 2, 0, 2, 0, quarter)
+        garrived(h, 2, 0, 3, quarter, quarter)
+        gsend_block(h, 2, 0, 1, 1, 4 + 2)
+        gsend_block(h, 2, 0, 1, 3, 8 + 2)
+    for h in range(2):
+        for df in (0, 3):
+            garrived(h, df, 3, 4 + df)
+            gsend_block(h, df, 3, 1, 1, 12 + df)
+    wrows = w_ref.shape[0] // 2
+
+    def wregion(x, lo=None):
+        return wg_ref.at[x] if lo is None else wg_ref.at[x, pl.ds(lo * wrows, wrows)]
+
+    def wsend_block(r, slot, x):
+        send(r, r, wsem, slot, at.on_x(x))
+
+    arrived(wregion(at.x_of(3)), wsem, 0)
+    wsend_block(wregion(at.x_of(3), 0), 3, at.x_of(1))
+    arrived(wregion(at.x_of(1)), wsem, 1)
+    wsend_block(wregion(at.x_of(1), 1), 4, at.x_of(3))
+    wsend_block(wregion(at.x_of(3)), 5, at.x_other(0))
+    wsend_block(wregion(at.x_of(1)), 6, at.x_other(0))
+    for h in range(2):
+        for df in (1, 2):
+            garrived(h, df, 1, 8 + df)
+            gsend_block(h, df, 1, 1, 3, 12 + df)
+    arrived(wregion(at.x_of(2), 0), wsem, 3)
+    wsend_block(wregion(at.x_of(2), 0), 7, at.x_other(0))
+    arrived(wregion(at.x_of(2), 1), wsem, 4)
+    wsend_block(wregion(at.x_of(2), 1), 8, at.x_other(0))
+    for h in range(2):
+        for df in (1, 2):
+            garrived(h, df, 3, 4 + df)
+        for df in (0, 3):
+            garrived(h, df, 1, 8 + df)
+        for df in range(4):
+            garrived(h, df, 2, 12 + df)
+    arrived(wregion(at.x_other(0)), wsem, 2)
+    arrived(wregion(at.x_other(3)), wsem, 5)
+    arrived(wregion(at.x_other(1)), wsem, 6)
+    arrived(wregion(at.x_other(2), 0), wsem, 7)
+    arrived(wregion(at.x_other(2), 1), wsem, 8)
+    own_w.wait()
+    for copy in started:
+        copy.wait_send()
+
+
+def gather_inputs(x_pad, w_loc, xs, yzs):
+    _, gp, rows = x_pad.shape
+    dma = pltpu.SemaphoreType.DMA
+    return pl.pallas_call(
+        functools.partial(gather_kernel, xs),
+        out_shape=(
+            jax.ShapeDtypeStruct((xs, yzs, gp, rows), x_pad.dtype),
+            jax.ShapeDtypeStruct((xs,) + w_loc.shape, w_loc.dtype),
+        ),
+        in_specs=[pl.BlockSpec(memory_space=pltpu.VMEM)] * 2,
+        out_specs=(pl.BlockSpec(memory_space=pl.ANY), pl.BlockSpec(memory_space=pl.ANY)),
+        scratch_shapes=[dma((2,)), dma((xs - 1,)), dma((xs - 1,)), dma((2, 16)), dma((2, 16)), dma((9,)), dma((9,))],
+        compiler_params=pltpu.CompilerParams(collective_id=0, has_side_effects=True, vmem_limit_bytes=VMEM_LIMIT),
+        name="gather_inputs",
+    )(x_pad, w_loc)
+
+
+def scatter_kernel(xs, c_a, w_ref, a_ref, o_ref, xg_ref, y_ref, zb, r1, r2, r3, r4, xv, yv, loc_sem, s1, q1, s2, q2, s3, q3, s4, q4, ys, yq):
+    at = Where(xs)
+    order = ("z", "y")
+    hr = zb.shape[2] // 2
+    gp = xv.shape[1]
+    own_x = pltpu.make_async_copy(xg_ref.at[:, at.j], xv, loc_sem.at[0])
+    own_x.start()
+    at.greet()
+    started = []
+
+    def send(src, dst, ssem, rsem, peer):
+        copy = remote(src, dst, ssem, rsem, peer)
+        copy.start()
+        started.append(copy)
+
+    def arrived(dst, ssem, rsem):
+        remote(dst, dst, ssem, rsem, at.on_yz(at.block(0, 1))).wait_recv()
+
+    def zat(h, df, dg):
+        dz, dy = (df, dg) if order[h] == "z" else (dg, df)
+        return zb.at[dz, dy, pl.ds(h * hr, hr)]
+
+    def compute(dz, dy):
+        w = w_ref[at.block(dz, dy)]
+        z = jnp.dot(w[:, c_a:], a_ref[...], preferred_element_type=jnp.float32)
+        z = z + lax.dot_general(w[:, :c_a], o_ref[...], (((1,), (1,)), ((), ())), preferred_element_type=jnp.float32)
+        zb[dz, dy] = z
+
+    def compute_cell(i, dz):
+        compute(dz, i)
+        return dz
+
+    for dy in range(RING):
+        compute(2, dy)
+    for dz in (0, 1, 3):
+        compute(dz, 2)
+    for h in range(2):
+        for dg in range(RING):
+            d = 1 if dg < 2 else 3
+            send(zat(h, 2, dg), r1.at[h, dg], s1.at[h, dg], q1.at[h, dg], at.step(order[h], 0, d))
+    for dz in (1, 3, 0):
+        for dy in (0, 1, 3):
+            compute(dz, dy)
+    def send2(h, up, dg):
+        df, d, s = (1, 1, 0) if up else (3, 3, 1)
+        send(zat(h, df, dg), r2.at[h, s, dg], s2.at[h, s, dg], q2.at[h, s, dg], at.step(order[h], 0, d))
+
+    for h in range(2):
+        for dg in (2, 3):
+            send2(h, True, dg)
+        for dg in (0, 1):
+            send2(h, False, dg)
+    for k in range(2):
+        for h in range(2):
+            for up in (True, False):
+                dg = k if up else 2 + k
+                arrived(r1.at[h, dg], s1.at[h, dg], q1.at[h, dg])
+                ref = zat(h, 1 if up else 3, dg)
+                ref[...] = ref[...] + r1[h, dg]
+                send2(h, up, dg)
+    def plane(h, dg):
+        for s in range(2):
+            arrived(r2.at[h, s, dg], s2.at[h, s, dg], q2.at[h, s, dg])
+        ref = zat(h, 0, dg)
+        ref[...] = ref[...] + r2[h, 0, dg] + r2[h, 1, dg]
+
+    hh = hr // 2
+
+    def part(h, dg, k):
+        dz, dy = (0, dg) if order[h] == "z" else (dg, 0)
+        return zb.at[dz, dy, pl.ds(h * hr + k * hh, hh)]
+
+    def send4(h, up, k):
+        dg, d, s = (1, 1, 0) if up else (3, 3, 1)
+        send(part(h, dg, k), r4.at[h, s, k], s4.at[h, s, k], q4.at[h, s, k], at.step(order[h], 1, d))
+
+    for h in range(2):
+        plane(h, 2)
+        send(part(h, 2, 0), r3.at[h, 0], s3.at[h, 0], q3.at[h, 0], at.step(order[h], 1, 1))
+        send(part(h, 2, 1), r3.at[h, 1], s3.at[h, 1], q3.at[h, 1], at.step(order[h], 1, 3))
+    for h in range(2):
+        plane(h, 1)
+        send4(h, True, 1)
+        plane(h, 3)
+        send4(h, False, 0)
+    for h in range(2):
+        plane(h, 0)
+    for h in range(2):
+        arrived(r3.at[h, 0], s3.at[h, 0], q3.at[h, 0])
+        ref = part(h, 1, 0)
+        ref[...] = ref[...] + r3[h, 0]
+        send4(h, True, 0)
+        arrived(r3.at[h, 1], s3.at[h, 1], q3.at[h, 1])
+        ref = part(h, 3, 1)
+        ref[...] = ref[...] + r3[h, 1]
+        send4(h, False, 1)
+    own_x.wait()
+    for h in range(2):
+        for k in range(2):
+            for s in range(2):
+                arrived(r4.at[h, s, k], s4.at[h, s, k], q4.at[h, s, k])
+            z = zb[0, 0, pl.ds(h * hr + k * hh, hh)] + r4[h, 0, k] + r4[h, 1, k]
+            n = hh // gp
+            for i in range(n):
+                x = h * 2 * n + k * n + i
+                yv[x] = (xv[x].astype(jnp.float32) + z[i * gp:(i + 1) * gp]).astype(jnp.bfloat16)
+    own_y = pltpu.make_async_copy(yv.at[at.x], y_ref.at[at.x], loc_sem.at[1])
+    own_y.start()
+    for d in range(1, xs):
+        to = (at.x + d) % xs
+        send(yv.at[to], y_ref.at[at.x], ys.at[d - 1], yq.at[d - 1], at.on_x(to))
+    for d in range(1, xs):
+        arrived(y_ref.at[(at.x + xs - d) % xs], ys.at[d - 1], yq.at[d - 1])
+    own_y.wait()
+    for copy in started:
+        copy.wait_send()
+
+
+def project_and_scatter(w2, mlp_t, attn_rows, xg):
+    yzs, block, _ = w2.shape
+    xs, _, gp, rows = xg.shape
+    c_a = attn_rows.shape[1]
+    dma = pltpu.SemaphoreType.DMA
+    vmem = lambda *s: pltpu.VMEM(s, jnp.float32)
+    hr = block // 2
+    return pl.pallas_call(
+        functools.partial(scatter_kernel, xs, c_a),
+        out_shape=jax.ShapeDtypeStruct((xs, gp, rows), jnp.bfloat16),
+        in_specs=[pl.BlockSpec(memory_space=pltpu.VMEM)] * 3 + [pl.BlockSpec(memory_space=pl.ANY)],
+        out_specs=pl.BlockSpec(memory_space=pl.ANY),
+        scratch_shapes=[
+            vmem(RING, RING, block, rows),
+            vmem(2, RING, hr, rows),
+            vmem(2, 2, RING, hr, rows),
+            vmem(2, 2, hr // 2, rows),
+            vmem(2, 2, 2, hr // 2, rows),
+            pltpu.VMEM((xs, gp, rows), jnp.bfloat16),
+            pltpu.VMEM((xs, gp, rows), jnp.bfloat16),
+            dma((2,)),
+            dma((2, RING)), dma((2, RING)),
+            dma((2, 2, RING)), dma((2, 2, RING)),
+            dma((2, 2)), dma((2, 2)),
+            dma((2, 2, 2)), dma((2, 2, 2)),
+            dma((xs - 1,)), dma((xs - 1,)),
+        ],
+        compiler_params=pltpu.CompilerParams(collective_id=1, has_side_effects=True, vmem_limit_bytes=VMEM_LIMIT),
+        name="project_and_scatter",
+    )(w2, mlp_t, attn_rows, xg)
 
 
 def solution(mesh):
@@ -50,23 +374,23 @@
         w1_loc = jnp.concatenate([wqkv_loc, wgate_loc, wup_loc], axis=1)
         n1 = w1_loc.shape[1]
         w1_loc = jnp.pad(w1_loc.reshape(yzs, grp, n1), ((0, 0), (0, pad), (0, 0))).reshape(yzs * gp, n1)
-        w1 = lax.all_gather(w1_loc, "x", axis=0, tiled=True)
         w2_loc = jnp.concatenate([wao_loc, wmo_loc], axis=0).T
         n2 = w2_loc.shape[1]
         w2_loc = jnp.pad(w2_loc.reshape(yzs, grp, n2), ((0, 0), (0, pad), (0, 0))).reshape(yzs * gp, n2)
         w2 = lax.all_gather(w2_loc, "x", axis=0, tiled=False)
+        w2_p = w2.reshape(xs, yzs, gp, n2).transpose(1, 0, 2, 3).reshape(yzs, xs * gp, n2)
 
         x_t = x_loc.T.reshape(grp, xs, rows).transpose(1, 0, 2)
         gain_row = jnp.broadcast_to(jnp.pad(gain_loc, (0, rows - grp)).reshape(1, 1, rows), (xs, 1, rows))
         x_pad = jnp.concatenate([x_t, gain_row, jnp.zeros((xs, pad - 1, rows), bf16)], axis=1)
-        x_mine = lax.all_to_all(x_pad, "x", 0, 0, tiled=True)
-        x_all = lax.all_gather(x_mine, "yz", axis=0, tiled=False)
+        x_all, w1 = gather_inputs(x_pad, w1_loc, xs, yzs)
+        w1 = w1.reshape(xs * yzs * gp, n1)
         gain = x_all[:, :, grp, :grp].astype(f32)[..., None]
         x_f32 = x_all[:, :, :grp, :].astype(f32)
         row_mean = jnp.sum(x_f32, axis=(0, 1, 2), keepdims=True) / d_model
         row_var = jnp.sum(x_f32 * x_f32, axis=(0, 1, 2), keepdims=True) / d_model - row_mean * row_mean
         normed = ((x_f32 - row_mean) * lax.rsqrt(row_var + 1e-6) * gain).astype(bf16)
-        normed = jnp.pad(normed, ((0, 0), (0, 0), (0, pad), (0, 0))).transpose(1, 0, 2, 3).reshape(xs * yzs * gp, rows)
+        normed = jnp.pad(normed, ((0, 0), (0, 0), (0, pad), (0, 0))).reshape(xs * yzs * gp, rows)
 
         c_q = wqkv_loc.shape[1]
         c_f = wgate_loc.shape[1]
@@ -88,14 +412,7 @@
         attn_dev = attend_local(q_rot, k_all, v_all, len_loc).reshape(dev_rows, attn_cols)
         attn_rows = lax.all_to_all(attn_dev, "yz", 1, 0, tiled=True)
 
-        w2_p = w2.reshape(xs, yzs, gp, n2).transpose(1, 0, 2, 3).reshape(yzs * xs * gp, n2)
-        c_a = wao_loc.shape[0]
-        z_part = jnp.dot(w2_p[:, c_a:], mlp_t, preferred_element_type=f32)
-        z_part = z_part + lax.dot_general(w2_p[:, :c_a], attn_rows, (((1,), (1,)), ((), ())), preferred_element_type=f32)
-        z_loc = lax.psum_scatter(z_part, "yz", scatter_dimension=0, tiled=True)
-        z_loc = z_loc.reshape(xs, gp, rows)
-        y_mine = (x_mine.astype(f32) + z_loc).astype(bf16)
-        y_back = lax.all_to_all(y_mine, "x", 0, 0, tiled=True)
+        y_back = project_and_scatter(w2_p, mlp_t, attn_rows, x_all)
         y_loc = y_back[:, :grp].transpose(1, 0, 2).reshape(grp, n_rows).T
         return y_loc, k_all, v_all
 

time: 367 us -> 267 us (0.73)
  waiting for transfers between devices: 214 us -> 0.67 us
  Pallas kernels: 0 us -> 165 us
  blocking collectives: 27.7 us -> 0 us
  matrix products: 51.7 us -> 28.3 us
    pallas_call x0 -> x2, Pallas kernels: none -> 165 us  [the longest x1 83.5 us: project_and_scatter(): pl.pallas_call(functools.partial(scatter_kernel, xs, c_a), out_shape=jax....]
    all_gather x2 -> x0, waiting for transfers between devices: 96.9 us -> none  [the longest x1 48.9 us: local_layer(): x_all = lax.all_gather(x_mine, 'yz', axis=0, tiled=False)]
    reduce_scatter x1 -> x0, waiting for transfers between devices: 93.8 us -> none  [local_layer(): z_loc = lax.psum_scatter(z_part, 'yz', scatter_dimension=0, tiled=True)]
    all_to_all x2 -> x0, blocking collectives: 27.7 us -> none  [the longest x1 14 us: local_layer(): y_back = lax.all_to_all(y_mine, 'x', 0, 0, tiled=True)]
    all_gather x1, waiting for transfers between devices: 22.9 us -> 0.01 us  [local_layer(): w2 = lax.all_gather(w2_loc, 'x', axis=0, tiled=False)]
    dot_general x2 -> x0, matrix products: 22 us -> none  [the longest x1 11.4 us: local_layer(): lax.dot_general(w2_p[:, :c_a], attn_rows, (((1,), (1,)), ((), ())), prefe...]
    unnamed x26 -> x24, local copies, waits for them, and re-layouts: 1.41 us -> 7.13 us
    transpose x4 -> x1, local copies, waits for them, and re-layouts: 10.4 us -> 5.67 us  [local_layer(): w2.reshape(xs, yzs, gp, n2).transpose(1, 0, 2, 3).reshape(yzs, xs * gp, n2)]
  transfers between devices with their start and end apart: 6 -> 3, of which waited for: 5 -> 1; matrix products, arithmetic and copies ran while one was open for 16% -> 24% of each run, Pallas kernels for 0% -> 31%
where the time goes in v2:
time: 267 us; the launch traced here: 266 us
  Pallas kernels  165 us (62%)
  local copies, waits for them, and re-layouts  32.3 us (12%)
  matrix products  28.3 us (11%)
  between operations  14.4 us (5%)
  other arithmetic  13.9 us (5%)
  starting transfers between devices  12 us (4%)
    pallas_call x1, Pallas kernels, project_and_scatter(): pl.pallas_call(functools.partial(scatter_kernel, xs, c_a), out_shape=jax....  83.5 us
    pallas_call x1, Pallas kernels, gather_inputs(): pl.pallas_call(functools.partial(gather_kernel, xs), out_shape=(jax.Shape...  81.3 us
    dot_general x1, matrix products, local_layer(): lax.dot_general(w1[:, c_q:c_q + c_f], normed, cd, preferred_element_type=...  11.3 us
    dot_general x1, matrix products, local_layer(): lax.dot_general(w1[:, c_q + c_f:], normed, cd, preferred_element_type=f32)  10.1 us
    all_gather x1, local copies, waits for them, and re-layouts, local_layer(): w2 = lax.all_gather(w2_loc, 'x', axis=0, tiled=False)  7.97 us
    unnamed x24, local copies, waits for them, and re-layouts  7.13 us
    all_to_all x1, starting transfers between devices, local_layer(): attn_rows = lax.all_to_all(attn_dev, 'yz', 1, 0, tiled=True)  6.01 us
    all_to_all x1, starting transfers between devices, local_layer(): qkv_dev = lax.all_to_all(qkv, 'yz', 0, 1, tiled=True)  5.96 us
  transfers between devices with their start and end apart: 3, of which 1 were waited for; matrix products, arithmetic and copies ran while one was open for 24% of the time, Pallas kernels for 31%

profile of v2, /device:TPU:1, one launch (start us, length us, event | category | flops | bytes accessed | tf_op | source)
XLA Modules:
  0.0 266.3 jit_solution(5682702241792055244)
XLA Ops:
  7.2 0.0 copy-start.7
  7.2 0.0 copy-start.5
  7.2 0.0 copy-start.6
  7.2 0.0 all-gather.2.cloned.1.call-start
  7.2 1.2 maximum_bitcast_fusion
  8.5 0.3 copy.23
  8.8 0.2 reshape.196
  9.0 0.1 pad.16
  9.1 1.2 copy.24
  10.3 0.0 all-gather.2.cloned.1.call-update
  10.3 0.0 copy-done.7
  10.3 0.1 copy.28
  10.4 0.0 copy-done.5
  10.5 0.0 copy-done.6
  10.5 0.0 copy-start.9
  10.5 1.3 concatenate.23
  11.8 0.4 reshape.200
  12.2 1.1 pad.18
  13.4 1.2 copy.33
  14.6 0.2 copy.36
  14.8 0.0 copy-done.9
  14.8 0.1 pad.26.clone
  14.9 0.9 maximum_maximum_fusion.x_ref
  15.8 81.3 %gather_inputs.1 = (bf16[8,16,24,1024]{3,2,1,0:T(8,128)(2,1)}, bf16[8,384,1600]{2,1,0:T(8,128)(2,1)}) custom-call(bf16[8,24,1024]{2,1,0:T(8,128)(2,1)} %maximum_maximum_fusion.x_ref, bf16[384,1600]{1,0:T(8,128)(2,1)} %bitcast.43), custom_call_target="tpu_custom_call" | custom-call | tf_op jit(solution)/shard_map/gather_inputs/pallas_call | solution.py:188
  97.1 0.0 copy-start
  97.1 4.9 %convert_reduce_fusion = (f32[1024]{0:T(1024)S(1)}, f32[1024]{0:T(1024)S(1)}) fusion(bf16[8,16,24,1024]{3,2,1,0:T(8,128)(2,1)} %get-tuple-element.6.xg_ref), kind=kLoop, calls=%fused_computation.3 | loop fusion | flops 11532288 | bytes 5775360 | tf_op jit(solution)/shard_map/reduce_sum | solution.py:390
  102.0 0.1 slice_convert_fusion.1
  102.1 2.0 fusion.3
  104.1 1.4 pad.19
  105.5 0.0 copy-start.2
  105.5 2.6 copy-done.2
  108.1 2.9 %fusion.27 = bf16[1024,192]{0,1:T(8,128)(2,1)S(1)} fusion(bf16[3072,1024]{1,0:T(8,128)(2,1)S(1)} %bitcast.40, bf16[3072,1600]{1,0:T(8,128)(2,1)} %bitcast.53), kind=kOutput, calls=%fused_computation.29 | convolution fusion | flops 1208156160 | bytes 8257536 | tf_op jit(solution)/shard_map/dot_general | solution.py:398
  111.0 1.0 copy.29
  112.0 6.0 %all-to-all-start = ((bf16[16,64,192]{2,1,0:T(8,128)(2,1)}), bf16[16,64,192]{2,1,0:T(8,128)(2,1)S(1)}, u32[]{:S(2)}, u32[]{:S(2)}) async-start(bf16[16,64,192]{2,1,0:T(8,128)(2,1)} %bitcast.11), calls=%async_computation | async-start | bytes 1048576 | tf_op jit(solution)/shard_map/all_to_all | solution.py:403
  118.0 0.0 copy-start.8
  118.0 10.1 %fusion.19 = bf16[704,1024]{1,0:T(8,128)(2,1)} fusion(bf16[3072,1024]{1,0:T(8,128)(2,1)} %bitcast.41, bf16[3072,1600]{1,0:T(8,128)(2,1)} %bitcast.54), kind=kOutput, calls=%fused_computation.22 | convolution fusion | flops 4429905920 | bytes 12451840 | tf_op jit(solution)/shard_map/dot_general | solution.py:400
  128.1 0.0 copy-done.8
  128.1 0.1 iota_compare_fusion.1
  128.2 0.7 all-to-all-done
  128.8 0.3 copy.30
  129.1 0.5 all_to_all.31
  129.7 0.1 reshape.206
  129.9 0.2 multiply_cosine_fusion
  130.1 0.1 pad_maximum_fusion
  130.1 0.4 subtract_convert_fusion
  130.5 3.5 %broadcast_select_fusion.1 = (bf16[64,128,128]{2,1,0:T(8,128)(2,1)S(1)}, bf16[64,128,128]{2,1,0:T(8,128)(2,1)S(1)}) fusion(bf16[64,128,128]{2,1,0:T(8,128)(2,1)} %param.17, pred[64,128]{1,0:T(8,128)(4,1)S(1)} %get-tuple-element.24, bf16[64,128]{1,0:T(8,128)(2,1)S(1)} %pad_maximum_fusion, bf16[64,128,128]{2,1,0:T(8,128)(2,1)} %param.18, ...), kind=kLoop, calls=%fused_computation.20 | loop fusion | flops 2097152 | bytes 8429568 | tf_op jit(solution)/shard_map/jit(_where)/select_n | solution.py:410
  134.1 0.0 copy-start.1
  134.1 0.0 copy-start.4
  134.1 1.3 copy-done.1
  135.4 1.2 fusion.26
  136.6 0.5 fusion.36
  137.1 2.8 %convolution_convert_fusion = bf16[64,22,128]{2,1,0:T(8,128)(2,1)S(1)} fusion(bf16[64,128,128]{2,1,0:T(8,128)(2,1)S(1)} %get-tuple-element.16, f32[64,22]{1,0:T(8,128)S(1)} %fusion.36, f32[64,22,128]{2,1,0:T(8,128)S(1)} %fusion.26), kind=kOutput, calls=%fused_computation.30 | convolution fusion | flops 46859776 | bytes 3184128 | tf_op jit(solution)/shard_map/bht,btd->bhd/dot_general | solution.py:33
  139.9 1.1 all_to_all.32
  141.0 0.9 copy.31
  141.9 6.0 %all-to-all-start.1 = ((bf16[64,16,176]{2,0,1:T(8,128)(2,1)}), bf16[64,16,176]{2,0,1:T(8,128)(2,1)S(1)}, u32[]{:S(2)}, u32[]{:S(2)}) async-start(bf16[64,16,176]{2,0,1:T(8,128)(2,1)} %copy.31), calls=%async_computation.1 | async-start | bytes 1048576 | tf_op jit(solution)/shard_map/all_to_all | solution.py:413
  148.0 11.3 %fusion.13.a_ref = bf16[704,1024]{1,0:T(8,128)(2,1)} fusion(bf16[704,1024]{1,0:T(8,128)(2,1)} %fusion.19, bf16[3072,1024]{1,0:T(8,128)(2,1)} %bitcast.42, bf16[3072,1600]{1,0:T(8,128)(2,1)} %bitcast.55), kind=kOutput, calls=%fused_computation.18 | convolution fusion | flops 4435673088 | bytes 13893632 | tf_op jit(solution)/shard_map/dot_general | solution.py:399
  159.3 8.0 %copy.25 = bf16[8,384,880]{2,1,0:T(8,128)(2,1)} copy(bf16[8,384,880]{1,2,0:T(8,128)(2,1)} %all-gather.2.cloned.1.call-done) | data formatting | bytes 10813440 | tf_op jit(solution)/shard_map/all_gather | solution.py:380
  167.2 5.7 %copy.26 = bf16[16,8,24,880]{3,2,1,0:T(8,128)(2,1)} copy(bf16[16,8,24,880]{3,2,0,1:T(8,128)(2,1)} %bitcast.39) | data formatting | bytes 10813440 | tf_op jit(solution)/shard_map/transpose | solution.py:381
  172.9 0.0 all-to-all-done.1
  172.9 0.8 copy-done.3
  173.7 83.5 %project_and_scatter.1 = bf16[8,24,1024]{2,1,0:T(8,128)(2,1)} custom-call(bf16[16,192,880]{2,1,0:T(8,128)(2,1)} %bitcast.38, bf16[704,1024]{1,0:T(8,128)(2,1)} %fusion.13.a_ref, bf16[1024,176]{1,0:T(8,128)(2,1)} %bitcast.45, bf16[8,16,24,1024]{3,2,1,0:T(8,128)(2,1)} %get-tuple-element.6.xg_ref), custom_call_target="tpu_custom_call" | custom-call | tf_op jit(solution)/shard_map/project_and_scatter/pallas_call | solution.py:327
  257.2 1.0 slice_bitcast_fusion
  258.3 0.2 copy.32
  258.5 1.0 copy.34
  (13 shorter events, 0.2 us)
Async XLA Ops:
  7.2 3.1 %copy-start.7 = (bf16[352,192]{0,1:T(8,128)(2,1)S(1)}, bf16[352,192]{0,1:T(8,128)(2,1)}, u32[]{:S(2)}) copy-start(bf16[352,192]{0,1:T(8,128)(2,1)} %param.12) | copy-start | bytes 405508
  7.2 3.3 %copy-start.5 = (bf16[352,704]{1,0:T(8,128)(2,1)S(1)}, bf16[352,704]{1,0:T(8,128)(2,1)}, u32[]{:S(2)}) copy-start(bf16[352,704]{1,0:T(8,128)(2,1)} %param.13) | copy-start | bytes 1486852
  7.2 3.3 %copy-start.6 = (bf16[352,704]{1,0:T(8,128)(2,1)S(1)}, bf16[352,704]{1,0:T(8,128)(2,1)}, u32[]{:S(2)}) copy-start(bf16[352,704]{1,0:T(8,128)(2,1)} %param.14) | copy-start | bytes 1486852
  7.2 152.1 %all-gather.2.cloned.1.call-start = ((), (), s32[]{:S(2)}) async-start(), calls=%async_computation.2 | async-start | bytes 6082560 | tf_op jit(solution)/shard_map/all_gather | solution.py:380
  10.5 4.4 %copy-start.9 = (bf16[22]{0:T(256)(128)(2,1)S(1)}, bf16[22]{0:T(256)(128)(2,1)}, u32[]{:S(2)}) copy-start(bf16[22]{0:T(256)(128)(2,1)} %param.11) | copy-start | bytes 136
  97.1 4.9 %copy-start = (bf16[8,16,24,1024]{3,2,1,0:T(8,128)(2,1)S(1)}, bf16[8,16,24,1024]{3,2,1,0:T(8,128)(2,1)}, u32[]{:S(2)}) copy-start(bf16[8,16,24,1024]{3,2,1,0:T(8,128)(2,1)} %get-tuple-element.6.xg_ref) | copy-start | bytes 18874372
  105.5 2.6 copy-start.2
  112.0 16.8 %all-to-all-start = ((bf16[16,64,192]{2,1,0:T(8,128)(2,1)}), bf16[16,64,192]{2,1,0:T(8,128)(2,1)S(1)}, u32[]{:S(2)}, u32[]{:S(2)}) async-start(bf16[16,64,192]{2,1,0:T(8,128)(2,1)} %bitcast.11), calls=%async_computation | async-start | bytes 1048576 | tf_op jit(solution)/shard_map/all_to_all | solution.py:403
  118.0 10.1 %copy-start.8 = (s32[64]{0:T(128)S(1)}, s32[64]{0:T(128)}, u32[]{:S(2)}) copy-start(s32[64]{0:T(128)} %param.19) | copy-start | bytes 772
  134.1 1.3 copy-start.1
  134.1 6.9 %copy-start.4 = (bf16[64,128,128]{2,1,0:T(8,128)(2,1)}, bf16[64,128,128]{2,1,0:T(8,128)(2,1)S(1)}, u32[]{:S(2)}) copy-start(bf16[64,128,128]{2,1,0:T(8,128)(2,1)S(1)} %get-tuple-element.16) | copy-start | bytes 6291460
  141.9 31.0 %all-to-all-start.1 = ((bf16[64,16,176]{2,0,1:T(8,128)(2,1)}), bf16[64,16,176]{2,0,1:T(8,128)(2,1)S(1)}, u32[]{:S(2)}, u32[]{:S(2)}) async-start(bf16[64,16,176]{2,0,1:T(8,128)(2,1)} %copy.31), calls=%async_computation.1 | async-start | bytes 1048576 | tf_op jit(solution)/shard_map/all_to_all | solution.py:413
  172.9 0.8 copy-start.3
Sparse Core Ops, SparseCore 0:
  10.4 64.0 all-gather.1

commit v3 on v2

v3 whole, which is shorter than its diff:
```python
import functools

import jax
import jax.numpy as jnp
from jax import lax
from jax.experimental import pallas as pl
from jax.experimental.pallas import tpu as pltpu
from jax.sharding import PartitionSpec as P

MESH = pl.DeviceIdType.MESH
RING = 4
VMEM_LIMIT = 62 * 1024 * 1024


def apply_rope(vecs, positions):
    half_dim = vecs.shape[-1] // 2
    inv_freq = 10000.0 ** (-jnp.arange(half_dim, dtype=jnp.float32) / half_dim)
    angles = positions.astype(jnp.float32)[..., None] * inv_freq
    cos_t = jnp.cos(angles)
    sin_t = jnp.sin(angles)
    first_half = vecs[..., :half_dim]
    second_half = vecs[..., half_dim:]
    return jnp.concatenate([first_half * cos_t - second_half * sin_t, second_half * cos_t + first_half * sin_t], axis=-1)


def attend_local(q_rot, k_all, v_all, ctx_len):
    head_dim = q_rot.shape[-1]
    positions = jnp.arange(k_all.shape[1])
    scores = jnp.einsum("bhd,btd->bht", q_rot, k_all, preferred_element_type=jnp.float32) * head_dim ** -0.5
    visible = (positions[None, :] <= ctx_len[:, None])[:, None, :]
    scores = jnp.where(visible, scores, -1e30)
    attn_probs = jax.nn.softmax(scores, axis=-1).astype(jnp.bfloat16)
    return jnp.einsum("bht,btd->bhd", attn_probs, v_all, preferred_element_type=jnp.float32).astype(jnp.bfloat16)


class Where:
    def __init__(self, xs, yzs):
        self.xs = xs
        self.yzs = yzs
        self.dp = lax.axis_index("dp")
        self.x = lax.axis_index("x")
        self.j = lax.axis_index("yz")
        self.zz = self.j // RING
        self.yy = self.j % RING
        self.chip = self.x // 2
        self.core = self.x % 2

    def block(self, dz, dy):
        return ((self.zz + dz) % RING) * RING + (self.yy + dy) % RING

    def on_yz(self, j):
        return (self.dp, j, self.x)

    def on_x(self, x):
        return (self.dp, self.j, x)

    def axis_block(self, first, df, dg):
        return self.block(df, dg) if first == "z" else self.block(dg, df)

    def step(self, first, axis, d):
        return self.on_yz(self.axis_block(first, d, 0) if axis == 0 else self.axis_block(first, 0, d))

    def x_of(self, dc):
        return ((self.chip + dc) % RING) * 2 + self.core

    def x_other(self, dc):
        return ((self.chip + dc) % RING) * 2 + (1 - self.core)

    def greet(self):
        barrier = pltpu.get_barrier_semaphore()
        peers = [self.on_x((self.x + d) % self.xs) for d in range(1, self.xs)]
        peers += [self.on_yz((self.j + d) % self.yzs) for d in range(1, self.yzs)]
        for peer in peers:
            pl.semaphore_signal(barrier, inc=1, device_id=peer, device_id_type=MESH)
        pl.semaphore_wait(barrier, len(peers))


class Copies:
    def __init__(self, any_peer):
        self.any_peer = any_peer
        self.started = []

    def send(self, src, dst, ssem, rsem, peer):
        copy = pltpu.make_async_remote_copy(src_ref=src, dst_ref=dst, send_sem=ssem, recv_sem=rsem, device_id=peer, device_id_type=MESH)
        copy.start()
        self.started.append(copy)

    def arrived(self, dst, ssem, rsem):
        pltpu.make_async_remote_copy(
            src_ref=dst, dst_ref=dst, send_sem=ssem, recv_sem=rsem, device_id=self.any_peer, device_id_type=MESH
        ).wait_recv()

    def finish(self):
        for copy in self.started:
            copy.wait_send()


def front_kernel(xs, yzs, grp, c_q, c_f, x_ref, w1_ref, w2_ref, act_ref, qkv_ref, w2g_ref, xo_ref, xg, h, w1, qkv_s, loc_sem, xsend, xrecv, gsend, grecv, wsend, wrecv, vsend, vrecv, qsend, qrecv):
    f32, bf16 = jnp.float32, jnp.bfloat16
    at = Where(xs, yzs)
    half = xs // 2
    quarter = half // 2
    gp, rows = x_ref.shape[1:]
    dev_rows = rows // yzs
    kx = w1_ref.shape[1]
    at.greet()
    copies = Copies(at.on_yz(at.block(0, 1)))

    def send(src, dst, sems, idx, peer):
        copies.send(src, dst, sems[0].at[idx], sems[1].at[idx], peer)

    def arrived(region, sems, idx):
        copies.arrived(region, sems[0].at[idx], sems[1].at[idx])

    xsem, wsem, vsem, qsem = (xsend, xrecv), (wsend, wrecv), (vsend, vrecv), (qsend, qrecv)
    own_x = pltpu.make_async_copy(x_ref.at[at.x], xg.at[at.x, at.j], loc_sem.at[0])
    own_x.start()
    for d in range(1, xs):
        to = (at.x + d) % xs
        send(x_ref.at[to], xg.at[at.x, at.j], xsem, d - 1, at.on_x(to))

    n1 = w1_ref.shape[0]
    n2 = w2_ref.shape[0]

    def w1_at(x, k=None):
        cols = pl.ds(pl.multiple_of(x * kx, 128), kx)
        return w1.at[:, cols] if k is None else w1.at[pl.ds(k * (n1 // 2), n1 // 2), cols]

    def w2_at(x, k=None):
        return w2g_ref.at[:, x] if k is None else w2g_ref.at[pl.ds(k * (n2 // 2), n2 // 2), x]

    def spread_own(src, region, sems, loc):
        own = pltpu.make_async_copy(src, region(at.x), loc_sem.at[loc])
        own.start()
        send(src, region(at.x), sems, 0, at.on_x(at.x_of(1)))
        send(src, region(at.x), sems, 1, at.on_x(at.x_of(3)))
        send(src, region(at.x), sems, 2, at.on_x(at.x_other(0)))
        return own

    def pass_on(r, sems, slot, x):
        send(r, r, sems, slot, at.on_x(x))

    def forward_near(region, sems):
        arrived(region(at.x_of(3)), sems, 0)
        pass_on(region(at.x_of(3), 0), sems, 3, at.x_of(1))
        arrived(region(at.x_of(1)), sems, 1)
        pass_on(region(at.x_of(1), 1), sems, 4, at.x_of(3))
        pass_on(region(at.x_of(3)), sems, 5, at.x_other(0))
        pass_on(region(at.x_of(1)), sems, 6, at.x_other(0))

    def forward_far(region, sems):
        arrived(region(at.x_of(2), 0), sems, 3)
        pass_on(region(at.x_of(2), 0), sems, 7, at.x_other(0))
        arrived(region(at.x_of(2), 1), sems, 4)
        pass_on(region(at.x_of(2), 1), sems, 8, at.x_other(0))

    def all_in(region, sems, own):
        arrived(region(at.x_other(0)), sems, 2)
        arrived(region(at.x_other(3)), sems, 5)
        arrived(region(at.x_other(1)), sems, 6)
        arrived(region(at.x_other(2), 0), sems, 7)
        arrived(region(at.x_other(2), 1), sems, 8)
        own.wait()

    own_w1 = spread_own(w1_ref, w1_at, wsem, 1)
    own_x.wait()
    for d in range(1, xs):
        arrived(xg.at[(at.x + xs - d) % xs, at.j], xsem, d - 1)

    order = ("y", "z")

    def region(h_, df, dg, lo=0, n=half):
        return xg.at[pl.ds(h_ * half + lo, n), at.axis_block(order[h_], df, dg)]

    def gsend_block(h_, df, dg, axis, d, slot, lo=0, n=half):
        r = region(h_, df, dg, lo, n)
        send(r, r, (gsend.at[h_], grecv.at[h_]), slot, at.step(order[h_], axis, d))

    def garrived(h_, df, dg, slot, lo=0, n=half):
        arrived(region(h_, df, dg, lo, n), (gsend.at[h_], grecv.at[h_]), slot)

    for h_ in range(2):
        gsend_block(h_, 0, 0, 0, 1, 0)
        gsend_block(h_, 0, 0, 0, 3, 1)
        gsend_block(h_, 0, 0, 1, 1, 4)
        gsend_block(h_, 0, 0, 1, 3, 8)
    xo_ref[...] = xg[:, at.j]
    for h_ in range(2):
        garrived(h_, 3, 0, 0)
        gsend_block(h_, 3, 0, 0, 1, 2, 0, quarter)
        garrived(h_, 1, 0, 1)
        gsend_block(h_, 1, 0, 0, 3, 3, quarter, quarter)
        gsend_block(h_, 3, 0, 1, 1, 4 + 3)
        gsend_block(h_, 3, 0, 1, 3, 8 + 3)
        gsend_block(h_, 1, 0, 1, 1, 4 + 1)
        gsend_block(h_, 1, 0, 1, 3, 8 + 1)
    for h_ in range(2):
        garrived(h_, 2, 0, 2, 0, quarter)
        garrived(h_, 2, 0, 3, quarter, quarter)
        gsend_block(h_, 2, 0, 1, 1, 4 + 2)
        gsend_block(h_, 2, 0, 1, 3, 8 + 2)
    for h_ in range(2):
        for df in (0, 3):
            garrived(h_, df, 3, 4 + df)
            gsend_block(h_, df, 3, 1, 1, 12 + df)
    forward_near(w1_at, wsem)
    own_w2 = spread_own(w2_ref, w2_at, vsem, 2)
    for h_ in range(2):
        for df in (1, 2):
            garrived(h_, df, 1, 8 + df)
            gsend_block(h_, df, 1, 1, 3, 12 + df)
    for h_ in range(2):
        for df in (1, 2):
            garrived(h_, df, 3, 4 + df)
        for df in (0, 3):
            garrived(h_, df, 1, 8 + df)
        for df in range(4):
            garrived(h_, df, 2, 12 + df)

    pairs = yzs // 2
    feature = lax.broadcasted_iota(jnp.int32, (2, gp, 1), 1).reshape(2 * gp, 1)
    real = feature < grp
    diagonal = lax.broadcasted_iota(jnp.int32, (gp, 128), 0) == lax.broadcasted_iota(jnp.int32, (gp, 128), 1)

    def load(q):
        return xg[q // pairs, pl.ds((q % pairs) * 2, 2)].astype(f32).reshape(2 * gp, rows)

    def add_up(q, sums):
        v = jnp.where(real, load(q), 0.0)
        parts = v.reshape(2 * gp // 8, 8, rows)
        return sums[0] + jnp.sum(parts, axis=0), sums[1] + jnp.sum(parts * parts, axis=0)

    zero = jnp.zeros((8, rows), f32)
    s1, s2 = lax.fori_loop(0, xs * pairs, add_up, (zero, zero))
    d_model = grp * xs * yzs
    mean = jnp.sum(s1, axis=0, keepdims=True) / d_model
    var = jnp.sum(s2, axis=0, keepdims=True) / d_model - mean * mean
    scale = lax.rsqrt(var + 1e-6)

    def normalize(q, c):
        v = load(q)
        gains = [
            jnp.sum(jnp.where(diagonal, v[k * gp + grp:k * gp + grp + 1, :128], 0.0), axis=1, keepdims=True)
            for k in range(2)
        ]
        out = (v - mean) * scale * jnp.concatenate(gains, axis=0)
        h[pl.ds(pl.multiple_of(q * 2 * gp, 16), 2 * gp), :] = jnp.where(real, out, 0.0).astype(bf16)
        return c

    lax.fori_loop(0, xs * pairs, normalize, 0)
    forward_far(w1_at, wsem)
    all_in(w1_at, wsem, own_w1)

    nt = 256

    def query(n, c):
        q = jnp.dot(w1[:c_q], h[:, pl.ds(pl.multiple_of(n * nt, nt), nt)], preferred_element_type=f32)
        qkv_s[pl.ds(pl.multiple_of(n * nt, nt), nt), :] = q.T.astype(bf16)
        return c

    lax.fori_loop(0, rows // nt, query, 0)
    own_q = pltpu.make_async_copy(qkv_s.at[pl.ds(pl.multiple_of(at.j * dev_rows, dev_rows), dev_rows)], qkv_ref.at[at.j], loc_sem.at[3])
    own_q.start()
    for d in range(1, yzs):
        to = (at.j + d) % yzs
        src = qkv_s.at[pl.ds(pl.multiple_of(to * dev_rows, dev_rows), dev_rows)]
        send(src, qkv_ref.at[at.j], qsem, d - 1, at.on_yz(to))

    def mlp(n, c):
        cols = pl.ds(pl.multiple_of(n * nt, nt), nt)
        gate = jnp.dot(w1[c_q:c_q + c_f], h[:, cols], preferred_element_type=f32).astype(bf16).astype(f32)
        up = jnp.dot(w1[c_q + c_f:], h[:, cols], preferred_element_type=f32).astype(bf16).astype(f32)
        act_ref[:, cols] = (jax.nn.silu(gate) * up).astype(bf16)
        return c

    steps = rows // nt
    lax.fori_loop(0, steps // 2, mlp, 0)
    forward_near(w2_at, vsem)
    lax.fori_loop(steps // 2, steps, mlp, 0)
    forward_far(w2_at, vsem)
    for d in range(1, yzs):
        arrived(qkv_ref.at[(at.j + yzs - d) % yzs], qsem, d - 1)
    own_q.wait()
    all_in(w2_at, vsem, own_w2)
    copies.finish()


def front(x_pad, w1_loc, w2_loc, xs, yzs, grp, c_q, c_f):
    _, gp, rows = x_pad.shape
    n1, kx = w1_loc.shape
    dma = pltpu.SemaphoreType.DMA
    bf16 = jnp.bfloat16
    vspec, aspec = pl.BlockSpec(memory_space=pltpu.VMEM), pl.BlockSpec(memory_space=pl.ANY)
    sems = lambda *s: [dma(s), dma(s)]
    return pl.pallas_call(
        functools.partial(front_kernel, xs, yzs, grp, c_q, c_f),
        out_shape=(
            jax.ShapeDtypeStruct((c_f, rows), bf16),
            jax.ShapeDtypeStruct((yzs, rows // yzs, c_q), bf16),
            jax.ShapeDtypeStruct((yzs, xs) + w2_loc.shape[1:], bf16),
            jax.ShapeDtypeStruct((xs, gp, rows), bf16),
        ),
        in_specs=[vspec] * 3,
        out_specs=(vspec, aspec, aspec, vspec),
        scratch_shapes=[
            pltpu.VMEM((xs, yzs, gp, rows), bf16),
            pltpu.VMEM((xs * yzs * gp, rows), bf16),
            pltpu.VMEM((n1, xs * kx), bf16),
            pltpu.VMEM((rows, c_q), bf16),
            dma((4,)),
        ] + sems(xs - 1) + sems(2, 16) + sems(9) + sems(9) + sems(yzs - 1),
        compiler_params=pltpu.CompilerParams(collective_id=0, has_side_effects=True, vmem_limit_bytes=VMEM_LIMIT),
        name="front",
    )(x_pad, w1_loc, w2_loc)


def back_kernel(xs, yzs, w_ref, a_ref, o_ref, x_ref, y_ref, act, ob, zb, r1, r2, r3, r4, yv, loc_sem, os, oq, s1, q1, s2, q2, s3, q3, s4, q4, ys, yq):
    at = Where(xs, yzs)
    order = ("z", "y")
    hr = zb.shape[2] // 2
    gp = x_ref.shape[1]
    dev_rows = o_ref.shape[1]
    c_f = a_ref.shape[0]
    own_a = pltpu.make_async_copy(a_ref, act.at[pl.ds(0, c_f)], loc_sem.at[2])
    own_a.start()
    at.greet()
    copies = Copies(at.on_yz(at.block(0, 1)))
    send, arrived = copies.send, copies.arrived

    def mine(j):
        return ob.at[pl.ds(pl.multiple_of(j * dev_rows, dev_rows), dev_rows)]

    own_o = pltpu.make_async_copy(o_ref.at[at.j], mine(at.j), loc_sem.at[0])
    own_o.start()
    for d in range(1, yzs):
        to = (at.j + d) % yzs
        send(o_ref.at[to], mine(at.j), os.at[d - 1], oq.at[d - 1], at.on_yz(to))
    own_o.wait()
    for d in range(1, yzs):
        arrived(mine((at.j + yzs - d) % yzs), os.at[d - 1], oq.at[d - 1])
    act[pl.ds(c_f, ob.shape[1]), :] = ob[...].T
    own_a.wait()

    def zat(h, df, dg):
        dz, dy = (df, dg) if order[h] == "z" else (dg, df)
        return zb.at[dz, dy, pl.ds(h * hr, hr)]

    def compute(dz, dy):
        zb[dz, dy] = jnp.dot(w_ref[at.block(dz, dy)], act[...], preferred_element_type=jnp.float32)

    def compute_range(dz, dys):
        def body(i, c):
            compute(dz, i)
            return c

        lax.fori_loop(dys[0], dys[1], body, 0)

    def first(i, c):
        dz = jnp.where(i < RING, 2, (i - RING) + (i - RING) // 2)
        dy = jnp.where(i < RING, i, 2)
        compute(dz, dy)
        return c

    lax.fori_loop(0, 2 * RING - 1, first, 0)
    for h in range(2):
        for dg in range(RING):
            d = 1 if dg < 2 else 3
            send(zat(h, 2, dg), r1.at[h, dg], s1.at[h, dg], q1.at[h, dg], at.step(order[h], 0, d))

    def second(i, c):
        k, m = i // 3, i % 3
        compute(k + k // 2, m + m // 2)
        return c

    lax.fori_loop(0, 9, second, 0)

    def send2(h, up, dg):
        df, d, s = (1, 1, 0) if up else (3, 3, 1)
        send(zat(h, df, dg), r2.at[h, s, dg], s2.at[h, s, dg], q2.at[h, s, dg], at.step(order[h], 0, d))

    for h in range(2):
        for dg in (2, 3):
            send2(h, True, dg)
        for dg in (0, 1):
            send2(h, False, dg)
    for k in range(2):
        for h in range(2):
            for up in (True, False):
                dg = k if up else 2 + k
                arrived(r1.at[h, dg], s1.at[h, dg], q1.at[h, dg])
                ref = zat(h, 1 if up else 3, dg)
                ref[...] = ref[...] + r1[h, dg]
                send2(h, up, dg)

    def plane(h, dg):
        for s in range(2):
            arrived(r2.at[h, s, dg], s2.at[h, s, dg], q2.at[h, s, dg])
        ref = zat(h, 0, dg)
        ref[...] = ref[...] + r2[h, 0, dg] + r2[h, 1, dg]

    hh = hr // 2

    def part(h, dg, k):
        dz, dy = (0, dg) if order[h] == "z" else (dg, 0)
        return zb.at[dz, dy, pl.ds(h * hr + k * hh, hh)]

    def send4(h, up, k):
        dg, d, s = (1, 1, 0) if up else (3, 3, 1)
        send(part(h, dg, k), r4.at[h, s, k], s4.at[h, s, k], q4.at[h, s, k], at.step(order[h], 1, d))

    for h in range(2):
        plane(h, 2)
        send(part(h, 2, 0), r3.at[h, 0], s3.at[h, 0], q3.at[h, 0], at.step(order[h], 1, 1))
        send(part(h, 2, 1), r3.at[h, 1], s3.at[h, 1], q3.at[h, 1], at.step(order[h], 1, 3))
    for h in range(2):
        plane(h, 1)
        send4(h, True, 1)
        plane(h, 3)
        send4(h, False, 0)
    for h in range(2):
        plane(h, 0)
    for h in range(2):
        arrived(r3.at[h, 0], s3.at[h, 0], q3.at[h, 0])
        ref = part(h, 1, 0)
        ref[...] = ref[...] + r3[h, 0]
        send4(h, True, 0)
        arrived(r3.at[h, 1], s3.at[h, 1], q3.at[h, 1])
        ref = part(h, 3, 1)
        ref[...] = ref[...] + r3[h, 1]
        send4(h, False, 1)
    for h in range(2):
        for k in range(2):
            for s in range(2):
                arrived(r4.at[h, s, k], s4.at[h, s, k], q4.at[h, s, k])
            z = zb[0, 0, pl.ds(h * hr + k * hh, hh)] + r4[h, 0, k] + r4[h, 1, k]
            n = hh // gp
            for i in range(n):
                x = h * 2 * n + k * n + i
                yv[x] = (x_ref[x].astype(jnp.float32) + z[i * gp:(i + 1) * gp]).astype(jnp.bfloat16)
    own_y = pltpu.make_async_copy(yv.at[at.x], y_ref.at[at.x], loc_sem.at[1])
    own_y.start()
    for d in range(1, xs):
        to = (at.x + d) % xs
        send(yv.at[to], y_ref.at[at.x], ys.at[d - 1], yq.at[d - 1], at.on_x(to))
    for d in range(1, xs):
        arrived(y_ref.at[(at.x + xs - d) % xs], ys.at[d - 1], yq.at[d - 1])
    own_y.wait()
    copies.finish()


def back(w2, act, attn, x_own):
    yzs, block, n2 = w2.shape
    xs, gp, rows = x_own.shape
    dma = pltpu.SemaphoreType.DMA
    bf16 = jnp.bfloat16
    vmem = lambda *s: pltpu.VMEM(s, jnp.float32)
    vspec, aspec = pl.BlockSpec(memory_space=pltpu.VMEM), pl.BlockSpec(memory_space=pl.ANY)
    sems = lambda *s: [dma(s), dma(s)]
    hr = block // 2
    return pl.pallas_call(
        functools.partial(back_kernel, xs, yzs),
        out_shape=jax.ShapeDtypeStruct((xs, gp, rows), bf16),
        in_specs=[vspec, aspec, vspec, vspec],
        out_specs=aspec,
        scratch_shapes=[
            pltpu.VMEM((n2, rows), bf16),
            pltpu.VMEM((rows, attn.shape[2]), bf16),
            vmem(RING, RING, block, rows),
            vmem(2, RING, hr, rows),
            vmem(2, 2, RING, hr, rows),
            vmem(2, 2, hr // 2, rows),
            vmem(2, 2, 2, hr // 2, rows),
            pltpu.VMEM((xs, gp, rows), bf16),
            dma((3,)),
        ] + sems(yzs - 1) + sems(2, RING) + sems(2, 2, RING) + sems(2, 2) + sems(2, 2, 2) + sems(xs - 1),
        compiler_params=pltpu.CompilerParams(collective_id=1, has_side_effects=True, vmem_limit_bytes=VMEM_LIMIT),
        name="back",
    )(w2, act, attn, x_own)


def solution(mesh):
    xs = mesh.shape["x"]
    yzs = mesh.shape["yz"]
    both_axes = ("x", "yz")
    row_spec = P("dp", both_axes)
    in_w_spec = P("x", "yz")
    out_w_spec = P("yz", "x")
    cache_spec = P(("dp", "x", "yz"), None, None)
    len_spec = P(("dp", "x", "yz"))

    def local_layer(x_loc, gain_loc, wqkv_loc, wgate_loc, wup_loc, wao_loc, wmo_loc, kc_loc, vc_loc, len_loc):
        n_rows, grp = x_loc.shape
        pad = -grp % 8
        gp = grp + pad
        head_dim = kc_loc.shape[2]
        dev_rows = kc_loc.shape[0]
        rows = n_rows // xs
        attn_cols = wao_loc.shape[0] * yzs
        num_heads = attn_cols // head_dim
        f32, bf16 = jnp.float32, jnp.bfloat16

        def pad_groups(w):
            n = w.shape[1]
            return jnp.pad(w.reshape(yzs, grp, n), ((0, 0), (0, pad), (0, 0)))

        w1_loc = jnp.concatenate([wqkv_loc, wgate_loc, wup_loc], axis=1)
        w1_loc = pad_groups(w1_loc).reshape(yzs * gp, -1).T
        w2_loc = pad_groups(jnp.concatenate([wmo_loc, wao_loc], axis=0).T)

        x_t = x_loc.T.reshape(grp, xs, rows).transpose(1, 0, 2)
        gain_row = jnp.broadcast_to(jnp.pad(gain_loc, (0, rows - grp)).reshape(1, 1, rows), (xs, 1, rows))
        x_pad = jnp.concatenate([x_t, gain_row, jnp.zeros((xs, pad - 1, rows), bf16)], axis=1)
        c_q = wqkv_loc.shape[1]
        c_f = wgate_loc.shape[1]
        act, qkv_in, w2, x_own = front(x_pad, w1_loc, w2_loc, xs, yzs, grp, c_q, c_f)

        qkv_dev = qkv_in.transpose(1, 0, 2).reshape(dev_rows, yzs * c_q)
        q_heads = qkv_dev[:, :attn_cols].reshape(dev_rows, num_heads, head_dim)
        k_new = qkv_dev[:, attn_cols:attn_cols + head_dim]
        v_new = qkv_dev[:, attn_cols + head_dim:]
        q_rot = apply_rope(q_heads.astype(f32), len_loc[:, None]).astype(bf16)
        k_rot = apply_rope(k_new.astype(f32), len_loc).astype(bf16)
        new_slot = (jnp.arange(kc_loc.shape[1])[None, :] == len_loc[:, None])[:, :, None]
        k_all = jnp.where(new_slot, k_rot[:, None, :], kc_loc)
        v_all = jnp.where(new_slot, v_new[:, None, :], vc_loc)
        attn = attend_local(q_rot, k_all, v_all, len_loc).reshape(dev_rows, yzs, attn_cols // yzs).transpose(1, 0, 2)

        y_back = back(w2.reshape(yzs, xs * gp, -1), act, attn, x_own)
        y_loc = y_back[:, :grp].transpose(1, 0, 2).reshape(grp, n_rows).T
        return y_loc, k_all, v_all

    in_specs = (row_spec, P(both_axes), in_w_spec, in_w_spec, in_w_spec, out_w_spec, out_w_spec, cache_spec, cache_spec, len_spec)
    out_specs = (row_spec, cache_spec, cache_spec)
    return jax.shard_map(local_layer, mesh=mesh, in_specs=in_specs, out_specs=out_specs, check_vma=False)
```

time: 267 us -> 213 us (0.80)
  matrix products: 28.3 us -> 4.02 us
  Pallas kernels: 165 us -> 184 us
  local copies, waits for them, and re-layouts: 32.3 us -> 16.8 us
  between operations: 14.4 us -> 0.88 us
  starting transfers between devices: 12 us -> 0 us
  other arithmetic: 13.9 us -> 6.98 us
    dot_general x3 -> x0, matrix products: 24.2 us -> none  [the longest x1 11.3 us: local_layer(): lax.dot_general(w1[:, c_q:c_q + c_f], normed, cd, preferred_element_type=...]
    pallas_call x2, Pallas kernels: 165 us -> 184 us  [the longest x1 92.8 us: back(): pl.pallas_call(functools.partial(back_kernel, xs, yzs), out_shape=jax.Sha...]
    all_to_all x2 -> x0, starting transfers between devices: 12 us -> none  [the longest x1 6.01 us: local_layer(): attn_rows = lax.all_to_all(attn_dev, 'yz', 1, 0, tiled=True)]
    all_gather x1 -> x0, local copies, waits for them, and re-layouts: 7.97 us -> none  [local_layer(): w2 = lax.all_gather(w2_loc, 'x', axis=0, tiled=False)]
    reduce_sum x1 -> x0, other arithmetic: 4.88 us -> none  [local_layer(): row_mean = jnp.sum(x_f32, axis=(0, 1, 2), keepdims=True) / d_model]
    transpose x2, local copies, waits for them, and re-layouts: 6 us -> 1.67 us  [the longest x1 1.33 us: local_layer(): qkv_dev = qkv_in.transpose(1, 0, 2).reshape(dev_rows, yzs * c_q)]
    reshape x2 -> x6, local copies, waits for them, and re-layouts: 0.6 us -> 4.69 us  [the longest x2 2.01 us: local_layer(): attend_local(q_rot, k_all, v_all, len_loc)]
    all_to_all x4 -> x0, local copies, waits for them, and re-layouts: 2.85 us -> none  [the longest x2 2.01 us: local_layer(): attn_rows = lax.all_to_all(attn_dev, 'yz', 1, 0, tiled=True)]
  transfers between devices with their start and end apart: 3 -> 0, of which waited for: 1 -> 0; matrix products, arithmetic and copies ran while one was open for 24% -> 0% of each run, Pallas kernels for 31% -> 0%
where the time goes in v3:
time: 213 us
  Pallas kernels  184 us (86%)
  local copies, waits for them, and re-layouts  16.8 us (8%)
  other arithmetic  6.98 us (3%)
  matrix products  4.02 us (2%)
    pallas_call x1, Pallas kernels, back(): pl.pallas_call(functools.partial(back_kernel, xs, yzs), out_shape=jax.Sha...  92.8 us
    pallas_call x1, Pallas kernels, front(): pl.pallas_call(functools.partial(front_kernel, xs, yzs, grp, c_q, c_f), o...  91.4 us
    unnamed x18, local copies, waits for them, and re-layouts  5.8 us

profile of v3, /device:TPU:1, one launch (start us, length us, event | category | flops | bytes accessed | tf_op | source)
XLA Modules:
  0.0 212.9 jit_solution(1901383835292806590)
XLA Ops:
  0.6 0.0 copy-start.5
  0.6 0.0 copy-start.6
  0.7 0.7 convert_element_type.34
  1.4 0.1 pad.23.clone
  1.5 0.7 pad.12
  2.1 0.7 iota_compare_fusion.1
  2.9 1.0 copy.17
  3.9 1.2 copy.23
  5.2 0.2 copy.28
  5.4 0.9 maximum_maximum_fusion.x_ref
  6.3 0.0 copy-done.5
  6.3 0.0 copy-done.6
  6.3 0.1 maximum_bitcast_fusion
  6.4 0.0 copy-start.3
  6.4 0.0 copy-start.4
  6.4 0.3 copy.19
  6.7 0.2 reshape.163
  7.0 0.9 pad.14.w2_ref
  7.9 0.0 copy-done.3
  7.9 0.0 copy-done.4
  7.9 1.3 concatenate.22
  9.2 0.4 reshape.161
  9.6 0.1 pad.13
  9.7 1.5 copy.18
  11.2 91.4 %front.1 = (bf16[704,1024]{1,0:T(8,128)(2,1)}, bf16[16,64,192]{2,1,0:T(8,128)(2,1)}, bf16[16,8,24,880]{3,2,1,0:T(8,128)(2,1)}, bf16[8,24,1024]{2,1,0:T(8,128)(2,1)}) custom-call(bf16[8,24,1024]{2,1,0:T(8,128)(2,1)} %maximum_maximum_fusion.x_ref, bf16[1600,384]{1,0:T(8,128)(2,1)} %bitcast.30, bf16[16,24,880]{2,1,0:T(8,128)(2,1)} %pad.14.w2_ref), custom_call_target="tpu_custom_call" | custom-call | tf_op jit(solution)/shard_map/front/pallas_call | solution.py:295
  102.7 1.3 copy.20
  104.0 0.5 reshape.165
  104.6 0.2 multiply_cosine_fusion
  104.8 0.1 pad_maximum_fusion
  104.9 0.1 reshape.168
  105.0 0.0 copy-start.1
  105.0 0.4 subtract_convert_fusion
  105.4 1.2 copy-done.1
  106.6 3.4 %broadcast_select_fusion.1 = (bf16[64,128,128]{2,1,0:T(8,128)(2,1)S(1)}, bf16[64,128,128]{2,1,0:T(8,128)(2,1)S(1)}) fusion(bf16[64,128,128]{2,1,0:T(8,128)(2,1)S(1)} %copy-done.1, pred[64,128]{1,0:T(8,128)(4,1)S(1)} %get-tuple-element.24, bf16[64,128]{1,0:T(8,128)(2,1)S(1)} %pad_maximum_fusion, bf16[64,128,128]{2,1,0:T(8,128)(2,1)} %param.18, ...), kind=kLoop, calls=%fused_computation.2 | loop fusion | flops 2097152 | bytes 8429568 | tf_op jit(solution)/shard_map/jit(_where)/select_n | solution.py:524
  110.0 0.0 copy-start
  110.0 0.0 copy-start.2
  110.0 1.3 copy-done
  111.3 1.2 fusion.3
  112.5 0.5 fusion.10
  113.0 0.0 copy-done.2
  113.1 2.8 %convolution_convert_fusion = bf16[64,22,128]{2,1,0:T(8,128)(2,1)S(1)} fusion(bf16[64,128,128]{2,1,0:T(8,128)(2,1)S(1)} %get-tuple-element.18, f32[64,22]{1,0:T(8,128)S(1)} %fusion.10, f32[64,22,128]{2,1,0:T(8,128)S(1)} %fusion.3), kind=kOutput, calls=%fused_computation.7 | convolution fusion | flops 46859776 | bytes 3184128 | tf_op jit(solution)/shard_map/bht,btd->bhd/dot_general | solution.py:33
  115.8 1.1 reshape.166
  116.9 0.9 copy.27
  117.8 92.8 %back.1 = bf16[8,24,1024]{2,1,0:T(8,128)(2,1)} custom-call(bf16[16,192,880]{2,1,0:T(8,128)(2,1)} %bitcast.28, bf16[704,1024]{1,0:T(8,128)(2,1)} %get-tuple-element.8.a_ref, bf16[16,64,176]{2,1,0:T(8,128)(2,1)} %bitcast.31, bf16[8,24,1024]{2,1,0:T(8,128)(2,1)} %get-tuple-element.10.x_ref), custom_call_target="tpu_custom_call" | custom-call | tf_op jit(solution)/shard_map/back/pallas_call | solution.py:460
  210.6 1.0 slice_bitcast_fusion
  211.6 0.2 copy.22
  211.9 1.0 copy.24
  (6 shorter events, 0.1 us)
Async XLA Ops:
  0.6 5.7 %copy-start.5 = (bf16[704,352]{1,0:T(8,128)(2,1)S(1)}, bf16[704,352]{1,0:T(8,128)(2,1)}, u32[]{:S(2)}) copy-start(bf16[704,352]{1,0:T(8,128)(2,1)} %param.16) | copy-start | bytes 1486852
  0.6 5.7 %copy-start.6 = (bf16[176,352]{1,0:T(8,128)(2,1)S(1)}, bf16[176,352]{1,0:T(8,128)(2,1)}, u32[]{:S(2)}) copy-start(bf16[176,352]{1,0:T(8,128)(2,1)} %param.15) | copy-start | bytes 371716
  6.4 1.5 copy-start.3
  6.4 1.5 copy-start.4
  105.0 1.6 copy-start.1
  110.0 1.3 copy-start
  110.0 3.1 %copy-start.2 = (bf16[64,128,128]{2,1,0:T(8,128)(2,1)}, bf16[64,128,128]{2,1,0:T(8,128)(2,1)S(1)}, u32[]{:S(2)}) copy-start(bf16[64,128,128]{2,1,0:T(8,128)(2,1)S(1)} %get-tuple-element.18) | copy-start | bytes 6291460

commit v4 on v3

v4 whole, which is shorter than its diff:
```python
import functools

import jax
import jax.numpy as jnp
from jax import lax
from jax.experimental import pallas as pl
from jax.experimental.pallas import tpu as pltpu
from jax.sharding import PartitionSpec as P

MESH = pl.DeviceIdType.MESH
RING = 4
UP, FAR, DOWN = 1, 2, 3
VMEM_LIMIT = 62 * 1024 * 1024


def rope_tables(positions, head_dim):
    half_dim = head_dim // 2
    inv_freq = 10000.0 ** (-jnp.arange(half_dim, dtype=jnp.float32) / half_dim)
    angles = positions.astype(jnp.float32)[..., None] * inv_freq
    cos_t = jnp.cos(angles)
    sin_t = jnp.sin(angles)
    return jnp.concatenate([cos_t, cos_t], axis=-1), jnp.concatenate([-sin_t, sin_t], axis=-1)


class Where:
    def __init__(self, xs, yzs):
        self.xs = xs
        self.yzs = yzs
        self.dp = lax.axis_index("dp")
        self.x = lax.axis_index("x")
        self.j = lax.axis_index("yz")
        self.zz = self.j // RING
        self.yy = self.j % RING
        self.chip = self.x // 2
        self.core = self.x % 2

    def block(self, dz, dy):
        return ((self.zz + dz) % RING) * RING + (self.yy + dy) % RING

    def on_yz(self, j):
        return (self.dp, j, self.x)

    def on_x(self, x):
        return (self.dp, self.j, x)

    def axis_block(self, first, df, dg):
        return self.block(df, dg) if first == "z" else self.block(dg, df)

    def step(self, first, axis, d):
        return self.on_yz(self.axis_block(first, d, 0) if axis == 0 else self.axis_block(first, 0, d))

    def x_of(self, dc):
        return ((self.chip + dc) % RING) * 2 + self.core

    def x_other(self, dc):
        return ((self.chip + dc) % RING) * 2 + (1 - self.core)

    def greet(self):
        barrier = pltpu.get_barrier_semaphore()
        peers = [self.on_x((self.x + d) % self.xs) for d in range(1, self.xs)]
        peers += [self.on_yz((self.j + d) % self.yzs) for d in range(1, self.yzs)]
        for peer in peers:
            pl.semaphore_signal(barrier, inc=1, device_id=peer, device_id_type=MESH)
        pl.semaphore_wait(barrier, len(peers))


class Copies:
    def __init__(self, any_peer):
        self.any_peer = any_peer
        self.started = []

    def send(self, src, dst, ssem, rsem, peer):
        copy = pltpu.make_async_remote_copy(src_ref=src, dst_ref=dst, send_sem=ssem, recv_sem=rsem, device_id=peer, device_id_type=MESH)
        copy.start()
        self.started.append(copy)

    def arrived(self, dst, ssem, rsem):
        pltpu.make_async_remote_copy(
            src_ref=dst, dst_ref=dst, send_sem=ssem, recv_sem=rsem, device_id=self.any_peer, device_id_type=MESH
        ).wait_recv()

    def finish(self):
        for copy in self.started:
            copy.wait_send()


def front_kernel(
    xs, yzs, grp, c_q, c_f, num_heads, len_ref, x_ref, w1_ref, w2_ref, cos_ref, sin_ref, kc_ref, vc_ref,
    act_ref, w2g_ref, xo_ref, ko_ref, vo_ref,
    xg, h, gcol, w1, qkv_s, qkv_in, heads, k_s, v_s, ko_s, vo_s, o_send, ob,
    loc_sem, xsend, xrecv, gsend, grecv, wsend, wrecv, vsend, vrecv, qsend, qrecv, osend, orecv,
):
    f32, bf16 = jnp.float32, jnp.bfloat16
    at = Where(xs, yzs)
    half = xs // 2
    quarter = half // 2
    gp, rows = x_ref.shape[1:]
    dev_rows = rows // yzs
    kx = w1_ref.shape[1]
    read_k = pltpu.make_async_copy(kc_ref, k_s, loc_sem.at[4])
    read_k.start()
    read_v = pltpu.make_async_copy(vc_ref, v_s, loc_sem.at[5])
    read_v.start()
    at.greet()
    copies = Copies(at.on_yz(at.block(0, UP)))

    def send(src, dst, sems, idx, peer):
        copies.send(src, dst, sems[0].at[idx], sems[1].at[idx], peer)

    def arrived(region, sems, idx):
        copies.arrived(region, sems[0].at[idx], sems[1].at[idx])

    xsem, wsem, vsem, qsem = (xsend, xrecv), (wsend, wrecv), (vsend, vrecv), (qsend, qrecv)
    own_x = pltpu.make_async_copy(x_ref.at[at.x], xg.at[at.x, at.j], loc_sem.at[0])
    own_x.start()
    for d in range(1, xs):
        to = (at.x + d) % xs
        send(x_ref.at[to], xg.at[at.x, at.j], xsem, d - 1, at.on_x(to))

    n1 = w1_ref.shape[0]
    n2 = w2_ref.shape[0]

    def w1_at(x, k=None):
        cols = pl.ds(pl.multiple_of(x * kx, 128), kx)
        return w1.at[:, cols] if k is None else w1.at[pl.ds(k * (n1 // 2), n1 // 2), cols]

    def w2_at(x, k=None):
        return w2g_ref.at[:, x] if k is None else w2g_ref.at[pl.ds(k * (n2 // 2), n2 // 2), x]

    def spread_own(src, region, sems, loc):
        own = pltpu.make_async_copy(src, region(at.x), loc_sem.at[loc])
        own.start()
        send(src, region(at.x), sems, 0, at.on_x(at.x_of(UP)))
        send(src, region(at.x), sems, 1, at.on_x(at.x_of(DOWN)))
        send(src, region(at.x), sems, 2, at.on_x(at.x_other(0)))
        return own

    def pass_on(r, sems, slot, x):
        send(r, r, sems, slot, at.on_x(x))

    def forward_near(region, sems):
        arrived(region(at.x_of(DOWN)), sems, 0)
        pass_on(region(at.x_of(DOWN), 0), sems, 3, at.x_of(UP))
        arrived(region(at.x_of(UP)), sems, 1)
        pass_on(region(at.x_of(UP), 1), sems, 4, at.x_of(DOWN))
        pass_on(region(at.x_of(DOWN)), sems, 5, at.x_other(0))
        pass_on(region(at.x_of(UP)), sems, 6, at.x_other(0))

    def forward_far(region, sems):
        arrived(region(at.x_of(FAR), 0), sems, 3)
        pass_on(region(at.x_of(FAR), 0), sems, 7, at.x_other(0))
        arrived(region(at.x_of(FAR), 1), sems, 4)
        pass_on(region(at.x_of(FAR), 1), sems, 8, at.x_other(0))

    def all_in(region, sems, own):
        arrived(region(at.x_other(0)), sems, 2)
        arrived(region(at.x_other(DOWN)), sems, 5)
        arrived(region(at.x_other(UP)), sems, 6)
        arrived(region(at.x_other(FAR), 0), sems, 7)
        arrived(region(at.x_other(FAR), 1), sems, 8)
        own.wait()

    own_w1 = spread_own(w1_ref, w1_at, wsem, 1)
    own_x.wait()
    for d in range(1, xs):
        arrived(xg.at[(at.x + xs - d) % xs, at.j], xsem, d - 1)

    order = ("y", "z")
    halves = range(len(order))
    first_axis, second_axis = halves
    slot_up, slot_down, slot_far = RING, 2 * RING, 3 * RING

    def region(s, df, dg, lo=0, n=half):
        return xg.at[pl.ds(s * half + lo, n), at.axis_block(order[s], df, dg)]

    def pass_rows(s, df, dg, axis, d, slot, lo=0, n=half):
        r = region(s, df, dg, lo, n)
        send(r, r, (gsend.at[s], grecv.at[s]), slot, at.step(order[s], axis, d))

    def rows_in(s, df, dg, slot, lo=0, n=half):
        arrived(region(s, df, dg, lo, n), (gsend.at[s], grecv.at[s]), slot)

    def both_ways(s, df):
        pass_rows(s, df, 0, second_axis, UP, slot_up + df)
        pass_rows(s, df, 0, second_axis, DOWN, slot_down + df)

    for s in halves:
        pass_rows(s, 0, 0, first_axis, UP, 0)
        pass_rows(s, 0, 0, first_axis, DOWN, 1)
        both_ways(s, 0)
    xo_ref[:] = xg[:, at.j]
    for s in halves:
        rows_in(s, DOWN, 0, 0)
        pass_rows(s, DOWN, 0, first_axis, UP, FAR, 0, quarter)
        rows_in(s, UP, 0, 1)
        pass_rows(s, UP, 0, first_axis, DOWN, DOWN, quarter, quarter)
        both_ways(s, DOWN)
        both_ways(s, UP)
    for s in halves:
        rows_in(s, FAR, 0, FAR, 0, quarter)
        rows_in(s, FAR, 0, DOWN, quarter, quarter)
        both_ways(s, FAR)
    for s in halves:
        for df in (0, DOWN):
            rows_in(s, df, DOWN, slot_up + df)
            pass_rows(s, df, DOWN, second_axis, UP, slot_far + df)
    forward_near(w1_at, wsem)
    own_w2 = spread_own(w2_ref, w2_at, vsem, 2)
    for s in halves:
        for df in (UP, FAR):
            rows_in(s, df, UP, slot_down + df)
            pass_rows(s, df, UP, second_axis, DOWN, slot_far + df)
    for s in halves:
        for df in (UP, FAR):
            rows_in(s, df, DOWN, slot_up + df)
        for df in (0, DOWN):
            rows_in(s, df, UP, slot_down + df)
        for df in range(RING):
            rows_in(s, df, FAR, slot_far + df)

    pairs = yzs // 2
    feature = lax.broadcasted_iota(jnp.int32, (2, gp, 1), 1).reshape(2 * gp, 1)
    real = feature < grp
    diagonal = lax.broadcasted_iota(jnp.int32, (gp, 128), 0) == lax.broadcasted_iota(jnp.int32, (gp, 128), 1)

    def load(q):
        return xg[q // pairs, pl.ds((q % pairs) * 2, 2)].astype(f32).reshape(2 * gp, rows)

    def add_up(q, sums):
        raw = load(q)
        for k in range(2):
            row = raw[k * gp + grp:k * gp + grp + 1, :128]
            col = jnp.sum(jnp.where(diagonal, row, 0.0), axis=1, keepdims=True)
            gcol[q, pl.ds(k * gp, gp), :] = jnp.broadcast_to(col, (gp, 128))
        parts = jnp.where(real, raw, 0.0).reshape(2 * gp // 8, 8, rows)
        return sums[0] + jnp.sum(parts, axis=0), sums[1] + jnp.sum(parts * parts, axis=0)

    zero = jnp.zeros((8, rows), f32)
    s1, s2 = lax.fori_loop(0, xs * pairs, add_up, (zero, zero), unroll=4)
    forward_far(w1_at, wsem)
    d_model = grp * xs * yzs
    mean = jnp.sum(s1, axis=0, keepdims=True) / d_model
    var = jnp.sum(s2, axis=0, keepdims=True) / d_model - mean * mean
    scale = lax.rsqrt(var + 1e-6)

    def normalize(q, c):
        gain = jnp.concatenate([gcol[q]] * (rows // 128), axis=1)
        out = jnp.where(real, (load(q) - mean) * scale * gain, 0.0)
        h[pl.ds(pl.multiple_of(q * 2 * gp, 16), 2 * gp), :] = out.astype(bf16)
        return c

    lax.fori_loop(0, xs * pairs, normalize, 0, unroll=2)
    all_in(w1_at, wsem, own_w1)

    nt = 256

    def query(n, c):
        q = jnp.dot(w1[:c_q], h[:, pl.ds(pl.multiple_of(n * nt, nt), nt)], preferred_element_type=f32)
        qkv_s[pl.ds(pl.multiple_of(n * nt, nt), nt), :] = q.T.astype(bf16)
        return c

    lax.fori_loop(0, rows // nt, query, 0)
    def rows_of(ref, j):
        return ref.at[pl.ds(pl.multiple_of(j * dev_rows, dev_rows), dev_rows)]

    own_q = pltpu.make_async_copy(rows_of(qkv_s, at.j), qkv_in.at[at.j], loc_sem.at[3])
    own_q.start()
    for d in range(1, yzs):
        to = (at.j + d) % yzs
        send(rows_of(qkv_s, to), qkv_in.at[at.j], qsem, d - 1, at.on_yz(to))

    def mlp(n, c):
        cols = pl.ds(pl.multiple_of(n * nt, nt), nt)
        gate = jnp.dot(w1[c_q:c_q + c_f], h[:, cols], preferred_element_type=f32).astype(bf16).astype(f32)
        up = jnp.dot(w1[c_q + c_f:], h[:, cols], preferred_element_type=f32).astype(bf16).astype(f32)
        act_ref[pl.ds(0, c_f), cols] = (jax.nn.silu(gate) * up).astype(bf16)
        return c

    lax.fori_loop(0, rows // nt, mlp, 0)
    for d in range(1, yzs):
        arrived(qkv_in.at[(at.j + yzs - d) % yzs], qsem, d - 1)
    own_q.wait()
    forward_near(w2_at, vsem)

    head_dim = k_s.shape[2]
    per = 2 * c_q // head_dim
    for p in range(yzs // 2):
        both = jnp.concatenate([qkv_in[2 * p], qkv_in[2 * p + 1]], axis=1).astype(f32)
        for i in range(per):
            hd = p * per + i
            u = both[:, i * head_dim:(i + 1) * head_dim]
            if hd <= num_heads:
                u = u * cos_ref[:] + pltpu.roll(u, head_dim // 2, 1) * sin_ref[:]
                u = u.astype(bf16).astype(f32)
            heads[hd] = u
    read_k.wait()
    read_v.wait()

    group = 8
    t_len = k_s.shape[1]
    hp = heads.shape[0]
    position = lax.broadcasted_iota(jnp.int32, (t_len, head_dim), 0)
    along = lax.broadcasted_iota(jnp.int32, (hp, t_len), 1)

    def attend(g, c):
        first = pl.multiple_of(g * group, group)
        block = jnp.swapaxes(heads[:, pl.ds(first, group), :], 0, 1)
        scores, values = [], []
        for i in range(group):
            b = first + i
            last = len_ref[b]
            mine = block[i]
            slot = position == last
            kb, vb = [
                jnp.where(slot, mine[row:row + 1], old[b].astype(f32)).astype(bf16)
                for row, old in ((num_heads, k_s), (num_heads + 1, v_s))
            ]
            ko_s[b] = kb
            vo_s[b] = vb
            values.append(vb)
            score = lax.dot_general(mine.astype(bf16), kb, (((1,), (1,)), ((), ())), preferred_element_type=f32) * head_dim ** -0.5
            scores.append(jnp.where(along <= last, score, -1e30))
        scores = jnp.concatenate(scores, axis=0)
        e = jnp.exp(scores - jnp.max(scores, axis=1, keepdims=True))
        probs = (e / jnp.sum(e, axis=1, keepdims=True)).reshape(group, hp, t_len).astype(bf16)
        outs = [jnp.dot(probs[i], values[i], preferred_element_type=f32) for i in range(group)]
        heads[:, pl.ds(first, group), :] = jnp.swapaxes(jnp.stack(outs, axis=0), 0, 1)
        return c

    c_a = ob.shape[1]
    part = dev_rows // 2

    def rows_part(j, k):
        return ob.at[pl.ds(pl.multiple_of(j * dev_rows + k * part, part), part)]

    own_o = []
    for k in range(2):
        lax.fori_loop(k * part // group, (k + 1) * part // group, attend, 0)
        take = pl.ds(k * part, part)
        for jj in range(yzs):
            lo, hi = jj * c_a // head_dim, ((jj + 1) * c_a - 1) // head_dim + 1
            wide = jnp.concatenate([heads[hd, take, :] for hd in range(lo, hi)], axis=1)
            start = jj * c_a - lo * head_dim
            o_send[k, jj] = wide[:, start:start + c_a].astype(bf16)
        own = pltpu.make_async_copy(o_send.at[k, at.j], rows_part(at.j, k), loc_sem.at[6 + k])
        own.start()
        own_o.append(own)
        for d in range(1, yzs):
            to = (at.j + d) % yzs
            send(o_send.at[k, to], rows_part(at.j, k), (osend.at[k], orecv.at[k]), d - 1, at.on_yz(to))
    writes = []
    for out, ref, loc in ((ko_s, ko_ref, 4), (vo_s, vo_ref, 5)):
        write = pltpu.make_async_copy(out, ref, loc_sem.at[loc])
        write.start()
        writes.append(write)
    forward_far(w2_at, vsem)
    for k in range(2):
        for d in range(1, yzs):
            arrived(rows_part((at.j + yzs - d) % yzs, k), (osend.at[k], orecv.at[k]), d - 1)
        own_o[k].wait()
    act_ref[pl.ds(c_f, c_a), :] = ob[:].T
    all_in(w2_at, vsem, own_w2)
    for write in writes:
        write.wait()
    copies.finish()


def front(x_pad, w1_loc, w2_loc, tables, k_cache, v_cache, ctx_len, xs, yzs, grp, c_q, c_f):
    _, gp, rows = x_pad.shape
    n1, kx = w1_loc.shape
    n2 = w2_loc.shape[2]
    dev_rows, t_len, head_dim = k_cache.shape
    hp = yzs * c_q // head_dim
    num_heads = hp - 2
    c_a = n2 - c_f
    dma = pltpu.SemaphoreType.DMA
    f32, bf16 = jnp.float32, jnp.bfloat16
    vspec, aspec = pl.BlockSpec(memory_space=pltpu.VMEM), pl.BlockSpec(memory_space=pl.ANY)
    sems = lambda *s: [dma(s), dma(s)]
    cache = jax.ShapeDtypeStruct(k_cache.shape, bf16)
    return pl.pallas_call(
        functools.partial(front_kernel, xs, yzs, grp, c_q, c_f, num_heads),
        out_shape=(
            jax.ShapeDtypeStruct((n2, rows), bf16),
            jax.ShapeDtypeStruct((yzs, xs) + w2_loc.shape[1:], bf16),
            jax.ShapeDtypeStruct((xs, gp, rows), bf16),
            cache,
            cache,
        ),
        in_specs=[pl.BlockSpec(memory_space=pltpu.SMEM)] + [vspec] * 5 + [aspec] * 2,
        out_specs=(vspec, aspec, vspec, aspec, aspec),
        scratch_shapes=[
            pltpu.VMEM((xs, yzs, gp, rows), bf16),
            pltpu.VMEM((xs * yzs * gp, rows), bf16),
            pltpu.VMEM((xs * yzs // 2, 2 * gp, 128), f32),
            pltpu.VMEM((n1, xs * kx), bf16),
            pltpu.VMEM((rows, c_q), bf16),
            pltpu.VMEM((yzs, dev_rows, c_q), bf16),
            pltpu.VMEM((hp, dev_rows, head_dim), f32),
        ] + [pltpu.VMEM(k_cache.shape, bf16)] * 4 + [
            pltpu.VMEM((2, yzs, dev_rows // 2, c_a), bf16),
            pltpu.VMEM((rows, c_a), bf16),
            dma((8,)),
        ] + sems(xs - 1) + sems(2, RING * RING) + sems(9) + sems(9) + sems(yzs - 1) + sems(2, yzs - 1),
        compiler_params=pltpu.CompilerParams(collective_id=0, has_side_effects=True, vmem_limit_bytes=VMEM_LIMIT),
        name="front",
    )(ctx_len, x_pad, w1_loc, w2_loc, *tables, k_cache, v_cache)


def back_kernel(xs, yzs, w_ref, act, x_ref, y_ref, zb, r1, r2, r3, r4, yv, loc_sem, s1, q1, s2, q2, s3, q3, s4, q4, ys, yq):
    at = Where(xs, yzs)
    order = ("z", "y")
    hr = zb.shape[2] // 2
    gp = x_ref.shape[1]
    at.greet()
    copies = Copies(at.on_yz(at.block(0, UP)))
    send, arrived = copies.send, copies.arrived

    def zat(h, df, dg):
        dz, dy = (df, dg) if order[h] == "z" else (dg, df)
        return zb.at[dz, dy, pl.ds(h * hr, hr)]

    def compute(dz, dy):
        zb[dz, dy] = jnp.dot(w_ref[at.block(dz, dy)], act[:], preferred_element_type=jnp.float32)

    def send1(h, dg):
        d = 1 if dg < 2 else 3
        send(zat(h, 2, dg), r1.at[h, dg], s1.at[h, dg], q1.at[h, dg], at.step(order[h], 0, d))

    compute(2, 2)
    send1(0, 2)
    send1(1, 2)
    for k in (0, 1, 3):
        compute(2, k)
        send1(0, k)
        compute(k, 2)
        send1(1, k)

    def second(i, c):
        k, m = i // 3, i % 3
        compute(k + k // 2, m + m // 2)
        return c

    lax.fori_loop(0, 9, second, 0)

    def send2(h, up, dg):
        df, d, s = (1, 1, 0) if up else (3, 3, 1)
        send(zat(h, df, dg), r2.at[h, s, dg], s2.at[h, s, dg], q2.at[h, s, dg], at.step(order[h], 0, d))

    for h in range(2):
        for dg in (2, 3):
            send2(h, True, dg)
        for dg in (0, 1):
            send2(h, False, dg)
    for k in range(2):
        for h in range(2):
            for up in (True, False):
                dg = k if up else 2 + k
                arrived(r1.at[h, dg], s1.at[h, dg], q1.at[h, dg])
                ref = zat(h, 1 if up else 3, dg)
                ref[:] = ref[:] + r1[h, dg]
                send2(h, up, dg)

    def plane(h, dg):
        for s in range(2):
            arrived(r2.at[h, s, dg], s2.at[h, s, dg], q2.at[h, s, dg])
        ref = zat(h, 0, dg)
        ref[:] = ref[:] + r2[h, 0, dg] + r2[h, 1, dg]

    hh = hr // 2

    def part(h, dg, k):
        dz, dy = (0, dg) if order[h] == "z" else (dg, 0)
        return zb.at[dz, dy, pl.ds(h * hr + k * hh, hh)]

    def send4(h, up, k):
        dg, d, s = (1, 1, 0) if up else (3, 3, 1)
        send(part(h, dg, k), r4.at[h, s, k], s4.at[h, s, k], q4.at[h, s, k], at.step(order[h], 1, d))

    for h in range(2):
        plane(h, 2)
        send(part(h, 2, 0), r3.at[h, 0], s3.at[h, 0], q3.at[h, 0], at.step(order[h], 1, 1))
        send(part(h, 2, 1), r3.at[h, 1], s3.at[h, 1], q3.at[h, 1], at.step(order[h], 1, 3))
    for h in range(2):
        plane(h, 1)
        send4(h, True, 1)
        plane(h, 3)
        send4(h, False, 0)
    for h in range(2):
        plane(h, 0)
    for h in range(2):
        arrived(r3.at[h, 0], s3.at[h, 0], q3.at[h, 0])
        ref = part(h, 1, 0)
        ref[:] = ref[:] + r3[h, 0]
        send4(h, True, 0)
        arrived(r3.at[h, 1], s3.at[h, 1], q3.at[h, 1])
        ref = part(h, 3, 1)
        ref[:] = ref[:] + r3[h, 1]
        send4(h, False, 1)
    def y_copy(x, d):
        return pltpu.make_async_remote_copy(
            src_ref=yv.at[x], dst_ref=y_ref.at[at.x], send_sem=ys.at[d - 1], recv_sem=yq.at[d - 1], device_id=at.on_x(x), device_id_type=MESH
        )

    for h in range(2):
        for k in range(2):
            for s in range(2):
                arrived(r4.at[h, s, k], s4.at[h, s, k], q4.at[h, s, k])
            z = zb[0, 0, pl.ds(h * hr + k * hh, hh)] + r4[h, 0, k] + r4[h, 1, k]
            n = hh // gp
            for i in range(n):
                x = h * 2 * n + k * n + i
                yv[x] = (x_ref[x].astype(jnp.float32) + z[i * gp:(i + 1) * gp]).astype(jnp.bfloat16)
                d = lax.rem(x - at.x + xs, xs)

                @pl.when(d == 0)
                def _():
                    pltpu.make_async_copy(yv.at[x], y_ref.at[x], loc_sem.at[0]).start()

                @pl.when(d != 0)
                def _():
                    y_copy(x, d).start()

    for d in range(1, xs):
        arrived(y_ref.at[(at.x + xs - d) % xs], ys.at[d - 1], yq.at[d - 1])
    pltpu.make_async_copy(yv.at[at.x], y_ref.at[at.x], loc_sem.at[0]).wait()
    for d in range(1, xs):
        y_copy((at.x + d) % xs, d).wait_send()
    copies.finish()


def back(w2, act, x_own):
    _, block, _ = w2.shape
    yzs = w2.shape[0]
    xs, gp, rows = x_own.shape
    dma = pltpu.SemaphoreType.DMA
    bf16 = jnp.bfloat16
    vmem = lambda *s: pltpu.VMEM(s, jnp.float32)
    vspec, aspec = pl.BlockSpec(memory_space=pltpu.VMEM), pl.BlockSpec(memory_space=pl.ANY)
    sems = lambda *s: [dma(s), dma(s)]
    hr = block // 2
    return pl.pallas_call(
        functools.partial(back_kernel, xs, yzs),
        out_shape=jax.ShapeDtypeStruct((xs, gp, rows), bf16),
        in_specs=[vspec] * 3,
        out_specs=aspec,
        scratch_shapes=[
            vmem(RING, RING, block, rows),
            vmem(2, RING, hr, rows),
            vmem(2, 2, RING, hr, rows),
            vmem(2, 2, hr // 2, rows),
            vmem(2, 2, 2, hr // 2, rows),
            pltpu.VMEM((xs, gp, rows), bf16),
            dma((1,)),
        ] + sems(2, RING) + sems(2, 2, RING) + sems(2, 2) + sems(2, 2, 2) + sems(xs - 1),
        compiler_params=pltpu.CompilerParams(collective_id=1, has_side_effects=True, vmem_limit_bytes=VMEM_LIMIT),
        name="back",
    )(w2, act, x_own)


def solution(mesh):
    xs = mesh.shape["x"]
    yzs = mesh.shape["yz"]
    both_axes = ("x", "yz")
    row_spec = P("dp", both_axes)
    in_w_spec = P("x", "yz")
    out_w_spec = P("yz", "x")
    cache_spec = P(("dp", "x", "yz"), None, None)
    len_spec = P(("dp", "x", "yz"))

    def local_layer(x_loc, gain_loc, wqkv_loc, wgate_loc, wup_loc, wao_loc, wmo_loc, kc_loc, vc_loc, len_loc):
        n_rows, grp = x_loc.shape
        pad = -grp % 8
        gp = grp + pad
        rows = n_rows // xs
        bf16 = jnp.bfloat16

        def pad_groups(w):
            n = w.shape[1]
            return jnp.pad(w.reshape(yzs, grp, n), ((0, 0), (0, pad), (0, 0)))

        w1_loc = jnp.concatenate([wqkv_loc, wgate_loc, wup_loc], axis=1)
        w1_loc = pad_groups(w1_loc).reshape(yzs * gp, -1).T
        w2_loc = pad_groups(jnp.concatenate([wmo_loc, wao_loc], axis=0).T)

        x_t = x_loc.T.reshape(grp, xs, rows).transpose(1, 0, 2)
        gain_row = jnp.broadcast_to(jnp.pad(gain_loc, (0, rows - grp)).reshape(1, 1, rows), (xs, 1, rows))
        x_pad = jnp.concatenate([x_t, gain_row, jnp.zeros((xs, pad - 1, rows), bf16)], axis=1)
        c_q = wqkv_loc.shape[1]
        c_f = wgate_loc.shape[1]
        tables = rope_tables(len_loc, kc_loc.shape[2])
        act, w2, x_own, k_all, v_all = front(x_pad, w1_loc, w2_loc, tables, kc_loc, vc_loc, len_loc, xs, yzs, grp, c_q, c_f)
        y_back = back(w2.reshape(yzs, xs * gp, -1), act, x_own)
        y_loc = y_back[:, :grp].transpose(1, 0, 2).reshape(grp, n_rows).T
        return y_loc, k_all, v_all

    in_specs = (row_spec, P(both_axes), in_w_spec, in_w_spec, in_w_spec, out_w_spec, out_w_spec, cache_spec, cache_spec, len_spec)
    out_specs = (row_spec, cache_spec, cache_spec)
    return jax.shard_map(local_layer, mesh=mesh, in_specs=in_specs, out_specs=out_specs, check_vma=False)
```

time: 213 us -> 187 us (0.88)
  Pallas kernels: 184 us -> 169 us
  other arithmetic: 6.98 us -> 2.56 us
  matrix products: 4.02 us -> 0 us
  local copies, waits for them, and re-layouts: 16.8 us -> 14.1 us
    pallas_call x1, Pallas kernels: 92.8 us -> 79.9 us  [back(): pl.pallas_call(functools.partial(back_kernel, xs, yzs), out_shape=jax.Sha...]
    dot_general x2 -> x0, matrix products: 4.02 us -> none  [the longest x1 2.77 us: attend_local(): jnp.einsum('bht,btd->bhd', attn_probs, v_all, preferred_element_type=jnp....]
    select_n x1 -> x0, other arithmetic: 3.36 us -> none  [local_layer(): k_all = jnp.where(new_slot, k_rot[:, None, :], kc_loc)]
    reshape x3 -> x0, local copies, waits for them, and re-layouts: 2.55 us -> none  [the longest x2 2.01 us: local_layer(): attend_local(q_rot, k_all, v_all, len_loc)]
    pallas_call x1, Pallas kernels: 91.4 us -> 89 us  [front(): pl.pallas_call(functools.partial(front_kernel, xs, yzs, grp, c_q, c_f, nu...]
where the time goes in v4:
time: 187 us; the launch traced here: 186 us
  Pallas kernels  169 us (90%)
  local copies, waits for them, and re-layouts  14.1 us (8%)
  other arithmetic  2.56 us (1%)
    pallas_call x1, Pallas kernels, front(): pl.pallas_call(functools.partial(front_kernel, xs, yzs, grp, c_q, c_f, nu...  89 us
    pallas_call x1, Pallas kernels, back(): pl.pallas_call(functools.partial(back_kernel, xs, yzs), out_shape=jax.Sha...  79.9 us
    unnamed x18, local copies, waits for them, and re-layouts  6.94 us

profile of v4, /device:TPU:1, one launch (start us, length us, event | category | flops | bytes accessed | tf_op | source)
XLA Modules:
  0.0 186.4 jit_solution(16539678265032437262)
XLA Ops:
  0.6 0.7 convert_element_type.9
  1.3 0.1 pad.23.clone
  1.4 0.7 pad.12
  2.1 0.2 fusion
  2.3 0.0 copy-start.4
  2.3 0.0 copy-start.5
  2.3 0.7 pad_maximum_fusion
  3.0 1.0 copy.17
  4.1 1.2 copy.21
  5.3 0.2 copy.24
  5.5 0.9 maximum_maximum_fusion.x_ref
  6.4 0.0 copy-done.4
  6.4 0.0 copy-done.5
  6.4 0.1 maximum_bitcast_fusion
  6.5 0.0 copy-start.2
  6.5 0.0 copy-start.3
  6.5 0.3 copy.19
  6.9 0.2 reshape.38
  7.1 0.9 pad.14.w2_ref
  8.0 0.0 copy-done.2
  8.0 0.0 copy-done.3
  8.0 1.3 concatenate.16
  9.3 0.4 reshape.36
  9.7 0.1 pad.13
  9.8 1.5 copy.18
  11.4 89.0 %front.1 = (bf16[880,1024]{1,0:T(8,128)(2,1)}, bf16[16,8,24,880]{3,2,1,0:T(8,128)(2,1)}, bf16[8,24,1024]{2,1,0:T(8,128)(2,1)}, bf16[64,128,128]{2,1,0:T(8,128)(2,1)}, bf16[64,128,128]{2,1,0:T(8,128)(2,1)}) custom-call(s32[64]{0:T(128)} %len_ref.1, bf16[8,24,1024]{2,1,0:T(8,128)(2,1)} %maximum_maximum_fusion.x_ref, bf16[1600,384]{1,0:T(8,128)(2,1)} %bitcast.22, ...), custom_call_target="tpu_custom_call" | custom-call | tf_op jit(solution)/shard_map/front/pallas_call | solution.py:381
  100.3 79.9 %back.1 = bf16[8,24,1024]{2,1,0:T(8,128)(2,1)} custom-call(bf16[16,192,880]{2,1,0:T(8,128)(2,1)} %bitcast.20, bf16[880,1024]{1,0:T(8,128)(2,1)} %get-tuple-element.9.act, bf16[8,24,1024]{2,1,0:T(8,128)(2,1)} %get-tuple-element.10.x_ref), custom_call_target="tpu_custom_call" | custom-call | tf_op jit(solution)/shard_map/back/pallas_call | solution.py:542
  180.3 0.0 copy-start.1
  180.3 1.2 slice_bitcast_fusion
  181.5 0.2 copy.20
  181.7 1.0 copy.22
  182.7 0.0 copy-done.1
  182.7 0.0 copy-start
  182.7 1.3 copy.27
  184.0 1.0 copy-done
  185.0 1.3 copy.28
  (4 shorter events, 0.1 us)
Async XLA Ops:
  2.3 4.1 %copy-start.4 = (bf16[704,352]{1,0:T(8,128)(2,1)S(1)}, bf16[704,352]{1,0:T(8,128)(2,1)}, u32[]{:S(2)}) copy-start(bf16[704,352]{1,0:T(8,128)(2,1)} %param.16) | copy-start | bytes 1486852
  2.3 4.1 %copy-start.5 = (bf16[176,352]{1,0:T(8,128)(2,1)S(1)}, bf16[176,352]{1,0:T(8,128)(2,1)}, u32[]{:S(2)}) copy-start(bf16[176,352]{1,0:T(8,128)(2,1)} %param.15) | copy-start | bytes 371716
  6.5 1.5 copy-start.2
  6.5 1.5 copy-start.3
  180.3 2.4 %copy-start.1 = (bf16[64,128,128]{2,1,0:T(8,128)(2,1)S(1)}, bf16[64,128,128]{2,1,0:T(8,128)(2,1)}, u32[]{:S(2)}) copy-start(bf16[64,128,128]{2,1,0:T(8,128)(2,1)} %get-tuple-element.22) | copy-start | bytes 6291460
  182.7 2.3 %copy-start = (bf16[64,128,128]{2,1,0:T(8,128)(2,1)S(1)}, bf16[64,128,128]{2,1,0:T(8,128)(2,1)}, u32[]{:S(2)}) copy-start(bf16[64,128,128]{2,1,0:T(8,128)(2,1)} %get-tuple-element.23) | copy-start | bytes 6291460

commit v5 on v4

--- a/solution.py
+++ b/solution.py
@@ -84,14 +84,147 @@
             copy.wait_send()
 
 
-def front_kernel(
+def layer_kernel(
     xs, yzs, grp, c_q, c_f, num_heads, len_ref, x_ref, w1_ref, w2_ref, cos_ref, sin_ref, kc_ref, vc_ref,
-    act_ref, w2g_ref, xo_ref, ko_ref, vo_ref,
-    xg, h, gcol, w1, qkv_s, qkv_in, heads, k_s, v_s, ko_s, vo_s, o_send, ob,
+    y_ref, ko_ref, vo_ref,
+    act, w2v, xo, k_s, v_s, o_send, ob,
     loc_sem, xsend, xrecv, gsend, grecv, wsend, wrecv, vsend, vrecv, qsend, qrecv, osend, orecv,
+    s1, q1, s2, q2, s3, q3, s4, q4, ys, yq, ready,
 ):
     f32, bf16 = jnp.float32, jnp.bfloat16
+    dma, vmem = pltpu.SemaphoreType.DMA, pltpu.VMEM
+    gp, rows = x_ref.shape[1:]
+    dev_rows, t_len, head_dim = k_s.shape
+    n1, kx = w1_ref.shape
+    c_a = ob.shape[1]
+    part = dev_rows // 2
+    block = xs * grp
+    hr = block // 2
     at = Where(xs, yzs)
+    any_peer = at.on_yz(at.block(0, UP))
+
+    def w2_at(x, k=None):
+        n2 = w2v.shape[0]
+        return w2v.at[:, x] if k is None else w2v.at[pl.ds(k * (n2 // 2), n2 // 2), x]
+
+    def o_rows(j, k):
+        return ob.at[pl.ds(pl.multiple_of(j * dev_rows + k * part, part), part)]
+
+    def o_copy(k, d):
+        to = (at.j + d) % yzs
+        return remote(o_send.at[k, to], o_rows(at.j, k), osend.at[k, d - 1], orecv.at[k, d - 1], at.on_yz(to))
+
+    def o_own(k):
+        return pltpu.make_async_copy(o_send.at[k, at.j], o_rows(at.j, k), loc_sem.at[6 + k])
+
+    def cache_writes():
+        return [pltpu.make_async_copy(src, dst, loc_sem.at[loc]) for src, dst, loc in ((k_s, ko_ref, 4), (v_s, vo_ref, 5))]
+
+    gather_and_attend = functools.partial(
+        first_phase, xs, yzs, grp, c_q, c_f, num_heads, at, any_peer, w2_at, o_copy, o_own, cache_writes,
+        len_ref, x_ref, w1_ref, w2_ref, cos_ref, sin_ref, kc_ref, vc_ref, act, xo, k_s, v_s, o_send,
+        loc_sem, (xsend, xrecv), (gsend, grecv), (wsend, wrecv), (vsend, vrecv), (qsend, qrecv),
+    )
+    pl.run_scoped(
+        gather_and_attend,
+        vmem((xs, yzs, gp, rows), bf16),
+        vmem((xs * yzs * gp, rows), bf16),
+        vmem((xs * yzs // 2, 2 * gp, 128), f32),
+        vmem((n1, xs * kx), bf16),
+        vmem((rows, c_q), bf16),
+        vmem((yzs, dev_rows, c_q), bf16),
+        vmem((num_heads + 2, dev_rows, head_dim), f32),
+    )
+
+    def finish_first():
+        late = Copies(any_peer)
+        forward_far(late, at, w2_at, (vsend, vrecv))
+        for k in range(2):
+            for d in range(1, yzs):
+                late.arrived(o_rows((at.j + yzs - d) % yzs, k), osend.at[k, d - 1], orecv.at[k, d - 1])
+            o_own(k).wait()
+        act[pl.ds(c_f, c_a), :] = ob[:].T
+        all_in(late, at, w2_at, (vsend, vrecv), pltpu.make_async_copy(w2_ref, w2_at(at.x), loc_sem.at[2]))
+        return late
+
+    def finish_last(late):
+        for write in cache_writes():
+            write.wait()
+        for k in range(2):
+            for d in range(1, yzs):
+                o_copy(k, d).wait_send()
+        for slot, k in enumerate((None, None, None, 0, 0, None, None)):
+            remote(w2_at(at.x, k), w2_at(at.x, k), vsend.at[slot], vrecv.at[slot], any_peer).wait_send()
+        late.finish()
+
+    sum_and_return = functools.partial(
+        second_phase, xs, yzs, grp, at, any_peer, finish_first, finish_last, w2v, act, xo, y_ref,
+        loc_sem, (s1, q1), (s2, q2), (s3, q3), (s4, q4), (ys, yq), ready,
+    )
+    big = hr // 2 + hr // 2 % 8
+    pl.run_scoped(
+        sum_and_return,
+        vmem((RING, RING, block, rows), f32),
+        vmem((2, RING, hr, rows), f32),
+        vmem((2, 2, RING, hr, rows), f32),
+        vmem((2, 2, big, rows), f32),
+        vmem((2, 2, 2, big, rows), f32),
+        vmem((xs, gp, rows), bf16),
+        vmem((block, w2v.shape[3]), f32),
+    )
+
+
+def remote(src, dst, ssem, rsem, peer):
+    return pltpu.make_async_remote_copy(src_ref=src, dst_ref=dst, send_sem=ssem, recv_sem=rsem, device_id=peer, device_id_type=MESH)
+
+
+def spread_own(copies, at, src, region, sems, loc_sem):
+    own = pltpu.make_async_copy(src, region(at.x), loc_sem)
+    own.start()
+    for slot, to in enumerate((at.x_of(UP), at.x_of(DOWN), at.x_other(0))):
+        copies.send(src, region(at.x), sems[0].at[slot], sems[1].at[slot], at.on_x(to))
+    return own
+
+
+def pass_on(copies, at, r, sems, slot, x):
+    copies.send(r, r, sems[0].at[slot], sems[1].at[slot], at.on_x(x))
+
+
+def block_in(copies, r, sems, slot):
+    copies.arrived(r, sems[0].at[slot], sems[1].at[slot])
+
+
+def forward_near(copies, at, region, sems):
+    block_in(copies, region(at.x_of(DOWN)), sems, 0)
+    pass_on(copies, at, region(at.x_of(DOWN), 0), sems, 3, at.x_of(UP))
+    block_in(copies, region(at.x_of(UP)), sems, 1)
+    pass_on(copies, at, region(at.x_of(UP), 1), sems, 4, at.x_of(DOWN))
+    pass_on(copies, at, region(at.x_of(DOWN)), sems, 5, at.x_other(0))
+    pass_on(copies, at, region(at.x_of(UP)), sems, 6, at.x_other(0))
+
+
+def forward_far(copies, at, region, sems):
+    for k in range(2):
+        r = region(at.x_of(FAR), k)
+        block_in(copies, r, sems, 3 + k)
+        pass_on(copies, at, r, sems, 7 + k, at.x_other(0))
+
+
+def all_in(copies, at, region, sems, own):
+    block_in(copies, region(at.x_other(0)), sems, 2)
+    block_in(copies, region(at.x_other(DOWN)), sems, 5)
+    block_in(copies, region(at.x_other(UP)), sems, 6)
+    for k in range(2):
+        block_in(copies, region(at.x_other(FAR), k), sems, 7 + k)
+    own.wait()
+
+
+def first_phase(
+    xs, yzs, grp, c_q, c_f, num_heads, at, any_peer, w2_at, o_copy, o_own, cache_writes,
+    len_ref, x_ref, w1_ref, w2_ref, cos_ref, sin_ref, kc_ref, vc_ref, act, xo, k_s, v_s, o_send,
+    loc_sem, xsem, gsem, wsem, vsem, qsem, xg, h, gcol, w1, qkv_s, qkv_in, heads,
+):
+    f32, bf16 = jnp.float32, jnp.bfloat16
     half = xs // 2
     quarter = half // 2
     gp, rows = x_ref.shape[1:]
@@ -102,7 +235,7 @@
     read_v = pltpu.make_async_copy(vc_ref, v_s, loc_sem.at[5])
     read_v.start()
     at.greet()
-    copies = Copies(at.on_yz(at.block(0, UP)))
+    copies, late = Copies(any_peer), Copies(any_peer)
 
     def send(src, dst, sems, idx, peer):
         copies.send(src, dst, sems[0].at[idx], sems[1].at[idx], peer)
@@ -110,7 +243,6 @@
     def arrived(region, sems, idx):
         copies.arrived(region, sems[0].at[idx], sems[1].at[idx])
 
-    xsem, wsem, vsem, qsem = (xsend, xrecv), (wsend, wrecv), (vsend, vrecv), (qsend, qrecv)
     own_x = pltpu.make_async_copy(x_ref.at[at.x], xg.at[at.x, at.j], loc_sem.at[0])
     own_x.start()
     for d in range(1, xs):
@@ -118,49 +250,12 @@
         send(x_ref.at[to], xg.at[at.x, at.j], xsem, d - 1, at.on_x(to))
 
     n1 = w1_ref.shape[0]
-    n2 = w2_ref.shape[0]
 
     def w1_at(x, k=None):
         cols = pl.ds(pl.multiple_of(x * kx, 128), kx)
         return w1.at[:, cols] if k is None else w1.at[pl.ds(k * (n1 // 2), n1 // 2), cols]
 
-    def w2_at(x, k=None):
-        return w2g_ref.at[:, x] if k is None else w2g_ref.at[pl.ds(k * (n2 // 2), n2 // 2), x]
-
-    def spread_own(src, region, sems, loc):
-        own = pltpu.make_async_copy(src, region(at.x), loc_sem.at[loc])
-        own.start()
-        send(src, region(at.x), sems, 0, at.on_x(at.x_of(UP)))
-        send(src, region(at.x), sems, 1, at.on_x(at.x_of(DOWN)))
-        send(src, region(at.x), sems, 2, at.on_x(at.x_other(0)))
-        return own
-
-    def pass_on(r, sems, slot, x):
-        send(r, r, sems, slot, at.on_x(x))
-
-    def forward_near(region, sems):
-        arrived(region(at.x_of(DOWN)), sems, 0)
-        pass_on(region(at.x_of(DOWN), 0), sems, 3, at.x_of(UP))
-        arrived(region(at.x_of(UP)), sems, 1)
-        pass_on(region(at.x_of(UP), 1), sems, 4, at.x_of(DOWN))
-        pass_on(region(at.x_of(DOWN)), sems, 5, at.x_other(0))
-        pass_on(region(at.x_of(UP)), sems, 6, at.x_other(0))
-
-    def forward_far(region, sems):
-        arrived(region(at.x_of(FAR), 0), sems, 3)
-        pass_on(region(at.x_of(FAR), 0), sems, 7, at.x_other(0))
-        arrived(region(at.x_of(FAR), 1), sems, 4)
-        pass_on(region(at.x_of(FAR), 1), sems, 8, at.x_other(0))
-
-    def all_in(region, sems, own):
-        arrived(region(at.x_other(0)), sems, 2)
-        arrived(region(at.x_other(DOWN)), sems, 5)
-        arrived(region(at.x_other(UP)), sems, 6)
-        arrived(region(at.x_other(FAR), 0), sems, 7)
-        arrived(region(at.x_other(FAR), 1), sems, 8)
-        own.wait()
-
-    own_w1 = spread_own(w1_ref, w1_at, wsem, 1)
+    own_w1 = spread_own(copies, at, w1_ref, w1_at, wsem, loc_sem.at[1])
     own_x.wait()
     for d in range(1, xs):
         arrived(xg.at[(at.x + xs - d) % xs, at.j], xsem, d - 1)
@@ -175,10 +270,10 @@
 
     def pass_rows(s, df, dg, axis, d, slot, lo=0, n=half):
         r = region(s, df, dg, lo, n)
-        send(r, r, (gsend.at[s], grecv.at[s]), slot, at.step(order[s], axis, d))
+        send(r, r, (gsem[0].at[s], gsem[1].at[s]), slot, at.step(order[s], axis, d))
 
     def rows_in(s, df, dg, slot, lo=0, n=half):
-        arrived(region(s, df, dg, lo, n), (gsend.at[s], grecv.at[s]), slot)
+        arrived(region(s, df, dg, lo, n), (gsem[0].at[s], gsem[1].at[s]), slot)
 
     def both_ways(s, df):
         pass_rows(s, df, 0, second_axis, UP, slot_up + df)
@@ -188,7 +283,7 @@
         pass_rows(s, 0, 0, first_axis, UP, 0)
         pass_rows(s, 0, 0, first_axis, DOWN, 1)
         both_ways(s, 0)
-    xo_ref[:] = xg[:, at.j]
+    xo[:] = xg[:, at.j]
     for s in halves:
         rows_in(s, DOWN, 0, 0)
         pass_rows(s, DOWN, 0, first_axis, UP, FAR, 0, quarter)
@@ -204,8 +299,8 @@
         for df in (0, DOWN):
             rows_in(s, df, DOWN, slot_up + df)
             pass_rows(s, df, DOWN, second_axis, UP, slot_far + df)
-    forward_near(w1_at, wsem)
-    own_w2 = spread_own(w2_ref, w2_at, vsem, 2)
+    forward_near(copies, at, w1_at, wsem)
+    spread_own(late, at, w2_ref, w2_at, vsem, loc_sem.at[2])
     for s in halves:
         for df in (UP, FAR):
             rows_in(s, df, UP, slot_down + df)
@@ -237,7 +332,7 @@
 
     zero = jnp.zeros((8, rows), f32)
     s1, s2 = lax.fori_loop(0, xs * pairs, add_up, (zero, zero), unroll=4)
-    forward_far(w1_at, wsem)
+    forward_far(copies, at, w1_at, wsem)
     d_model = grp * xs * yzs
     mean = jnp.sum(s1, axis=0, keepdims=True) / d_model
     var = jnp.sum(s2, axis=0, keepdims=True) / d_model - mean * mean
@@ -250,7 +345,7 @@
         return c
 
     lax.fori_loop(0, xs * pairs, normalize, 0, unroll=2)
-    all_in(w1_at, wsem, own_w1)
+    all_in(copies, at, w1_at, wsem, own_w1)
 
     nt = 256
 
@@ -273,14 +368,14 @@
         cols = pl.ds(pl.multiple_of(n * nt, nt), nt)
         gate = jnp.dot(w1[c_q:c_q + c_f], h[:, cols], preferred_element_type=f32).astype(bf16).astype(f32)
         up = jnp.dot(w1[c_q + c_f:], h[:, cols], preferred_element_type=f32).astype(bf16).astype(f32)
-        act_ref[pl.ds(0, c_f), cols] = (jax.nn.silu(gate) * up).astype(bf16)
+        act[pl.ds(0, c_f), cols] = (jax.nn.silu(gate) * up).astype(bf16)
         return c
 
     lax.fori_loop(0, rows // nt, mlp, 0)
     for d in range(1, yzs):
         arrived(qkv_in.at[(at.j + yzs - d) % yzs], qsem, d - 1)
     own_q.wait()
-    forward_near(w2_at, vsem)
+    forward_near(late, at, w2_at, vsem)
 
     head_dim = k_s.shape[2]
     per = 2 * c_q // head_dim
@@ -305,7 +400,7 @@
     def attend(g, c):
         first = pl.multiple_of(g * group, group)
         block = jnp.swapaxes(heads[:, pl.ds(first, group), :], 0, 1)
-        scores, values = [], []
+        scores, keys, values = [], [], []
         for i in range(group):
             b = first + i
             last = len_ref[b]
@@ -315,11 +410,13 @@
                 jnp.where(slot, mine[row:row + 1], old[b].astype(f32)).astype(bf16)
                 for row, old in ((num_heads, k_s), (num_heads + 1, v_s))
             ]
-            ko_s[b] = kb
-            vo_s[b] = vb
+            keys.append(kb)
             values.append(vb)
             score = lax.dot_general(mine.astype(bf16), kb, (((1,), (1,)), ((), ())), preferred_element_type=f32) * head_dim ** -0.5
             scores.append(jnp.where(along <= last, score, -1e30))
+        for i in range(group):
+            k_s[first + i] = keys[i]
+            v_s[first + i] = values[i]
         scores = jnp.concatenate(scores, axis=0)
         e = jnp.exp(scores - jnp.max(scores, axis=1, keepdims=True))
         probs = (e / jnp.sum(e, axis=1, keepdims=True)).reshape(group, hp, t_len).astype(bf16)
@@ -327,13 +424,8 @@
         heads[:, pl.ds(first, group), :] = jnp.swapaxes(jnp.stack(outs, axis=0), 0, 1)
         return c
 
-    c_a = ob.shape[1]
+    c_a = o_send.shape[3]
     part = dev_rows // 2
-
-    def rows_part(j, k):
-        return ob.at[pl.ds(pl.multiple_of(j * dev_rows + k * part, part), part)]
-
-    own_o = []
     for k in range(2):
         lax.fori_loop(k * part // group, (k + 1) * part // group, attend, 0)
         take = pl.ds(k * part, part)
@@ -342,78 +434,27 @@
             wide = jnp.concatenate([heads[hd, take, :] for hd in range(lo, hi)], axis=1)
             start = jj * c_a - lo * head_dim
             o_send[k, jj] = wide[:, start:start + c_a].astype(bf16)
-        own = pltpu.make_async_copy(o_send.at[k, at.j], rows_part(at.j, k), loc_sem.at[6 + k])
-        own.start()
-        own_o.append(own)
+        o_own(k).start()
         for d in range(1, yzs):
-            to = (at.j + d) % yzs
-            send(o_send.at[k, to], rows_part(at.j, k), (osend.at[k], orecv.at[k]), d - 1, at.on_yz(to))
-    writes = []
-    for out, ref, loc in ((ko_s, ko_ref, 4), (vo_s, vo_ref, 5)):
-        write = pltpu.make_async_copy(out, ref, loc_sem.at[loc])
+            o_copy(k, d).start()
+    for write in cache_writes():
         write.start()
-        writes.append(write)
-    forward_far(w2_at, vsem)
-    for k in range(2):
-        for d in range(1, yzs):
-            arrived(rows_part((at.j + yzs - d) % yzs, k), (osend.at[k], orecv.at[k]), d - 1)
-        own_o[k].wait()
-    act_ref[pl.ds(c_f, c_a), :] = ob[:].T
-    all_in(w2_at, vsem, own_w2)
-    for write in writes:
-        write.wait()
     copies.finish()
 
 
-def front(x_pad, w1_loc, w2_loc, tables, k_cache, v_cache, ctx_len, xs, yzs, grp, c_q, c_f):
-    _, gp, rows = x_pad.shape
-    n1, kx = w1_loc.shape
-    n2 = w2_loc.shape[2]
-    dev_rows, t_len, head_dim = k_cache.shape
-    hp = yzs * c_q // head_dim
-    num_heads = hp - 2
-    c_a = n2 - c_f
-    dma = pltpu.SemaphoreType.DMA
-    f32, bf16 = jnp.float32, jnp.bfloat16
-    vspec, aspec = pl.BlockSpec(memory_space=pltpu.VMEM), pl.BlockSpec(memory_space=pl.ANY)
-    sems = lambda *s: [dma(s), dma(s)]
-    cache = jax.ShapeDtypeStruct(k_cache.shape, bf16)
-    return pl.pallas_call(
-        functools.partial(front_kernel, xs, yzs, grp, c_q, c_f, num_heads),
-        out_shape=(
-            jax.ShapeDtypeStruct((n2, rows), bf16),
-            jax.ShapeDtypeStruct((yzs, xs) + w2_loc.shape[1:], bf16),
-            jax.ShapeDtypeStruct((xs, gp, rows), bf16),
-            cache,
-            cache,
-        ),
-        in_specs=[pl.BlockSpec(memory_space=pltpu.SMEM)] + [vspec] * 5 + [aspec] * 2,
-        out_specs=(vspec, aspec, vspec, aspec, aspec),
-        scratch_shapes=[
-            pltpu.VMEM((xs, yzs, gp, rows), bf16),
-            pltpu.VMEM((xs * yzs * gp, rows), bf16),
-            pltpu.VMEM((xs * yzs // 2, 2 * gp, 128), f32),
-            pltpu.VMEM((n1, xs * kx), bf16),
-            pltpu.VMEM((rows, c_q), bf16),
-            pltpu.VMEM((yzs, dev_rows, c_q), bf16),
-            pltpu.VMEM((hp, dev_rows, head_dim), f32),
-        ] + [pltpu.VMEM(k_cache.shape, bf16)] * 4 + [
-            pltpu.VMEM((2, yzs, dev_rows // 2, c_a), bf16),
-            pltpu.VMEM((rows, c_a), bf16),
-            dma((8,)),
-        ] + sems(xs - 1) + sems(2, RING * RING) + sems(9) + sems(9) + sems(yzs - 1) + sems(2, yzs - 1),
-        compiler_params=pltpu.CompilerParams(collective_id=0, has_side_effects=True, vmem_limit_bytes=VMEM_LIMIT),
-        name="front",
-    )(ctx_len, x_pad, w1_loc, w2_loc, *tables, k_cache, v_cache)
-
-
-def back_kernel(xs, yzs, w_ref, act, x_ref, y_ref, zb, r1, r2, r3, r4, yv, loc_sem, s1, q1, s2, q2, s3, q3, s4, q4, ys, yq):
-    at = Where(xs, yzs)
+def second_phase(
+    xs, yzs, grp, at, any_peer, finish_first, finish_last, w2v, act, xo, y_ref,
+    loc_sem, sem1, sem2, sem3, sem4, ysem, ready, zb, r1, r2, r3, r4, yv, ws,
+):
+    for d in (UP, DOWN):
+        for peer in (at.block(d, 0), at.block(0, d)):
+            pl.semaphore_signal(ready, inc=1, device_id=at.on_yz(peer), device_id_type=MESH)
+    yv[:] = jnp.zeros_like(yv)
+    late = finish_first()
+    (s1, q1), (s2, q2), (s3, q3), (s4, q4), (ys, yq) = sem1, sem2, sem3, sem4, ysem
     order = ("z", "y")
     hr = zb.shape[2] // 2
-    gp = x_ref.shape[1]
-    at.greet()
-    copies = Copies(at.on_yz(at.block(0, UP)))
+    copies = Copies(any_peer)
     send, arrived = copies.send, copies.arrived
 
     def zat(h, df, dg):
@@ -421,13 +462,17 @@
         return zb.at[dz, dy, pl.ds(h * hr, hr)]
 
     def compute(dz, dy):
-        zb[dz, dy] = jnp.dot(w_ref[at.block(dz, dy)], act[:], preferred_element_type=jnp.float32)
+        w = w2v[at.block(dz, dy)].astype(jnp.float32)
+        for x in range(xs):
+            ws[pl.ds(x * grp, grp), :] = w[x, :grp]
+        zb[dz, dy] = jnp.dot(ws[:].astype(jnp.bfloat16), act[:], preferred_element_type=jnp.float32)
 
     def send1(h, dg):
         d = 1 if dg < 2 else 3
         send(zat(h, 2, dg), r1.at[h, dg], s1.at[h, dg], q1.at[h, dg], at.step(order[h], 0, d))
 
     compute(2, 2)
+    pl.semaphore_wait(ready, RING)
     send1(0, 2)
     send1(1, 2)
     for k in (0, 1, 3):
@@ -467,20 +512,27 @@
         ref = zat(h, 0, dg)
         ref[:] = ref[:] + r2[h, 0, dg] + r2[h, 1, dg]
 
-    hh = hr // 2
+    big = r3.shape[2]
+    sizes = (big, hr - big)
 
     def part(h, dg, k):
         dz, dy = (0, dg) if order[h] == "z" else (dg, 0)
-        return zb.at[dz, dy, pl.ds(h * hr + k * hh, hh)]
+        return zb.at[dz, dy, pl.ds(h * hr + k * big, sizes[k])]
+
+    def r3_at(h, k):
+        return r3.at[h, k, pl.ds(0, sizes[k])]
+
+    def r4_at(h, s, k):
+        return r4.at[h, s, k, pl.ds(0, sizes[k])]
 
     def send4(h, up, k):
         dg, d, s = (1, 1, 0) if up else (3, 3, 1)
-        send(part(h, dg, k), r4.at[h, s, k], s4.at[h, s, k], q4.at[h, s, k], at.step(order[h], 1, d))
+        send(part(h, dg, k), r4_at(h, s, k), s4.at[h, s, k], q4.at[h, s, k], at.step(order[h], 1, d))
 
     for h in range(2):
         plane(h, 2)
-        send(part(h, 2, 0), r3.at[h, 0], s3.at[h, 0], q3.at[h, 0], at.step(order[h], 1, 1))
-        send(part(h, 2, 1), r3.at[h, 1], s3.at[h, 1], q3.at[h, 1], at.step(order[h], 1, 3))
+        send(part(h, 2, 0), r3_at(h, 0), s3.at[h, 0], q3.at[h, 0], at.step(order[h], 1, 1))
+        send(part(h, 2, 1), r3_at(h, 1), s3.at[h, 1], q3.at[h, 1], at.step(order[h], 1, 3))
     for h in range(2):
         plane(h, 1)
         send4(h, True, 1)
@@ -489,13 +541,13 @@
     for h in range(2):
         plane(h, 0)
     for h in range(2):
-        arrived(r3.at[h, 0], s3.at[h, 0], q3.at[h, 0])
+        arrived(r3_at(h, 0), s3.at[h, 0], q3.at[h, 0])
         ref = part(h, 1, 0)
-        ref[:] = ref[:] + r3[h, 0]
+        ref[:] = ref[:] + r3_at(h, 0)[:]
         send4(h, True, 0)
-        arrived(r3.at[h, 1], s3.at[h, 1], q3.at[h, 1])
+        arrived(r3_at(h, 1), s3.at[h, 1], q3.at[h, 1])
         ref = part(h, 3, 1)
-        ref[:] = ref[:] + r3[h, 1]
+        ref[:] = ref[:] + r3_at(h, 1)[:]
         send4(h, False, 1)
     def y_copy(x, d):
         return pltpu.make_async_remote_copy(
@@ -505,17 +557,18 @@
     for h in range(2):
         for k in range(2):
             for s in range(2):
-                arrived(r4.at[h, s, k], s4.at[h, s, k], q4.at[h, s, k])
-            z = zb[0, 0, pl.ds(h * hr + k * hh, hh)] + r4[h, 0, k] + r4[h, 1, k]
-            n = hh // gp
-            for i in range(n):
-                x = h * 2 * n + k * n + i
-                yv[x] = (x_ref[x].astype(jnp.float32) + z[i * gp:(i + 1) * gp]).astype(jnp.bfloat16)
+                arrived(r4_at(h, s, k), s4.at[h, s, k], q4.at[h, s, k])
+            ref = part(h, 0, k)
+            ref[:] = ref[:] + r4_at(h, 0, k)[:] + r4_at(h, 1, k)[:]
+            done = xs // 4
+            for x in range((2 * h + k) * done, (2 * h + k + 1) * done):
+                z = zb[0, 0, pl.ds(x * grp, grp), :]
+                yv[x, :grp, :] = (xo[x, :grp, :].astype(jnp.float32) + z).astype(jnp.bfloat16)
                 d = lax.rem(x - at.x + xs, xs)
 
                 @pl.when(d == 0)
                 def _():
-                    pltpu.make_async_copy(yv.at[x], y_ref.at[x], loc_sem.at[0]).start()
+                    pltpu.make_async_copy(yv.at[x], y_ref.at[x], loc_sem.at[3]).start()
 
                 @pl.when(d != 0)
                 def _():
@@ -523,39 +576,45 @@
 
     for d in range(1, xs):
         arrived(y_ref.at[(at.x + xs - d) % xs], ys.at[d - 1], yq.at[d - 1])
-    pltpu.make_async_copy(yv.at[at.x], y_ref.at[at.x], loc_sem.at[0]).wait()
+    pltpu.make_async_copy(yv.at[at.x], y_ref.at[at.x], loc_sem.at[3]).wait()
     for d in range(1, xs):
         y_copy((at.x + d) % xs, d).wait_send()
     copies.finish()
-
-
-def back(w2, act, x_own):
-    _, block, _ = w2.shape
-    yzs = w2.shape[0]
-    xs, gp, rows = x_own.shape
-    dma = pltpu.SemaphoreType.DMA
+    finish_last(late)
+
+
+def layer(x_pad, w1_loc, w2_loc, tables, k_cache, v_cache, ctx_len, xs, yzs, grp, c_q, c_f):
+    _, gp, rows = x_pad.shape
+    n2 = w2_loc.shape[2]
+    dev_rows, t_len, head_dim = k_cache.shape
+    num_heads = yzs * c_q // head_dim - 2
+    c_a = n2 - c_f
+    dma, vmem = pltpu.SemaphoreType.DMA, pltpu.VMEM
     bf16 = jnp.bfloat16
-    vmem = lambda *s: pltpu.VMEM(s, jnp.float32)
-    vspec, aspec = pl.BlockSpec(memory_space=pltpu.VMEM), pl.BlockSpec(memory_space=pl.ANY)
-    sems = lambda *s: [dma(s), dma(s)]
-    hr = block // 2
+    vspec, aspec = pl.BlockSpec(memory_space=vmem), pl.BlockSpec(memory_space=pl.ANY)
+    sems = lambda *shape: [dma(shape), dma(shape)]
+    cache = jax.ShapeDtypeStruct(k_cache.shape, bf16)
     return pl.pallas_call(
-        functools.partial(back_kernel, xs, yzs),
-        out_shape=jax.ShapeDtypeStruct((xs, gp, rows), bf16),
-        in_specs=[vspec] * 3,
-        out_specs=aspec,
+        functools.partial(layer_kernel, xs, yzs, grp, c_q, c_f, num_heads),
+        out_shape=(jax.ShapeDtypeStruct((xs, gp, rows), bf16), cache, cache),
+        in_specs=[pl.BlockSpec(memory_space=pltpu.SMEM)] + [vspec] * 5 + [aspec] * 2,
+        out_specs=(aspec, aspec, aspec),
         scratch_shapes=[
-            vmem(RING, RING, block, rows),
-            vmem(2, RING, hr, rows),
-            vmem(2, 2, RING, hr, rows),
-            vmem(2, 2, hr // 2, rows),
-            vmem(2, 2, 2, hr // 2, rows),
-            pltpu.VMEM((xs, gp, rows), bf16),
-            dma((1,)),
-        ] + sems(2, RING) + sems(2, 2, RING) + sems(2, 2) + sems(2, 2, 2) + sems(xs - 1),
-        compiler_params=pltpu.CompilerParams(collective_id=1, has_side_effects=True, vmem_limit_bytes=VMEM_LIMIT),
-        name="back",
-    )(w2, act, x_own)
+            vmem((n2, rows), bf16),
+            vmem((yzs, xs) + w2_loc.shape[1:], bf16),
+            vmem((xs, gp, rows), bf16),
+            vmem(k_cache.shape, bf16),
+            vmem(k_cache.shape, bf16),
+            vmem((2, yzs, dev_rows // 2, c_a), bf16),
+            vmem((rows, c_a), bf16),
+            dma((8,)),
+        ]
+        + sems(xs - 1) + sems(2, RING * RING) + sems(9) + sems(9) + sems(yzs - 1) + sems(2, yzs - 1)
+        + sems(2, RING) + sems(2, 2, RING) + sems(2, 2) + sems(2, 2, 2) + sems(xs - 1)
+        + [pltpu.SemaphoreType.REGULAR],
+        compiler_params=pltpu.CompilerParams(collective_id=0, has_side_effects=True, vmem_limit_bytes=VMEM_LIMIT),
+        name="layer",
+    )(ctx_len, x_pad, w1_loc, w2_loc, *tables, k_cache, v_cache)
 
 
 def solution(mesh):
@@ -589,8 +648,7 @@
         c_q = wqkv_loc.shape[1]
         c_f = wgate_loc.shape[1]
         tables = rope_tables(len_loc, kc_loc.shape[2])
-        act, w2, x_own, k_all, v_all = front(x_pad, w1_loc, w2_loc, tables, kc_loc, vc_loc, len_loc, xs, yzs, grp, c_q, c_f)
-        y_back = back(w2.reshape(yzs, xs * gp, -1), act, x_own)
+        y_back, k_all, v_all = layer(x_pad, w1_loc, w2_loc, tables, kc_loc, vc_loc, len_loc, xs, yzs, grp, c_q, c_f)
         y_loc = y_back[:, :grp].transpose(1, 0, 2).reshape(grp, n_rows).T
         return y_loc, k_all, v_all
 

time: 187 us -> 175 us (0.936)
  Pallas kernels: 169 us -> 157 us
    pallas_call x2 -> x1, Pallas kernels: 169 us -> 157 us  [layer(): pl.pallas_call(functools.partial(layer_kernel, xs, yzs, grp, c_q, c_f, nu...]
where the time goes in v5:
time: 175 us
  Pallas kernels  157 us (90%)
  local copies, waits for them, and re-layouts  14.5 us (8%)
  other arithmetic  2.56 us (1%)
    pallas_call x1, Pallas kernels, layer(): pl.pallas_call(functools.partial(layer_kernel, xs, yzs, grp, c_q, c_f, nu...  157 us
    unnamed x18, local copies, waits for them, and re-layouts  7.36 us

profile of v5, /device:TPU:1, one launch (start us, length us, event | category | flops | bytes accessed | tf_op | source)
XLA Modules:
  0.0 174.7 jit_solution(16750094808380141518)
XLA Ops:
  0.6 0.7 convert_element_type.9
  1.3 0.1 pad.23.clone
  1.4 0.7 pad.12
  2.1 0.2 fusion
  2.3 0.7 pad_maximum_fusion
  3.0 1.0 copy.17
  4.0 0.0 copy-start.4
  4.0 0.0 copy-start.5
  4.1 1.3 copy.21
  5.4 0.2 copy.24
  5.6 0.9 maximum_maximum_fusion.x_ref
  6.5 0.0 copy-done.4
  6.5 0.0 copy-done.5
  6.5 0.1 maximum_bitcast_fusion
  6.6 0.3 copy.19
  6.9 0.0 copy-start.2
  6.9 0.2 reshape.35
  7.1 0.0 copy-start.3
  7.1 0.9 pad.14.w2_ref
  8.0 0.0 copy-done.2
  8.0 0.4 copy-done.3
  8.4 1.3 concatenate.16
  9.7 0.4 reshape.33
  10.1 0.1 pad.13
  10.2 1.5 copy.18
  11.7 156.9 %layer.1 = (bf16[8,24,1024]{2,1,0:T(8,128)(2,1)}, bf16[64,128,128]{2,1,0:T(8,128)(2,1)}, bf16[64,128,128]{2,1,0:T(8,128)(2,1)}) custom-call(s32[64]{0:T(128)} %len_ref.1, bf16[8,24,1024]{2,1,0:T(8,128)(2,1)} %maximum_maximum_fusion.x_ref, bf16[1600,384]{1,0:T(8,128)(2,1)} %bitcast.20, bf16[16,24,880]{2,1,0:T(8,128)(2,1)} %pad.14.w2_ref, ...), custom_call_target="tpu_custom_call" | custom-call | tf_op jit(solution)/shard_map/layer/pallas_call | solution.py:597
  168.6 0.0 copy-start.1
  168.6 1.2 slice_bitcast_fusion
  169.8 0.2 copy.20
  170.0 1.0 copy.22
  171.0 0.0 copy-done.1
  171.0 0.0 copy-start
  171.0 1.3 copy.27
  172.3 1.0 copy-done
  173.4 1.3 copy.28
  (4 shorter events, 0.1 us)
Async XLA Ops:
  4.0 2.5 %copy-start.4 = (bf16[704,352]{1,0:T(8,128)(2,1)S(1)}, bf16[704,352]{1,0:T(8,128)(2,1)}, u32[]{:S(2)}) copy-start(bf16[704,352]{1,0:T(8,128)(2,1)} %param.16) | copy-start | bytes 1486852
  4.0 2.4 %copy-start.5 = (bf16[176,352]{1,0:T(8,128)(2,1)S(1)}, bf16[176,352]{1,0:T(8,128)(2,1)}, u32[]{:S(2)}) copy-start(bf16[176,352]{1,0:T(8,128)(2,1)} %param.15) | copy-start | bytes 371716
  6.9 1.1 copy-start.2
  7.1 1.3 copy-start.3
  168.6 2.4 %copy-start.1 = (bf16[64,128,128]{2,1,0:T(8,128)(2,1)S(1)}, bf16[64,128,128]{2,1,0:T(8,128)(2,1)}, u32[]{:S(2)}) copy-start(bf16[64,128,128]{2,1,0:T(8,128)(2,1)} %get-tuple-element.18) | copy-start | bytes 6291460
  171.0 2.3 %copy-start = (bf16[64,128,128]{2,1,0:T(8,128)(2,1)S(1)}, bf16[64,128,128]{2,1,0:T(8,128)(2,1)}, u32[]{:S(2)}) copy-start(bf16[64,128,128]{2,1,0:T(8,128)(2,1)} %get-tuple-element.19) | copy-start | bytes 6291460

commit v6 on v5

--- a/solution.py
+++ b/solution.py
@@ -55,13 +55,16 @@
     def x_other(self, dc):
         return ((self.chip + dc) % RING) * 2 + (1 - self.core)
 
+    def peers(self):
+        on_x = [self.on_x((self.x + d) % self.xs) for d in range(1, self.xs)]
+        return on_x + [self.on_yz((self.j + d) % self.yzs) for d in range(1, self.yzs)]
+
     def greet(self):
-        barrier = pltpu.get_barrier_semaphore()
-        peers = [self.on_x((self.x + d) % self.xs) for d in range(1, self.xs)]
-        peers += [self.on_yz((self.j + d) % self.yzs) for d in range(1, self.yzs)]
-        for peer in peers:
-            pl.semaphore_signal(barrier, inc=1, device_id=peer, device_id_type=MESH)
-        pl.semaphore_wait(barrier, len(peers))
+        for peer in self.peers():
+            pl.semaphore_signal(pltpu.get_barrier_semaphore(), inc=1, device_id=peer, device_id_type=MESH)
+
+    def greeted(self):
+        pl.semaphore_wait(pltpu.get_barrier_semaphore(), len(self.peers()))
 
 
 class Copies:
@@ -85,7 +88,7 @@
 
 
 def layer_kernel(
-    xs, yzs, grp, c_q, c_f, num_heads, len_ref, x_ref, w1_ref, w2_ref, cos_ref, sin_ref, kc_ref, vc_ref,
+    xs, yzs, gp, len_ref, x_ref, gain_ref, wq_ref, wg_ref, wu_ref, wa_ref, wm_ref, cos_ref, sin_ref, kc_ref, vc_ref,
     y_ref, ko_ref, vo_ref,
     act, w2v, xo, k_s, v_s, o_send, ob,
     loc_sem, xsend, xrecv, gsend, grecv, wsend, wrecv, vsend, vrecv, qsend, qrecv, osend, orecv,
@@ -93,10 +96,13 @@
 ):
     f32, bf16 = jnp.float32, jnp.bfloat16
     dma, vmem = pltpu.SemaphoreType.DMA, pltpu.VMEM
-    gp, rows = x_ref.shape[1:]
+    grp = x_ref.shape[0]
+    rows, c_a = ob.shape
     dev_rows, t_len, head_dim = k_s.shape
-    n1, kx = w1_ref.shape
-    c_a = ob.shape[1]
+    c_q, k_loc = wq_ref.shape
+    n1 = c_q + 2 * wg_ref.shape[1]
+    c_f = wm_ref.shape[0]
+    num_heads = yzs * c_a // head_dim
     part = dev_rows // 2
     block = xs * grp
     hr = block // 2
@@ -121,8 +127,9 @@
         return [pltpu.make_async_copy(src, dst, loc_sem.at[loc]) for src, dst, loc in ((k_s, ko_ref, 4), (v_s, vo_ref, 5))]
 
     gather_and_attend = functools.partial(
-        first_phase, xs, yzs, grp, c_q, c_f, num_heads, at, any_peer, w2_at, o_copy, o_own, cache_writes,
-        len_ref, x_ref, w1_ref, w2_ref, cos_ref, sin_ref, kc_ref, vc_ref, act, xo, k_s, v_s, o_send,
+        first_phase, xs, yzs, num_heads, at, any_peer, w2_at, o_copy, o_own, cache_writes,
+        len_ref, x_ref, gain_ref, wq_ref, wg_ref, wu_ref, wa_ref, wm_ref, cos_ref, sin_ref, kc_ref, vc_ref,
+        act, w2v, xo, k_s, v_s, o_send,
         loc_sem, (xsend, xrecv), (gsend, grecv), (wsend, wrecv), (vsend, vrecv), (qsend, qrecv),
     )
     pl.run_scoped(
@@ -130,21 +137,26 @@
         vmem((xs, yzs, gp, rows), bf16),
         vmem((xs * yzs * gp, rows), bf16),
         vmem((xs * yzs // 2, 2 * gp, 128), f32),
-        vmem((n1, xs * kx), bf16),
+        vmem((n1, xs * yzs * gp), bf16),
         vmem((rows, c_q), bf16),
         vmem((yzs, dev_rows, c_q), bf16),
         vmem((num_heads + 2, dev_rows, head_dim), f32),
+        vmem((xs, gp, rows), bf16),
+        vmem((gp, rows), f32),
+        vmem((k_loc + 8, c_f + c_a), f32),
+        vmem((yzs * gp, c_f), f32),
+        vmem((c_f + c_a, k_loc), f32),
     )
 
     def finish_first():
         late = Copies(any_peer)
-        forward_far(late, at, w2_at, (vsend, vrecv))
+        share_far(late, at, w2_at, (vsend, vrecv))
         for k in range(2):
             for d in range(1, yzs):
                 late.arrived(o_rows((at.j + yzs - d) % yzs, k), osend.at[k, d - 1], orecv.at[k, d - 1])
             o_own(k).wait()
         act[pl.ds(c_f, c_a), :] = ob[:].T
-        all_in(late, at, w2_at, (vsend, vrecv), pltpu.make_async_copy(w2_ref, w2_at(at.x), loc_sem.at[2]))
+        all_in(late, at, w2_at, (vsend, vrecv))
         return late
 
     def finish_last(late):
@@ -153,8 +165,9 @@
         for k in range(2):
             for d in range(1, yzs):
                 o_copy(k, d).wait_send()
-        for slot, k in enumerate((None, None, None, 0, 0, None, None)):
-            remote(w2_at(at.x, k), w2_at(at.x, k), vsend.at[slot], vrecv.at[slot], any_peer).wait_send()
+        for slot in range(9):
+            r = w2_at(at.x, None if slot in (4, 7, 8) else 0)
+            remote(r, r, vsend.at[slot], vrecv.at[slot], any_peer).wait_send()
         late.finish()
 
     sum_and_return = functools.partial(
@@ -178,12 +191,15 @@
     return pltpu.make_async_remote_copy(src_ref=src, dst_ref=dst, send_sem=ssem, recv_sem=rsem, device_id=peer, device_id_type=MESH)
 
 
-def spread_own(copies, at, src, region, sems, loc_sem):
-    own = pltpu.make_async_copy(src, region(at.x), loc_sem)
-    own.start()
-    for slot, to in enumerate((at.x_of(UP), at.x_of(DOWN), at.x_other(0))):
-        copies.send(src, region(at.x), sems[0].at[slot], sems[1].at[slot], at.on_x(to))
-    return own
+def spread_own(copies, at, region, sems):
+    def send(slot, k, x):
+        r = region(at.x, k)
+        copies.send(r, r, sems[0].at[slot], sems[1].at[slot], at.on_x(x))
+
+    for k in range(2):
+        send(2 * k, k, at.x_of(UP))
+        send(2 * k + 1, 1 - k, at.x_of(DOWN))
+    send(4, None, at.x_other(0))
 
 
 def pass_on(copies, at, r, sems, slot, x):
@@ -194,47 +210,59 @@
     copies.arrived(r, sems[0].at[slot], sems[1].at[slot])
 
 
-def forward_near(copies, at, region, sems):
-    block_in(copies, region(at.x_of(DOWN)), sems, 0)
-    pass_on(copies, at, region(at.x_of(DOWN), 0), sems, 3, at.x_of(UP))
-    block_in(copies, region(at.x_of(UP)), sems, 1)
-    pass_on(copies, at, region(at.x_of(UP), 1), sems, 4, at.x_of(DOWN))
-    pass_on(copies, at, region(at.x_of(DOWN)), sems, 5, at.x_other(0))
-    pass_on(copies, at, region(at.x_of(UP)), sems, 6, at.x_other(0))
-
-
-def forward_far(copies, at, region, sems):
+def forward_half(copies, at, region, sems):
+    for slot, k, here, to in ((0, 0, DOWN, UP), (1, 1, UP, DOWN)):
+        r = region(at.x_of(here), k)
+        block_in(copies, r, sems, slot)
+        pass_on(copies, at, r, sems, slot + 5, at.x_of(to))
+
+
+def share_near(copies, at, region, sems):
+    for slot, k, here in ((2, 1, DOWN), (3, 0, UP)):
+        block_in(copies, region(at.x_of(here), k), sems, slot)
+        pass_on(copies, at, region(at.x_of(here)), sems, slot + 5, at.x_other(0))
+
+
+def share_far(copies, at, region, sems):
     for k in range(2):
         r = region(at.x_of(FAR), k)
-        block_in(copies, r, sems, 3 + k)
-        pass_on(copies, at, r, sems, 7 + k, at.x_other(0))
-
-
-def all_in(copies, at, region, sems, own):
-    block_in(copies, region(at.x_other(0)), sems, 2)
-    block_in(copies, region(at.x_other(DOWN)), sems, 5)
-    block_in(copies, region(at.x_other(UP)), sems, 6)
+        block_in(copies, r, sems, 5 + k)
+        pass_on(copies, at, r, sems, 9 + k, at.x_other(0))
+
+
+def all_in(copies, at, region, sems):
+    for slot, here in ((4, 0), (7, DOWN), (8, UP)):
+        block_in(copies, region(at.x_other(here)), sems, slot)
     for k in range(2):
-        block_in(copies, region(at.x_other(FAR), k), sems, 7 + k)
-    own.wait()
+        block_in(copies, region(at.x_other(FAR), k), sems, 9 + k)
 
 
 def first_phase(
-    xs, yzs, grp, c_q, c_f, num_heads, at, any_peer, w2_at, o_copy, o_own, cache_writes,
-    len_ref, x_ref, w1_ref, w2_ref, cos_ref, sin_ref, kc_ref, vc_ref, act, xo, k_s, v_s, o_send,
-    loc_sem, xsem, gsem, wsem, vsem, qsem, xg, h, gcol, w1, qkv_s, qkv_in, heads,
+    xs, yzs, num_heads, at, any_peer, w2_at, o_copy, o_own, cache_writes,
+    len_ref, x_ref, gain_ref, wq_ref, wg_ref, wu_ref, wa_ref, wm_ref, cos_ref, sin_ref, kc_ref, vc_ref,
+    act, w2v, xo, k_s, v_s, o_send,
+    loc_sem, xsem, gsem, wsem, vsem, qsem, xg, h, gcol, w1, qkv_s, qkv_in, heads, x_send, stage, tall, wide_s, narrow,
 ):
     f32, bf16 = jnp.float32, jnp.bfloat16
     half = xs // 2
     quarter = half // 2
-    gp, rows = x_ref.shape[1:]
+    grp = x_ref.shape[0]
+    _, gp, rows = x_send.shape
     dev_rows = rows // yzs
-    kx = w1_ref.shape[1]
+    c_q, k_loc = wq_ref.shape
+    c_f, c_a = wm_ref.shape[0], wa_ref.shape[0]
+    kx = yzs * gp
+    at.greet()
     read_k = pltpu.make_async_copy(kc_ref, k_s, loc_sem.at[4])
     read_k.start()
     read_v = pltpu.make_async_copy(vc_ref, v_s, loc_sem.at[5])
     read_v.start()
-    at.greet()
+    stage[:] = jnp.zeros_like(stage)
+    stage[grp:grp + 1, :grp] = gain_ref[:].astype(f32)
+    for x in range(xs):
+        stage[:grp, :] = x_ref[:, x * rows:(x + 1) * rows].astype(f32)
+        x_send[x] = stage[:].astype(bf16)
+    at.greeted()
     copies, late = Copies(any_peer), Copies(any_peer)
 
     def send(src, dst, sems, idx, peer):
@@ -243,19 +271,31 @@
     def arrived(region, sems, idx):
         copies.arrived(region, sems[0].at[idx], sems[1].at[idx])
 
-    own_x = pltpu.make_async_copy(x_ref.at[at.x], xg.at[at.x, at.j], loc_sem.at[0])
+    own_x = pltpu.make_async_copy(x_send.at[at.x], xg.at[at.x, at.j], loc_sem.at[0])
     own_x.start()
     for d in range(1, xs):
         to = (at.x + d) % xs
-        send(x_ref.at[to], xg.at[at.x, at.j], xsem, d - 1, at.on_x(to))
-
-    n1 = w1_ref.shape[0]
+        send(x_send.at[to], xg.at[at.x, at.j], xsem, d - 1, at.on_x(to))
+
+    n1 = w1.shape[0]
 
     def w1_at(x, k=None):
         cols = pl.ds(pl.multiple_of(x * kx, 128), kx)
         return w1.at[:, cols] if k is None else w1.at[pl.ds(k * (n1 // 2), n1 // 2), cols]
 
-    own_w1 = spread_own(copies, at, w1_ref, w1_at, wsem, loc_sem.at[1])
+    own_cols = pl.ds(pl.multiple_of(at.x * kx, 128), kx)
+    tall[k_loc:, :] = jnp.zeros((tall.shape[0] - k_loc, tall.shape[1]), f32)
+    row = 0
+    for ref in (wq_ref, wg_ref, wu_ref):
+        w = ref[:].astype(f32)
+        w = w.T if ref is wq_ref else w
+        n = w.shape[1]
+        tall[:k_loc, :n] = w
+        for j in range(yzs):
+            wide_s[j * gp:(j + 1) * gp, :n] = tall[j * grp:j * grp + gp, :n]
+        w1[row:row + n, own_cols] = wide_s[:, :n].T.astype(bf16)
+        row += n
+    spread_own(copies, at, w1_at, wsem)
     own_x.wait()
     for d in range(1, xs):
         arrived(xg.at[(at.x + xs - d) % xs, at.j], xsem, d - 1)
@@ -284,6 +324,11 @@
         pass_rows(s, 0, 0, first_axis, DOWN, 1)
         both_ways(s, 0)
     xo[:] = xg[:, at.j]
+    narrow[:c_f, :] = wm_ref[:].astype(f32)
+    narrow[c_f:, :] = wa_ref[:].astype(f32)
+    tall[:k_loc, :] = narrow[:].T
+    for j in range(yzs):
+        w2v[j, at.x] = tall[j * grp:j * grp + gp, :].astype(bf16)
     for s in halves:
         rows_in(s, DOWN, 0, 0)
         pass_rows(s, DOWN, 0, first_axis, UP, FAR, 0, quarter)
@@ -295,12 +340,13 @@
         rows_in(s, FAR, 0, FAR, 0, quarter)
         rows_in(s, FAR, 0, DOWN, quarter, quarter)
         both_ways(s, FAR)
+    forward_half(copies, at, w1_at, wsem)
+    spread_own(late, at, w2_at, vsem)
     for s in halves:
         for df in (0, DOWN):
             rows_in(s, df, DOWN, slot_up + df)
             pass_rows(s, df, DOWN, second_axis, UP, slot_far + df)
-    forward_near(copies, at, w1_at, wsem)
-    spread_own(late, at, w2_ref, w2_at, vsem, loc_sem.at[2])
+    share_near(copies, at, w1_at, wsem)
     for s in halves:
         for df in (UP, FAR):
             rows_in(s, df, UP, slot_down + df)
@@ -332,7 +378,7 @@
 
     zero = jnp.zeros((8, rows), f32)
     s1, s2 = lax.fori_loop(0, xs * pairs, add_up, (zero, zero), unroll=4)
-    forward_far(copies, at, w1_at, wsem)
+    share_far(copies, at, w1_at, wsem)
     d_model = grp * xs * yzs
     mean = jnp.sum(s1, axis=0, keepdims=True) / d_model
     var = jnp.sum(s2, axis=0, keepdims=True) / d_model - mean * mean
@@ -345,7 +391,7 @@
         return c
 
     lax.fori_loop(0, xs * pairs, normalize, 0, unroll=2)
-    all_in(copies, at, w1_at, wsem, own_w1)
+    all_in(copies, at, w1_at, wsem)
 
     nt = 256
 
@@ -371,11 +417,13 @@
         act[pl.ds(0, c_f), cols] = (jax.nn.silu(gate) * up).astype(bf16)
         return c
 
-    lax.fori_loop(0, rows // nt, mlp, 0)
+    forward_half(late, at, w2_at, vsem)
+    steps = rows // nt
+    lax.fori_loop(0, steps - 1, mlp, 0)
     for d in range(1, yzs):
         arrived(qkv_in.at[(at.j + yzs - d) % yzs], qsem, d - 1)
     own_q.wait()
-    forward_near(late, at, w2_at, vsem)
+    share_near(late, at, w2_at, vsem)
 
     head_dim = k_s.shape[2]
     per = 2 * c_q // head_dim
@@ -424,7 +472,6 @@
         heads[:, pl.ds(first, group), :] = jnp.swapaxes(jnp.stack(outs, axis=0), 0, 1)
         return c
 
-    c_a = o_send.shape[3]
     part = dev_rows // 2
     for k in range(2):
         lax.fori_loop(k * part // group, (k + 1) * part // group, attend, 0)
@@ -439,6 +486,7 @@
             o_copy(k, d).start()
     for write in cache_writes():
         write.start()
+    lax.fori_loop(steps - 1, steps, mlp, 0)
     copies.finish()
 
 
@@ -500,7 +548,7 @@
     for k in range(2):
         for h in range(2):
             for up in (True, False):
-                dg = k if up else 2 + k
+                dg = 1 - k if up else 2 + k
                 arrived(r1.at[h, dg], s1.at[h, dg], q1.at[h, dg])
                 ref = zat(h, 1 if up else 3, dg)
                 ref[:] = ref[:] + r1[h, dg]
@@ -549,9 +597,13 @@
         ref = part(h, 3, 1)
         ref[:] = ref[:] + r3_at(h, 1)[:]
         send4(h, False, 1)
+    def y_cols(x):
+        rows = yv.shape[2]
+        return y_ref.at[:, pl.ds(pl.multiple_of(x * rows, 128), rows)]
+
     def y_copy(x, d):
         return pltpu.make_async_remote_copy(
-            src_ref=yv.at[x], dst_ref=y_ref.at[at.x], send_sem=ys.at[d - 1], recv_sem=yq.at[d - 1], device_id=at.on_x(x), device_id_type=MESH
+            src_ref=yv.at[x], dst_ref=y_cols(at.x), send_sem=ys.at[d - 1], recv_sem=yq.at[d - 1], device_id=at.on_x(x), device_id_type=MESH
         )
 
     for h in range(2):
@@ -568,40 +620,40 @@
 
                 @pl.when(d == 0)
                 def _():
-                    pltpu.make_async_copy(yv.at[x], y_ref.at[x], loc_sem.at[3]).start()
+                    pltpu.make_async_copy(yv.at[x], y_cols(x), loc_sem.at[3]).start()
 
                 @pl.when(d != 0)
                 def _():
                     y_copy(x, d).start()
 
     for d in range(1, xs):
-        arrived(y_ref.at[(at.x + xs - d) % xs], ys.at[d - 1], yq.at[d - 1])
-    pltpu.make_async_copy(yv.at[at.x], y_ref.at[at.x], loc_sem.at[3]).wait()
+        arrived(y_cols((at.x + xs - d) % xs), ys.at[d - 1], yq.at[d - 1])
+    pltpu.make_async_copy(yv.at[at.x], y_cols(at.x), loc_sem.at[3]).wait()
     for d in range(1, xs):
         y_copy((at.x + d) % xs, d).wait_send()
     copies.finish()
     finish_last(late)
 
 
-def layer(x_pad, w1_loc, w2_loc, tables, k_cache, v_cache, ctx_len, xs, yzs, grp, c_q, c_f):
-    _, gp, rows = x_pad.shape
-    n2 = w2_loc.shape[2]
-    dev_rows, t_len, head_dim = k_cache.shape
-    num_heads = yzs * c_q // head_dim - 2
-    c_a = n2 - c_f
+def layer(x_t, gain, weights, tables, k_cache, v_cache, ctx_len, xs, yzs, gp):
+    n_rows = x_t.shape[1]
+    rows = n_rows // xs
+    dev_rows = k_cache.shape[0]
+    c_a, c_f = weights[3].shape[0], weights[4].shape[0]
+    n2 = c_a + c_f
     dma, vmem = pltpu.SemaphoreType.DMA, pltpu.VMEM
     bf16 = jnp.bfloat16
     vspec, aspec = pl.BlockSpec(memory_space=vmem), pl.BlockSpec(memory_space=pl.ANY)
     sems = lambda *shape: [dma(shape), dma(shape)]
     cache = jax.ShapeDtypeStruct(k_cache.shape, bf16)
     return pl.pallas_call(
-        functools.partial(layer_kernel, xs, yzs, grp, c_q, c_f, num_heads),
-        out_shape=(jax.ShapeDtypeStruct((xs, gp, rows), bf16), cache, cache),
-        in_specs=[pl.BlockSpec(memory_space=pltpu.SMEM)] + [vspec] * 5 + [aspec] * 2,
+        functools.partial(layer_kernel, xs, yzs, gp),
+        out_shape=(jax.ShapeDtypeStruct((gp, n_rows), bf16), cache, cache),
+        in_specs=[pl.BlockSpec(memory_space=pltpu.SMEM)] + [vspec] * 9 + [aspec] * 2,
         out_specs=(aspec, aspec, aspec),
         scratch_shapes=[
             vmem((n2, rows), bf16),
-            vmem((yzs, xs) + w2_loc.shape[1:], bf16),
+            vmem((yzs, xs, gp, n2), bf16),
             vmem((xs, gp, rows), bf16),
             vmem(k_cache.shape, bf16),
             vmem(k_cache.shape, bf16),
@@ -609,12 +661,12 @@
             vmem((rows, c_a), bf16),
             dma((8,)),
         ]
-        + sems(xs - 1) + sems(2, RING * RING) + sems(9) + sems(9) + sems(yzs - 1) + sems(2, yzs - 1)
+        + sems(xs - 1) + sems(2, RING * RING) + sems(11) + sems(11) + sems(yzs - 1) + sems(2, yzs - 1)
         + sems(2, RING) + sems(2, 2, RING) + sems(2, 2) + sems(2, 2, 2) + sems(xs - 1)
         + [pltpu.SemaphoreType.REGULAR],
         compiler_params=pltpu.CompilerParams(collective_id=0, has_side_effects=True, vmem_limit_bytes=VMEM_LIMIT),
         name="layer",
-    )(ctx_len, x_pad, w1_loc, w2_loc, *tables, k_cache, v_cache)
+    )(ctx_len, x_t, gain, *weights, *tables, k_cache, v_cache)
 
 
 def solution(mesh):
@@ -628,28 +680,12 @@
     len_spec = P(("dp", "x", "yz"))
 
     def local_layer(x_loc, gain_loc, wqkv_loc, wgate_loc, wup_loc, wao_loc, wmo_loc, kc_loc, vc_loc, len_loc):
-        n_rows, grp = x_loc.shape
-        pad = -grp % 8
-        gp = grp + pad
-        rows = n_rows // xs
-        bf16 = jnp.bfloat16
-
-        def pad_groups(w):
-            n = w.shape[1]
-            return jnp.pad(w.reshape(yzs, grp, n), ((0, 0), (0, pad), (0, 0)))
-
-        w1_loc = jnp.concatenate([wqkv_loc, wgate_loc, wup_loc], axis=1)
-        w1_loc = pad_groups(w1_loc).reshape(yzs * gp, -1).T
-        w2_loc = pad_groups(jnp.concatenate([wmo_loc, wao_loc], axis=0).T)
-
-        x_t = x_loc.T.reshape(grp, xs, rows).transpose(1, 0, 2)
-        gain_row = jnp.broadcast_to(jnp.pad(gain_loc, (0, rows - grp)).reshape(1, 1, rows), (xs, 1, rows))
-        x_pad = jnp.concatenate([x_t, gain_row, jnp.zeros((xs, pad - 1, rows), bf16)], axis=1)
-        c_q = wqkv_loc.shape[1]
-        c_f = wgate_loc.shape[1]
+        grp = x_loc.shape[1]
+        gp = grp + -grp % 8
         tables = rope_tables(len_loc, kc_loc.shape[2])
-        y_back, k_all, v_all = layer(x_pad, w1_loc, w2_loc, tables, kc_loc, vc_loc, len_loc, xs, yzs, grp, c_q, c_f)
-        y_loc = y_back[:, :grp].transpose(1, 0, 2).reshape(grp, n_rows).T
+        weights = (wqkv_loc.T, wgate_loc, wup_loc, wao_loc, wmo_loc)
+        y_t, k_all, v_all = layer(x_loc.T, gain_loc.reshape(1, grp), weights, tables, kc_loc, vc_loc, len_loc, xs, yzs, gp)
+        y_loc = y_t[:grp].T
         return y_loc, k_all, v_all
 
     in_specs = (row_spec, P(both_axes), in_w_spec, in_w_spec, in_w_spec, out_w_spec, out_w_spec, cache_spec, cache_spec, len_spec)

time: 175 us -> 162 us (0.926)
  local copies, waits for them, and re-layouts: 14.5 us -> 6.4 us
  Pallas kernels: 157 us -> 152 us
    pallas_call x1, Pallas kernels: 157 us -> 152 us  [layer(): pl.pallas_call(functools.partial(layer_kernel, xs, yzs, gp), out_shape=(j...]
    unnamed x18 -> x4, local copies, waits for them, and re-layouts: 7.36 us -> 4.63 us
    reshape x5 -> x0, local copies, waits for them, and re-layouts: 2.36 us -> none  [the longest x1 1.54 us: local_layer(): w1_loc = pad_groups(w1_loc).reshape(yzs * gp, -1).T]
where the time goes in v6:
time: 162 us; the launch traced here: 161 us
  Pallas kernels  152 us (94%)
  local copies, waits for them, and re-layouts  6.4 us (4%)
    pallas_call x1, Pallas kernels, layer(): pl.pallas_call(functools.partial(layer_kernel, xs, yzs, gp), out_shape=(j...  152 us
    unnamed x4, local copies, waits for them, and re-layouts  4.63 us

profile of v6, /device:TPU:1, one launch (start us, length us, event | category | flops | bytes accessed | tf_op | source)
XLA Modules:
  0.0 160.7 jit_solution(16768583373093007049)
XLA Ops:
  0.6 0.7 convert_element_type.3
  1.3 0.2 fusion
  1.5 0.7 pad_maximum_fusion
  2.2 152.1 %layer.1 = (bf16[24,8192]{1,0:T(8,128)(2,1)}, bf16[64,128,128]{2,1,0:T(8,128)(2,1)}, bf16[64,128,128]{2,1,0:T(8,128)(2,1)}) custom-call(s32[64]{0:T(128)} %len_ref.1, bf16[22,8192]{1,0:T(8,128)(2,1)} %bitcast.5, bf16[1,22]{1,0:T(2,128)(2,1)} %bitcast.7, bf16[192,352]{1,0:T(8,128)(2,1)} %bitcast.6, bf16[352,704]{1,0:T(8,128)(2,1)} %wg_ref.1, ...), custom_call_target="tpu_custom_call" | custom-call | tf_op jit(solution)/shard_map/layer/pallas_call | solution.py:649
  154.3 1.8 %slice_bitcast_fusion = bf16[8192,22]{0,1:T(8,128)(2,1)} fusion(bf16[24,8192]{1,0:T(8,128)(2,1)} %get-tuple-element.6), kind=kLoop, calls=%fused_computation | loop fusion | bytes 720896 | tf_op jit(solution)/shard_map/transpose | solution.py:688
  156.1 0.0 copy-start
  156.1 3.3 %copy.15 = bf16[64,128,128]{2,1,0:T(8,128)(2,1)} copy(bf16[64,128,128]{2,1,0:T(8,128)(2,1)} %get-tuple-element.18) | data formatting | bytes 4194304
  159.4 0.0 copy-done
  159.4 1.3 copy.16
  (1 shorter events, 0.0 us)
Async XLA Ops:
  156.1 3.3 %copy-start = (bf16[64,128,128]{2,1,0:T(8,128)(2,1)S(1)}, bf16[64,128,128]{2,1,0:T(8,128)(2,1)}, u32[]{:S(2)}) copy-start(bf16[64,128,128]{2,1,0:T(8,128)(2,1)} %get-tuple-element.19) | copy-start | bytes 6291460

commit v7 on v6

--- a/solution.py
+++ b/solution.py
@@ -2,6 +2,7 @@
 
 import jax
 import jax.numpy as jnp
+import numpy as np
 from jax import lax
 from jax.experimental import pallas as pl
 from jax.experimental.pallas import tpu as pltpu
@@ -13,13 +14,10 @@
 VMEM_LIMIT = 62 * 1024 * 1024
 
 
-def rope_tables(positions, head_dim):
+def rope_frequencies(head_dim):
     half_dim = head_dim // 2
-    inv_freq = 10000.0 ** (-jnp.arange(half_dim, dtype=jnp.float32) / half_dim)
-    angles = positions.astype(jnp.float32)[..., None] * inv_freq
-    cos_t = jnp.cos(angles)
-    sin_t = jnp.sin(angles)
-    return jnp.concatenate([cos_t, cos_t], axis=-1), jnp.concatenate([-sin_t, sin_t], axis=-1)
+    inv_freq = np.float32(10000.0) ** (-np.arange(half_dim, dtype=np.float32) / np.float32(half_dim))
+    return jnp.asarray(np.concatenate([inv_freq, inv_freq])[None, :])
 
 
 class Where:
@@ -88,7 +86,7 @@
 
 
 def layer_kernel(
-    xs, yzs, gp, len_ref, x_ref, gain_ref, wq_ref, wg_ref, wu_ref, wa_ref, wm_ref, cos_ref, sin_ref, kc_ref, vc_ref,
+    xs, yzs, gp, len_ref, x_ref, gain_ref, wq_ref, wg_ref, wu_ref, wa_ref, wm_ref, freq_ref, kc_ref, vc_ref,
     y_ref, ko_ref, vo_ref,
     act, w2v, xo, k_s, v_s, o_send, ob,
     loc_sem, xsend, xrecv, gsend, grecv, wsend, wrecv, vsend, vrecv, qsend, qrecv, osend, orecv,
@@ -128,7 +126,7 @@
 
     gather_and_attend = functools.partial(
         first_phase, xs, yzs, num_heads, at, any_peer, w2_at, o_copy, o_own, cache_writes,
-        len_ref, x_ref, gain_ref, wq_ref, wg_ref, wu_ref, wa_ref, wm_ref, cos_ref, sin_ref, kc_ref, vc_ref,
+        len_ref, x_ref, gain_ref, wq_ref, wg_ref, wu_ref, wa_ref, wm_ref, freq_ref, kc_ref, vc_ref,
         act, w2v, xo, k_s, v_s, o_send,
         loc_sem, (xsend, xrecv), (gsend, grecv), (wsend, wrecv), (vsend, vrecv), (qsend, qrecv),
     )
@@ -136,16 +134,20 @@
         gather_and_attend,
         vmem((xs, yzs, gp, rows), bf16),
         vmem((xs * yzs * gp, rows), bf16),
-        vmem((xs * yzs // 2, 2 * gp, 128), f32),
+        vmem((xs, yzs, gp, 128), f32),
         vmem((n1, xs * yzs * gp), bf16),
-        vmem((rows, c_q), bf16),
-        vmem((yzs, dev_rows, c_q), bf16),
+        vmem((yzs, dev_rows + dev_rows // 2, 128), bf16),
+        vmem((yzs, dev_rows + dev_rows // 2, 128), bf16),
         vmem((num_heads + 2, dev_rows, head_dim), f32),
         vmem((xs, gp, rows), bf16),
         vmem((gp, rows), f32),
         vmem((k_loc + 8, c_f + c_a), f32),
         vmem((yzs * gp, c_f), f32),
         vmem((c_f + c_a, k_loc), f32),
+        vmem((dev_rows, head_dim), f32),
+        vmem((dev_rows, head_dim), f32),
+        *[vmem(ref.shape, ref.dtype) for ref in (x_ref, gain_ref, wq_ref, wg_ref, wu_ref, wa_ref, wm_ref, freq_ref)],
+        dma((8,)),
     )
 
     def finish_first():
@@ -239,9 +241,10 @@
 
 def first_phase(
     xs, yzs, num_heads, at, any_peer, w2_at, o_copy, o_own, cache_writes,
-    len_ref, x_ref, gain_ref, wq_ref, wg_ref, wu_ref, wa_ref, wm_ref, cos_ref, sin_ref, kc_ref, vc_ref,
+    len_ref, x_hbm, gain_hbm, wq_hbm, wg_hbm, wu_hbm, wa_hbm, wm_hbm, freq_hbm, kc_ref, vc_ref,
     act, w2v, xo, k_s, v_s, o_send,
-    loc_sem, xsem, gsem, wsem, vsem, qsem, xg, h, gcol, w1, qkv_s, qkv_in, heads, x_send, stage, tall, wide_s, narrow,
+    loc_sem, xsem, gsem, wsem, vsem, qsem, xg, h, gcol, w1, qkv_s, qkv_in, heads, x_send, stage, tall, wide_s, narrow, cos_s, sin_s,
+    x_ref, gain_ref, wq_ref, wg_ref, wu_ref, wa_ref, wm_ref, freq_ref, in_sem,
 ):
     f32, bf16 = jnp.float32, jnp.bfloat16
     half = xs // 2
@@ -253,11 +256,17 @@
     c_f, c_a = wm_ref.shape[0], wa_ref.shape[0]
     kx = yzs * gp
     at.greet()
+    operands = ((x_hbm, x_ref), (gain_hbm, gain_ref), (wq_hbm, wq_ref), (wg_hbm, wg_ref), (wu_hbm, wu_ref), (wa_hbm, wa_ref), (wm_hbm, wm_ref), (freq_hbm, freq_ref))
+    reads = [pltpu.make_async_copy(src, dst, in_sem.at[i]) for i, (src, dst) in enumerate(operands)]
+    for read in reads:
+        read.start()
     read_k = pltpu.make_async_copy(kc_ref, k_s, loc_sem.at[4])
     read_k.start()
     read_v = pltpu.make_async_copy(vc_ref, v_s, loc_sem.at[5])
     read_v.start()
     stage[:] = jnp.zeros_like(stage)
+    for read in reads:
+        read.wait()
     stage[grp:grp + 1, :grp] = gain_ref[:].astype(f32)
     for x in range(xs):
         stage[:grp, :] = x_ref[:, x * rows:(x + 1) * rows].astype(f32)
@@ -329,6 +338,16 @@
     tall[:k_loc, :] = narrow[:].T
     for j in range(yzs):
         w2v[j, at.x] = tall[j * grp:j * grp + gp, :].astype(bf16)
+    head_dim = k_s.shape[2]
+    request = lax.broadcasted_iota(jnp.int32, (dev_rows, head_dim), 0)
+    lane = lax.broadcasted_iota(jnp.int32, (dev_rows, head_dim), 1)
+
+    def place(b, p):
+        return jnp.where(request == b, len_ref[b].astype(f32), p)
+
+    angles = lax.fori_loop(0, dev_rows, place, jnp.zeros((dev_rows, head_dim), f32), unroll=8) * freq_ref[:]
+    cos_s[:] = jnp.cos(angles)
+    sin_s[:] = jnp.where(lane < head_dim // 2, -1.0, 1.0) * jnp.sin(angles)
     for s in halves:
         rows_in(s, DOWN, 0, 0)
         pass_rows(s, DOWN, 0, first_axis, UP, FAR, 0, quarter)
@@ -342,6 +361,24 @@
         both_ways(s, FAR)
     forward_half(copies, at, w1_at, wsem)
     spread_own(late, at, w2_at, vsem)
+
+    diagonal = lax.broadcasted_iota(jnp.int32, (gp, 128), 0) == lax.broadcasted_iota(jnp.int32, (gp, 128), 1)
+    feature = lax.broadcasted_iota(jnp.int32, (gp, 1), 0)
+
+    def add_up(s, dg, sums):
+        def body(i, c):
+            x, j = s * half + i // RING, at.axis_block(order[s], i % RING, dg)
+            raw = xg[x, j].astype(f32)
+            col = jnp.sum(jnp.where(diagonal, raw[grp:grp + 1, :128], 0.0), axis=1, keepdims=True)
+            gcol[x, j] = jnp.broadcast_to(col, (gp, 128))
+            parts = jnp.where(feature < grp, raw, 0.0).reshape(gp // 8, 8, rows)
+            return c[0] + jnp.sum(parts, axis=0), c[1] + jnp.sum(parts * parts, axis=0)
+
+        return lax.fori_loop(0, half * RING, body, sums, unroll=4)
+
+    sums = (jnp.zeros((8, rows), f32), jnp.zeros((8, rows), f32))
+    for s in halves:
+        sums = add_up(s, 0, sums)
     for s in halves:
         for df in (0, DOWN):
             rows_in(s, df, DOWN, slot_up + df)
@@ -356,28 +393,17 @@
             rows_in(s, df, DOWN, slot_up + df)
         for df in (0, DOWN):
             rows_in(s, df, UP, slot_down + df)
+    for dg in (DOWN, UP):
+        for s in halves:
+            sums = add_up(s, dg, sums)
+    for s in halves:
         for df in range(RING):
             rows_in(s, df, FAR, slot_far + df)
+        sums = add_up(s, FAR, sums)
 
     pairs = yzs // 2
-    feature = lax.broadcasted_iota(jnp.int32, (2, gp, 1), 1).reshape(2 * gp, 1)
-    real = feature < grp
-    diagonal = lax.broadcasted_iota(jnp.int32, (gp, 128), 0) == lax.broadcasted_iota(jnp.int32, (gp, 128), 1)
-
-    def load(q):
-        return xg[q // pairs, pl.ds((q % pairs) * 2, 2)].astype(f32).reshape(2 * gp, rows)
-
-    def add_up(q, sums):
-        raw = load(q)
-        for k in range(2):
-            row = raw[k * gp + grp:k * gp + grp + 1, :128]
-            col = jnp.sum(jnp.where(diagonal, row, 0.0), axis=1, keepdims=True)
-            gcol[q, pl.ds(k * gp, gp), :] = jnp.broadcast_to(col, (gp, 128))
-        parts = jnp.where(real, raw, 0.0).reshape(2 * gp // 8, 8, rows)
-        return sums[0] + jnp.sum(parts, axis=0), sums[1] + jnp.sum(parts * parts, axis=0)
-
-    zero = jnp.zeros((8, rows), f32)
-    s1, s2 = lax.fori_loop(0, xs * pairs, add_up, (zero, zero), unroll=4)
+    real = lax.broadcasted_iota(jnp.int32, (2, gp, 1), 1).reshape(2 * gp, 1) < grp
+    s1, s2 = sums
     share_far(copies, at, w1_at, wsem)
     d_model = grp * xs * yzs
     mean = jnp.sum(s1, axis=0, keepdims=True) / d_model
@@ -385,8 +411,9 @@
     scale = lax.rsqrt(var + 1e-6)
 
     def normalize(q, c):
-        gain = jnp.concatenate([gcol[q]] * (rows // 128), axis=1)
-        out = jnp.where(real, (load(q) - mean) * scale * gain, 0.0)
+        at_q = q // pairs, pl.ds((q % pairs) * 2, 2)
+        gain = jnp.concatenate([gcol[at_q].reshape(2 * gp, 128)] * (rows // 128), axis=1)
+        out = jnp.where(real, (xg[at_q].astype(f32).reshape(2 * gp, rows) - mean) * scale * gain, 0.0)
         h[pl.ds(pl.multiple_of(q * 2 * gp, 16), 2 * gp), :] = out.astype(bf16)
         return c
 
@@ -397,18 +424,26 @@
 
     def query(n, c):
         q = jnp.dot(w1[:c_q], h[:, pl.ds(pl.multiple_of(n * nt, nt), nt)], preferred_element_type=f32)
-        qkv_s[pl.ds(pl.multiple_of(n * nt, nt), nt), :] = q.T.astype(bf16)
+        q = q.T
+        for i in range(nt // dev_rows):
+            piece = q[i * dev_rows:(i + 1) * dev_rows]
+            to = n * (nt // dev_rows) + i
+            qkv_s[to, :dev_rows] = piece[:, :128].astype(bf16)
+            qkv_s[to, dev_rows:] = jnp.concatenate([piece[:dev_rows // 2, 128:], piece[dev_rows // 2:, 128:]], axis=1).astype(bf16)
         return c
 
+    def unpacked(j):
+        piece = qkv_in[j].astype(f32)
+        rest = piece[dev_rows:]
+        rest = jnp.concatenate([rest[:, :c_q - 128], rest[:, c_q - 128:]], axis=0)
+        return jnp.concatenate([piece[:dev_rows], rest], axis=1)
+
     lax.fori_loop(0, rows // nt, query, 0)
-    def rows_of(ref, j):
-        return ref.at[pl.ds(pl.multiple_of(j * dev_rows, dev_rows), dev_rows)]
-
-    own_q = pltpu.make_async_copy(rows_of(qkv_s, at.j), qkv_in.at[at.j], loc_sem.at[3])
+    own_q = pltpu.make_async_copy(qkv_s.at[at.j], qkv_in.at[at.j], loc_sem.at[3])
     own_q.start()
     for d in range(1, yzs):
         to = (at.j + d) % yzs
-        send(rows_of(qkv_s, to), qkv_in.at[at.j], qsem, d - 1, at.on_yz(to))
+        send(qkv_s.at[to], qkv_in.at[at.j], qsem, d - 1, at.on_yz(to))
 
     def mlp(n, c):
         cols = pl.ds(pl.multiple_of(n * nt, nt), nt)
@@ -417,23 +452,23 @@
         act[pl.ds(0, c_f), cols] = (jax.nn.silu(gate) * up).astype(bf16)
         return c
 
+    steps = rows // nt
+    lax.fori_loop(0, steps // 2, mlp, 0)
     forward_half(late, at, w2_at, vsem)
-    steps = rows // nt
-    lax.fori_loop(0, steps - 1, mlp, 0)
+    lax.fori_loop(steps // 2, steps - 1, mlp, 0)
     for d in range(1, yzs):
         arrived(qkv_in.at[(at.j + yzs - d) % yzs], qsem, d - 1)
     own_q.wait()
     share_near(late, at, w2_at, vsem)
 
-    head_dim = k_s.shape[2]
     per = 2 * c_q // head_dim
     for p in range(yzs // 2):
-        both = jnp.concatenate([qkv_in[2 * p], qkv_in[2 * p + 1]], axis=1).astype(f32)
+        both = jnp.concatenate([unpacked(2 * p), unpacked(2 * p + 1)], axis=1)
         for i in range(per):
             hd = p * per + i
             u = both[:, i * head_dim:(i + 1) * head_dim]
             if hd <= num_heads:
-                u = u * cos_ref[:] + pltpu.roll(u, head_dim // 2, 1) * sin_ref[:]
+                u = u * cos_s[:] + pltpu.roll(u, head_dim // 2, 1) * sin_s[:]
                 u = u.astype(bf16).astype(f32)
             heads[hd] = u
     read_k.wait()
@@ -635,7 +670,7 @@
     finish_last(late)
 
 
-def layer(x_t, gain, weights, tables, k_cache, v_cache, ctx_len, xs, yzs, gp):
+def layer(x_t, gain, weights, freq, k_cache, v_cache, ctx_len, xs, yzs, gp):
     n_rows = x_t.shape[1]
     rows = n_rows // xs
     dev_rows = k_cache.shape[0]
@@ -643,13 +678,13 @@
     n2 = c_a + c_f
     dma, vmem = pltpu.SemaphoreType.DMA, pltpu.VMEM
     bf16 = jnp.bfloat16
-    vspec, aspec = pl.BlockSpec(memory_space=vmem), pl.BlockSpec(memory_space=pl.ANY)
+    aspec = pl.BlockSpec(memory_space=pl.ANY)
     sems = lambda *shape: [dma(shape), dma(shape)]
     cache = jax.ShapeDtypeStruct(k_cache.shape, bf16)
     return pl.pallas_call(
         functools.partial(layer_kernel, xs, yzs, gp),
         out_shape=(jax.ShapeDtypeStruct((gp, n_rows), bf16), cache, cache),
-        in_specs=[pl.BlockSpec(memory_space=pltpu.SMEM)] + [vspec] * 9 + [aspec] * 2,
+        in_specs=[pl.BlockSpec(memory_space=pltpu.SMEM)] + [aspec] * 10,
         out_specs=(aspec, aspec, aspec),
         scratch_shapes=[
             vmem((n2, rows), bf16),
@@ -666,7 +701,46 @@
         + [pltpu.SemaphoreType.REGULAR],
         compiler_params=pltpu.CompilerParams(collective_id=0, has_side_effects=True, vmem_limit_bytes=VMEM_LIMIT),
         name="layer",
-    )(ctx_len, x_t, gain, *weights, *tables, k_cache, v_cache)
+    )(ctx_len, x_t, gain, *weights, freq, k_cache, v_cache)
+
+
+def results_kernel(chunks, y_ref, k_ref, v_ref, yo_ref, ko_ref, vo_ref, y_in, y_out, k_s, v_s, y_sem, in_sem, out_sem):
+    n = k_s.shape[0] // chunks
+    y_read = pltpu.make_async_copy(y_ref, y_in, y_sem.at[0])
+    y_read.start()
+    copies = []
+    for c in range(chunks):
+        for i, (src, buf, dst) in enumerate(((k_ref, k_s, ko_ref), (v_ref, v_s, vo_ref))):
+            take = pl.ds(c * n, n)
+            read = pltpu.make_async_copy(src.at[take], buf.at[take], in_sem.at[i, c])
+            read.start()
+            copies.append((read, pltpu.make_async_copy(buf.at[take], dst.at[take], out_sem.at[i, c])))
+    y_read.wait()
+    y_out[:] = y_in[:y_out.shape[0], :]
+    y_write = pltpu.make_async_copy(y_out, yo_ref, y_sem.at[1])
+    y_write.start()
+    for read, write in copies:
+        read.wait()
+        write.start()
+    y_write.wait()
+    for _, write in copies:
+        write.wait()
+
+
+def results(y_t, k_all, v_all, grp):
+    chunks = 4
+    dma, vmem = pltpu.SemaphoreType.DMA, pltpu.VMEM
+    aspec = pl.BlockSpec(memory_space=pl.ANY)
+    shapes = ((grp, y_t.shape[1]), k_all.shape, v_all.shape)
+    return pl.pallas_call(
+        functools.partial(results_kernel, chunks),
+        out_shape=tuple(jax.ShapeDtypeStruct(shape, y_t.dtype) for shape in shapes),
+        in_specs=[aspec] * 3,
+        out_specs=(aspec,) * 3,
+        scratch_shapes=[vmem(shape, y_t.dtype) for shape in (y_t.shape,) + shapes] + [dma((2,)), dma((2, chunks)), dma((2, chunks))],
+        compiler_params=pltpu.CompilerParams(vmem_limit_bytes=VMEM_LIMIT),
+        name="results",
+    )(y_t, k_all, v_all)
 
 
 def solution(mesh):
@@ -682,11 +756,11 @@
     def local_layer(x_loc, gain_loc, wqkv_loc, wgate_loc, wup_loc, wao_loc, wmo_loc, kc_loc, vc_loc, len_loc):
         grp = x_loc.shape[1]
         gp = grp + -grp % 8
-        tables = rope_tables(len_loc, kc_loc.shape[2])
+        freq = rope_frequencies(kc_loc.shape[2])
         weights = (wqkv_loc.T, wgate_loc, wup_loc, wao_loc, wmo_loc)
-        y_t, k_all, v_all = layer(x_loc.T, gain_loc.reshape(1, grp), weights, tables, kc_loc, vc_loc, len_loc, xs, yzs, gp)
-        y_loc = y_t[:grp].T
-        return y_loc, k_all, v_all
+        y_t, k_all, v_all = layer(x_loc.T, gain_loc.reshape(1, grp), weights, freq, kc_loc, vc_loc, len_loc, xs, yzs, gp)
+        y_t, k_all, v_all = results(y_t, k_all, v_all, grp)
+        return y_t.T, k_all, v_all
 
     in_specs = (row_spec, P(both_axes), in_w_spec, in_w_spec, in_w_spec, out_w_spec, out_w_spec, cache_spec, cache_spec, len_spec)
     out_specs = (row_spec, cache_spec, cache_spec)

time: 162 us -> 157 us (0.969)
  local copies, waits for them, and re-layouts: 6.4 us -> 0 us
  Pallas kernels: 152 us -> 156 us
    unnamed x4 -> x0, local copies, waits for them, and re-layouts: 4.63 us -> none
    pallas_call x0 -> x1, Pallas kernels: none -> 4.41 us  [results(): pl.pallas_call(functools.partial(results_kernel, chunks), out_shape=tuple...]
    transpose x1 -> x0, local copies, waits for them, and re-layouts: 1.77 us -> none  [local_layer(): y_loc = y_t[:grp].T]
where the time goes in v7:
time: 157 us; the launch traced here: 156 us
  Pallas kernels  156 us (99%)
    pallas_call x1, Pallas kernels, layer(): pl.pallas_call(functools.partial(layer_kernel, xs, yzs, gp), out_shape=(j...  151 us
    pallas_call x1, Pallas kernels, results(): pl.pallas_call(functools.partial(results_kernel, chunks), out_shape=tuple...  4.41 us

profile of v7, /device:TPU:1, one launch (start us, length us, event | category | flops | bytes accessed | tf_op | source)
XLA Modules:
  0.0 156.5 jit_solution(13561160888027983731)
XLA Ops:
  0.6 151.4 %layer.1 = (bf16[24,8192]{1,0:T(8,128)(2,1)}, bf16[64,128,128]{2,1,0:T(8,128)(2,1)}, bf16[64,128,128]{2,1,0:T(8,128)(2,1)}) custom-call(s32[64]{0:T(128)} %len_ref.1, bf16[22,8192]{1,0:T(8,128)(2,1)} %bitcast.4, bf16[1,22]{1,0:T(2,128)(2,1)} %bitcast.6, bf16[192,352]{1,0:T(8,128)(2,1)} %bitcast.5, bf16[352,704]{1,0:T(8,128)(2,1)} %wg_ref.1, ...), custom_call_target="tpu_custom_call" | custom-call | tf_op jit(solution)/shard_map/layer/pallas_call | solution.py:684
  152.1 4.4 %results.1 = (bf16[22,8192]{1,0:T(8,128)(2,1)}, bf16[64,128,128]{2,1,0:T(8,128)(2,1)}, bf16[64,128,128]{2,1,0:T(8,128)(2,1)}) custom-call(bf16[24,8192]{1,0:T(8,128)(2,1)} %get-tuple-element.9.y_ref, bf16[64,128,128]{2,1,0:T(8,128)(2,1)} %get-tuple-element.10.k_ref, bf16[64,128,128]{2,1,0:T(8,128)(2,1)} %get-tuple-element.11.v_ref), custom_call_target="tpu_custom_call" | custom-call | tf_op jit(solution)/shard_map/results/pallas_call | solution.py:735

commit v8 on v7

--- a/solution.py
+++ b/solution.py
@@ -136,8 +136,8 @@
         vmem((xs * yzs * gp, rows), bf16),
         vmem((xs, yzs, gp, 128), f32),
         vmem((n1, xs * yzs * gp), bf16),
-        vmem((yzs, dev_rows + dev_rows // 2, 128), bf16),
-        vmem((yzs, dev_rows + dev_rows // 2, 128), bf16),
+        vmem((2, yzs, part + part // 2, 128), bf16),
+        vmem((2, yzs, part + part // 2, 128), bf16),
         vmem((num_heads + 2, dev_rows, head_dim), f32),
         vmem((xs, gp, rows), bf16),
         vmem((gp, rows), f32),
@@ -147,7 +147,8 @@
         vmem((dev_rows, head_dim), f32),
         vmem((dev_rows, head_dim), f32),
         *[vmem(ref.shape, ref.dtype) for ref in (x_ref, gain_ref, wq_ref, wg_ref, wu_ref, wa_ref, wm_ref, freq_ref)],
-        dma((8,)),
+        pltpu.SMEM(len_ref.shape, len_ref.dtype),
+        dma((9,)),
     )
 
     def finish_first():
@@ -241,10 +242,10 @@
 
 def first_phase(
     xs, yzs, num_heads, at, any_peer, w2_at, o_copy, o_own, cache_writes,
-    len_ref, x_hbm, gain_hbm, wq_hbm, wg_hbm, wu_hbm, wa_hbm, wm_hbm, freq_hbm, kc_ref, vc_ref,
+    len_hbm, x_hbm, gain_hbm, wq_hbm, wg_hbm, wu_hbm, wa_hbm, wm_hbm, freq_hbm, kc_ref, vc_ref,
     act, w2v, xo, k_s, v_s, o_send,
     loc_sem, xsem, gsem, wsem, vsem, qsem, xg, h, gcol, w1, qkv_s, qkv_in, heads, x_send, stage, tall, wide_s, narrow, cos_s, sin_s,
-    x_ref, gain_ref, wq_ref, wg_ref, wu_ref, wa_ref, wm_ref, freq_ref, in_sem,
+    x_ref, gain_ref, wq_ref, wg_ref, wu_ref, wa_ref, wm_ref, freq_ref, len_ref, in_sem,
 ):
     f32, bf16 = jnp.float32, jnp.bfloat16
     half = xs // 2
@@ -256,7 +257,7 @@
     c_f, c_a = wm_ref.shape[0], wa_ref.shape[0]
     kx = yzs * gp
     at.greet()
-    operands = ((x_hbm, x_ref), (gain_hbm, gain_ref), (wq_hbm, wq_ref), (wg_hbm, wg_ref), (wu_hbm, wu_ref), (wa_hbm, wa_ref), (wm_hbm, wm_ref), (freq_hbm, freq_ref))
+    operands = ((x_hbm, x_ref), (gain_hbm, gain_ref), (wq_hbm, wq_ref), (wg_hbm, wg_ref), (wu_hbm, wu_ref), (wa_hbm, wa_ref), (wm_hbm, wm_ref), (freq_hbm, freq_ref), (len_hbm, len_ref))
     reads = [pltpu.make_async_copy(src, dst, in_sem.at[i]) for i, (src, dst) in enumerate(operands)]
     for read in reads:
         read.start()
@@ -265,12 +266,9 @@
     read_v = pltpu.make_async_copy(vc_ref, v_s, loc_sem.at[5])
     read_v.start()
     stage[:] = jnp.zeros_like(stage)
-    for read in reads:
+    for read in reads[:2]:
         read.wait()
     stage[grp:grp + 1, :grp] = gain_ref[:].astype(f32)
-    for x in range(xs):
-        stage[:grp, :] = x_ref[:, x * rows:(x + 1) * rows].astype(f32)
-        x_send[x] = stage[:].astype(bf16)
     at.greeted()
     copies, late = Copies(any_peer), Copies(any_peer)
 
@@ -280,11 +278,16 @@
     def arrived(region, sems, idx):
         copies.arrived(region, sems[0].at[idx], sems[1].at[idx])
 
+    for d in (*range(1, xs), 0):
+        to = (at.x + d) % xs
+        stage[:grp, :] = x_ref[:, pl.ds(pl.multiple_of(to * rows, 128), rows)].astype(f32)
+        x_send[to] = stage[:].astype(bf16)
+        if d:
+            send(x_send.at[to], xg.at[at.x, at.j], xsem, d - 1, at.on_x(to))
     own_x = pltpu.make_async_copy(x_send.at[at.x], xg.at[at.x, at.j], loc_sem.at[0])
     own_x.start()
-    for d in range(1, xs):
-        to = (at.x + d) % xs
-        send(x_send.at[to], xg.at[at.x, at.j], xsem, d - 1, at.on_x(to))
+    for read in reads[2:]:
+        read.wait()
 
     n1 = w1.shape[0]
 
@@ -404,7 +407,6 @@
     pairs = yzs // 2
     real = lax.broadcasted_iota(jnp.int32, (2, gp, 1), 1).reshape(2 * gp, 1) < grp
     s1, s2 = sums
-    share_far(copies, at, w1_at, wsem)
     d_model = grp * xs * yzs
     mean = jnp.sum(s1, axis=0, keepdims=True) / d_model
     var = jnp.sum(s2, axis=0, keepdims=True) / d_model - mean * mean
@@ -417,7 +419,10 @@
         h[pl.ds(pl.multiple_of(q * 2 * gp, 16), 2 * gp), :] = out.astype(bf16)
         return c
 
-    lax.fori_loop(0, xs * pairs, normalize, 0, unroll=2)
+    some = xs * pairs // 2
+    lax.fori_loop(0, some, normalize, 0, unroll=2)
+    share_far(copies, at, w1_at, wsem)
+    lax.fori_loop(some, xs * pairs, normalize, 0, unroll=2)
     all_in(copies, at, w1_at, wsem)
 
     nt = 256
@@ -426,24 +431,29 @@
         q = jnp.dot(w1[:c_q], h[:, pl.ds(pl.multiple_of(n * nt, nt), nt)], preferred_element_type=f32)
         q = q.T
         for i in range(nt // dev_rows):
-            piece = q[i * dev_rows:(i + 1) * dev_rows]
             to = n * (nt // dev_rows) + i
-            qkv_s[to, :dev_rows] = piece[:, :128].astype(bf16)
-            qkv_s[to, dev_rows:] = jnp.concatenate([piece[:dev_rows // 2, 128:], piece[dev_rows // 2:, 128:]], axis=1).astype(bf16)
+            for k in range(2):
+                piece = q[i * dev_rows + k * part:i * dev_rows + (k + 1) * part]
+                qkv_s[k, to, :part] = piece[:, :128].astype(bf16)
+                qkv_s[k, to, part:] = jnp.concatenate([piece[:part // 2, 128:], piece[part // 2:, 128:]], axis=1).astype(bf16)
         return c
 
-    def unpacked(j):
-        piece = qkv_in[j].astype(f32)
-        rest = piece[dev_rows:]
+    def unpacked(k, j):
+        piece = qkv_in[k, j].astype(f32)
+        rest = piece[part:]
         rest = jnp.concatenate([rest[:, :c_q - 128], rest[:, c_q - 128:]], axis=0)
-        return jnp.concatenate([piece[:dev_rows], rest], axis=1)
-
+        return jnp.concatenate([piece[:part], rest], axis=1)
+
+    part = dev_rows // 2
     lax.fori_loop(0, rows // nt, query, 0)
-    own_q = pltpu.make_async_copy(qkv_s.at[at.j], qkv_in.at[at.j], loc_sem.at[3])
-    own_q.start()
-    for d in range(1, yzs):
-        to = (at.j + d) % yzs
-        send(qkv_s.at[to], qkv_in.at[at.j], qsem, d - 1, at.on_yz(to))
+    own_q = []
+    for k in range(2):
+        own = pltpu.make_async_copy(qkv_s.at[k, at.j], qkv_in.at[k, at.j], loc_sem.at[2 + k])
+        own.start()
+        own_q.append(own)
+        for d in range(1, yzs):
+            to = (at.j + d) % yzs
+            send(qkv_s.at[k, to], qkv_in.at[k, at.j], (qsem[0].at[k], qsem[1].at[k]), d - 1, at.on_yz(to))
 
     def mlp(n, c):
         cols = pl.ds(pl.multiple_of(n * nt, nt), nt)
@@ -455,24 +465,20 @@
     steps = rows // nt
     lax.fori_loop(0, steps // 2, mlp, 0)
     forward_half(late, at, w2_at, vsem)
-    lax.fori_loop(steps // 2, steps - 1, mlp, 0)
-    for d in range(1, yzs):
-        arrived(qkv_in.at[(at.j + yzs - d) % yzs], qsem, d - 1)
-    own_q.wait()
-    share_near(late, at, w2_at, vsem)
 
     per = 2 * c_q // head_dim
-    for p in range(yzs // 2):
-        both = jnp.concatenate([unpacked(2 * p), unpacked(2 * p + 1)], axis=1)
-        for i in range(per):
-            hd = p * per + i
-            u = both[:, i * head_dim:(i + 1) * head_dim]
-            if hd <= num_heads:
-                u = u * cos_s[:] + pltpu.roll(u, head_dim // 2, 1) * sin_s[:]
-                u = u.astype(bf16).astype(f32)
-            heads[hd] = u
-    read_k.wait()
-    read_v.wait()
+
+    def rotate(k):
+        take = pl.ds(k * part, part)
+        for p in range(yzs // 2):
+            both = jnp.concatenate([unpacked(k, 2 * p), unpacked(k, 2 * p + 1)], axis=1)
+            for i in range(per):
+                hd = p * per + i
+                u = both[:, i * head_dim:(i + 1) * head_dim]
+                if hd <= num_heads:
+                    u = u * cos_s[take, :] + pltpu.roll(u, head_dim // 2, 1) * sin_s[take, :]
+                    u = u.astype(bf16).astype(f32)
+                heads[hd, take, :] = u
 
     group = 8
     t_len = k_s.shape[1]
@@ -507,8 +513,13 @@
         heads[:, pl.ds(first, group), :] = jnp.swapaxes(jnp.stack(outs, axis=0), 0, 1)
         return c
 
-    part = dev_rows // 2
+    read_k.wait()
+    read_v.wait()
     for k in range(2):
+        for d in range(1, yzs):
+            arrived(qkv_in.at[k, (at.j + yzs - d) % yzs], (qsem[0].at[k], qsem[1].at[k]), d - 1)
+        own_q[k].wait()
+        rotate(k)
         lax.fori_loop(k * part // group, (k + 1) * part // group, attend, 0)
         take = pl.ds(k * part, part)
         for jj in range(yzs):
@@ -521,7 +532,8 @@
             o_copy(k, d).start()
     for write in cache_writes():
         write.start()
-    lax.fori_loop(steps - 1, steps, mlp, 0)
+    share_near(late, at, w2_at, vsem)
+    lax.fori_loop(steps // 2, steps, mlp, 0)
     copies.finish()
 
 
@@ -684,7 +696,7 @@
     return pl.pallas_call(
         functools.partial(layer_kernel, xs, yzs, gp),
         out_shape=(jax.ShapeDtypeStruct((gp, n_rows), bf16), cache, cache),
-        in_specs=[pl.BlockSpec(memory_space=pltpu.SMEM)] + [aspec] * 10,
+        in_specs=[aspec] * 11,
         out_specs=(aspec, aspec, aspec),
         scratch_shapes=[
             vmem((n2, rows), bf16),
@@ -696,7 +708,7 @@
             vmem((rows, c_a), bf16),
             dma((8,)),
         ]
-        + sems(xs - 1) + sems(2, RING * RING) + sems(11) + sems(11) + sems(yzs - 1) + sems(2, yzs - 1)
+        + sems(xs - 1) + sems(2, RING * RING) + sems(11) + sems(11) + sems(2, yzs - 1) + sems(2, yzs - 1)
         + sems(2, RING) + sems(2, 2, RING) + sems(2, 2) + sems(2, 2, 2) + sems(xs - 1)
         + [pltpu.SemaphoreType.REGULAR],
         compiler_params=pltpu.CompilerParams(collective_id=0, has_side_effects=True, vmem_limit_bytes=VMEM_LIMIT),

time: 157 us -> 155 us (0.987)
  Pallas kernels: 156 us -> 154 us
    pallas_call x1, Pallas kernels: 151 us -> 150 us  [layer(): pl.pallas_call(functools.partial(layer_kernel, xs, yzs, gp), out_shape=(j...]
where the time goes in v8:
time: 155 us
  Pallas kernels  154 us (99%)
    pallas_call x1, Pallas kernels, layer(): pl.pallas_call(functools.partial(layer_kernel, xs, yzs, gp), out_shape=(j...  150 us
    pallas_call x1, Pallas kernels, results(): pl.pallas_call(functools.partial(results_kernel, chunks), out_shape=tuple...  4.41 us

profile of v8, /device:TPU:1, one launch (start us, length us, event | category | flops | bytes accessed | tf_op | source)
XLA Modules:
  0.0 154.6 jit_solution(13926448385106026946)
XLA Ops:
  0.6 149.5 %layer.1 = (bf16[24,8192]{1,0:T(8,128)(2,1)}, bf16[64,128,128]{2,1,0:T(8,128)(2,1)}, bf16[64,128,128]{2,1,0:T(8,128)(2,1)}) custom-call(s32[64]{0:T(128)} %len_ref.1, bf16[22,8192]{1,0:T(8,128)(2,1)} %bitcast.4, bf16[1,22]{1,0:T(2,128)(2,1)} %bitcast.6, bf16[192,352]{1,0:T(8,128)(2,1)} %bitcast.5, bf16[352,704]{1,0:T(8,128)(2,1)} %wg_ref.1, ...), custom_call_target="tpu_custom_call" | custom-call | tf_op jit(solution)/shard_map/layer/pallas_call | solution.py:696
  150.2 4.4 %results.1 = (bf16[22,8192]{1,0:T(8,128)(2,1)}, bf16[64,128,128]{2,1,0:T(8,128)(2,1)}, bf16[64,128,128]{2,1,0:T(8,128)(2,1)}) custom-call(bf16[24,8192]{1,0:T(8,128)(2,1)} %get-tuple-element.9.y_ref, bf16[64,128,128]{2,1,0:T(8,128)(2,1)} %get-tuple-element.10.k_ref, bf16[64,128,128]{2,1,0:T(8,128)(2,1)} %get-tuple-element.11.v_ref), custom_call_target="tpu_custom_call" | custom-call | tf_op jit(solution)/shard_map/results/pallas_call | solution.py:747

commit v9 on v8

--- a/solution.py
+++ b/solution.py
@@ -80,6 +80,9 @@
             src_ref=dst, dst_ref=dst, send_sem=ssem, recv_sem=rsem, device_id=self.any_peer, device_id_type=MESH
         ).wait_recv()
 
+    def sent(self, src, ssem, rsem):
+        remote(src, src, ssem, rsem, self.any_peer).wait_send()
+
     def finish(self):
         for copy in self.started:
             copy.wait_send()
@@ -90,7 +93,7 @@
     y_ref, ko_ref, vo_ref,
     act, w2v, xo, k_s, v_s, o_send, ob,
     loc_sem, xsend, xrecv, gsend, grecv, wsend, wrecv, vsend, vrecv, qsend, qrecv, osend, orecv,
-    s1, q1, s2, q2, s3, q3, s4, q4, ys, yq, ready,
+    ys, yq, ready,
 ):
     f32, bf16 = jnp.float32, jnp.bfloat16
     dma, vmem = pltpu.SemaphoreType.DMA, pltpu.VMEM
@@ -116,7 +119,7 @@
 
     def o_copy(k, d):
         to = (at.j + d) % yzs
-        return remote(o_send.at[k, to], o_rows(at.j, k), osend.at[k, d - 1], orecv.at[k, d - 1], at.on_yz(to))
+        return remote(o_send.at[k, to], o_rows(at.j, k), osend.at[k], orecv.at[k], at.on_yz(to))
 
     def o_own(k):
         return pltpu.make_async_copy(o_send.at[k, at.j], o_rows(at.j, k), loc_sem.at[6 + k])
@@ -155,8 +158,7 @@
         late = Copies(any_peer)
         share_far(late, at, w2_at, (vsend, vrecv))
         for k in range(2):
-            for d in range(1, yzs):
-                late.arrived(o_rows((at.j + yzs - d) % yzs, k), osend.at[k, d - 1], orecv.at[k, d - 1])
+            late.arrived(ob.at[pl.ds(0, (yzs - 1) * part)], osend.at[k], orecv.at[k])
             o_own(k).wait()
         act[pl.ds(c_f, c_a), :] = ob[:].T
         all_in(late, at, w2_at, (vsend, vrecv))
@@ -166,8 +168,7 @@
         for write in cache_writes():
             write.wait()
         for k in range(2):
-            for d in range(1, yzs):
-                o_copy(k, d).wait_send()
+            late.sent(o_send.at[k, pl.ds(0, yzs - 1)], osend.at[k], orecv.at[k])
         for slot in range(9):
             r = w2_at(at.x, None if slot in (4, 7, 8) else 0)
             remote(r, r, vsend.at[slot], vrecv.at[slot], any_peer).wait_send()
@@ -175,7 +176,7 @@
 
     sum_and_return = functools.partial(
         second_phase, xs, yzs, grp, at, any_peer, finish_first, finish_last, w2v, act, xo, y_ref,
-        loc_sem, (s1, q1), (s2, q2), (s3, q3), (s4, q4), (ys, yq), ready,
+        loc_sem, (gsend, grecv), (ys, yq), ready,
     )
     big = hr // 2 + hr // 2 % 8
     pl.run_scoped(
@@ -283,7 +284,7 @@
         stage[:grp, :] = x_ref[:, pl.ds(pl.multiple_of(to * rows, 128), rows)].astype(f32)
         x_send[to] = stage[:].astype(bf16)
         if d:
-            send(x_send.at[to], xg.at[at.x, at.j], xsem, d - 1, at.on_x(to))
+            remote(x_send.at[to], xg.at[at.x, at.j], xsem[0].at[0], xsem[1].at[0], at.on_x(to)).start()
     own_x = pltpu.make_async_copy(x_send.at[at.x], xg.at[at.x, at.j], loc_sem.at[0])
     own_x.start()
     for read in reads[2:]:
@@ -309,8 +310,8 @@
         row += n
     spread_own(copies, at, w1_at, wsem)
     own_x.wait()
-    for d in range(1, xs):
-        arrived(xg.at[(at.x + xs - d) % xs, at.j], xsem, d - 1)
+    arrived(xg.at[pl.ds(0, xs - 1), at.j], xsem, 0)
+    copies.sent(x_send.at[pl.ds(0, xs - 1)], xsem[0].at[0], xsem[1].at[0])
 
     order = ("y", "z")
     halves = range(len(order))
@@ -453,7 +454,7 @@
         own_q.append(own)
         for d in range(1, yzs):
             to = (at.j + d) % yzs
-            send(qkv_s.at[k, to], qkv_in.at[k, at.j], (qsem[0].at[k], qsem[1].at[k]), d - 1, at.on_yz(to))
+            remote(qkv_s.at[k, to], qkv_in.at[k, at.j], qsem[0].at[k], qsem[1].at[k], at.on_yz(to)).start()
 
     def mlp(n, c):
         cols = pl.ds(pl.multiple_of(n * nt, nt), nt)
@@ -516,8 +517,8 @@
     read_k.wait()
     read_v.wait()
     for k in range(2):
-        for d in range(1, yzs):
-            arrived(qkv_in.at[k, (at.j + yzs - d) % yzs], (qsem[0].at[k], qsem[1].at[k]), d - 1)
+        arrived(qkv_in.at[k, pl.ds(0, yzs - 1)], qsem, k)
+        copies.sent(qkv_s.at[k, pl.ds(0, yzs - 1)], qsem[0].at[k], qsem[1].at[k])
         own_q[k].wait()
         rotate(k)
         lax.fori_loop(k * part // group, (k + 1) * part // group, attend, 0)
@@ -539,14 +540,27 @@
 
 def second_phase(
     xs, yzs, grp, at, any_peer, finish_first, finish_last, w2v, act, xo, y_ref,
-    loc_sem, sem1, sem2, sem3, sem4, ysem, ready, zb, r1, r2, r3, r4, yv, ws,
+    loc_sem, gsem, ysem, ready, zb, r1, r2, r3, r4, yv, ws,
 ):
     for d in (UP, DOWN):
         for peer in (at.block(d, 0), at.block(0, d)):
             pl.semaphore_signal(ready, inc=1, device_id=at.on_yz(peer), device_id_type=MESH)
     yv[:] = jnp.zeros_like(yv)
     late = finish_first()
-    (s1, q1), (s2, q2), (s3, q3), (s4, q4), (ys, yq) = sem1, sem2, sem3, sem4, ysem
+    ys, yq = ysem
+
+    def pair1(h, dg):
+        return gsem[0].at[h, dg], gsem[1].at[h, dg]
+
+    def pair2(h, s, dg):
+        return pair1(h, RING + RING * s + dg)
+
+    def pair3(h, k):
+        return pair1(h, 3 * RING + k)
+
+    def pair4(h, s, k):
+        return pair1(h, 3 * RING + 2 + 2 * s + k)
+
     order = ("z", "y")
     hr = zb.shape[2] // 2
     copies = Copies(any_peer)
@@ -564,7 +578,7 @@
 
     def send1(h, dg):
         d = 1 if dg < 2 else 3
-        send(zat(h, 2, dg), r1.at[h, dg], s1.at[h, dg], q1.at[h, dg], at.step(order[h], 0, d))
+        send(zat(h, 2, dg), r1.at[h, dg], *pair1(h, dg), at.step(order[h], 0, d))
 
     compute(2, 2)
     pl.semaphore_wait(ready, RING)
@@ -585,7 +599,7 @@
 
     def send2(h, up, dg):
         df, d, s = (1, 1, 0) if up else (3, 3, 1)
-        send(zat(h, df, dg), r2.at[h, s, dg], s2.at[h, s, dg], q2.at[h, s, dg], at.step(order[h], 0, d))
+        send(zat(h, df, dg), r2.at[h, s, dg], *pair2(h, s, dg), at.step(order[h], 0, d))
 
     for h in range(2):
         for dg in (2, 3):
@@ -596,14 +610,14 @@
         for h in range(2):
             for up in (True, False):
                 dg = 1 - k if up else 2 + k
-                arrived(r1.at[h, dg], s1.at[h, dg], q1.at[h, dg])
+                arrived(r1.at[h, dg], *pair1(h, dg))
                 ref = zat(h, 1 if up else 3, dg)
                 ref[:] = ref[:] + r1[h, dg]
                 send2(h, up, dg)
 
     def plane(h, dg):
         for s in range(2):
-            arrived(r2.at[h, s, dg], s2.at[h, s, dg], q2.at[h, s, dg])
+            arrived(r2.at[h, s, dg], *pair2(h, s, dg))
         ref = zat(h, 0, dg)
         ref[:] = ref[:] + r2[h, 0, dg] + r2[h, 1, dg]
 
@@ -622,12 +636,12 @@
 
     def send4(h, up, k):
         dg, d, s = (1, 1, 0) if up else (3, 3, 1)
-        send(part(h, dg, k), r4_at(h, s, k), s4.at[h, s, k], q4.at[h, s, k], at.step(order[h], 1, d))
+        send(part(h, dg, k), r4_at(h, s, k), *pair4(h, s, k), at.step(order[h], 1, d))
 
     for h in range(2):
         plane(h, 2)
-        send(part(h, 2, 0), r3_at(h, 0), s3.at[h, 0], q3.at[h, 0], at.step(order[h], 1, 1))
-        send(part(h, 2, 1), r3_at(h, 1), s3.at[h, 1], q3.at[h, 1], at.step(order[h], 1, 3))
+        send(part(h, 2, 0), r3_at(h, 0), *pair3(h, 0), at.step(order[h], 1, 1))
+        send(part(h, 2, 1), r3_at(h, 1), *pair3(h, 1), at.step(order[h], 1, 3))
     for h in range(2):
         plane(h, 1)
         send4(h, True, 1)
@@ -636,11 +650,11 @@
     for h in range(2):
         plane(h, 0)
     for h in range(2):
-        arrived(r3_at(h, 0), s3.at[h, 0], q3.at[h, 0])
+        arrived(r3_at(h, 0), *pair3(h, 0))
         ref = part(h, 1, 0)
         ref[:] = ref[:] + r3_at(h, 0)[:]
         send4(h, True, 0)
-        arrived(r3_at(h, 1), s3.at[h, 1], q3.at[h, 1])
+        arrived(r3_at(h, 1), *pair3(h, 1))
         ref = part(h, 3, 1)
         ref[:] = ref[:] + r3_at(h, 1)[:]
         send4(h, False, 1)
@@ -648,15 +662,15 @@
         rows = yv.shape[2]
         return y_ref.at[:, pl.ds(pl.multiple_of(x * rows, 128), rows)]
 
-    def y_copy(x, d):
+    def y_copy(x):
         return pltpu.make_async_remote_copy(
-            src_ref=yv.at[x], dst_ref=y_cols(at.x), send_sem=ys.at[d - 1], recv_sem=yq.at[d - 1], device_id=at.on_x(x), device_id_type=MESH
+            src_ref=yv.at[x], dst_ref=y_cols(at.x), send_sem=ys.at[0], recv_sem=yq.at[0], device_id=at.on_x(x), device_id_type=MESH
         )
 
     for h in range(2):
         for k in range(2):
             for s in range(2):
-                arrived(r4_at(h, s, k), s4.at[h, s, k], q4.at[h, s, k])
+                arrived(r4_at(h, s, k), *pair4(h, s, k))
             ref = part(h, 0, k)
             ref[:] = ref[:] + r4_at(h, 0, k)[:] + r4_at(h, 1, k)[:]
             done = xs // 4
@@ -671,13 +685,11 @@
 
                 @pl.when(d != 0)
                 def _():
-                    y_copy(x, d).start()
-
-    for d in range(1, xs):
-        arrived(y_cols((at.x + xs - d) % xs), ys.at[d - 1], yq.at[d - 1])
+                    y_copy(x).start()
+
+    arrived(y_ref.at[:, pl.ds(0, (xs - 1) * yv.shape[2])], ys.at[0], yq.at[0])
     pltpu.make_async_copy(yv.at[at.x], y_cols(at.x), loc_sem.at[3]).wait()
-    for d in range(1, xs):
-        y_copy((at.x + d) % xs, d).wait_send()
+    copies.sent(yv.at[pl.ds(0, xs - 1)], ys.at[0], yq.at[0])
     copies.finish()
     finish_last(late)
 
@@ -708,8 +720,7 @@
             vmem((rows, c_a), bf16),
             dma((8,)),
         ]
-        + sems(xs - 1) + sems(2, RING * RING) + sems(11) + sems(11) + sems(2, yzs - 1) + sems(2, yzs - 1)
-        + sems(2, RING) + sems(2, 2, RING) + sems(2, 2) + sems(2, 2, 2) + sems(xs - 1)
+        + sems(1) + sems(2, RING * RING + 2) + sems(11) + sems(11) + sems(2) + sems(2) + sems(1)
         + [pltpu.SemaphoreType.REGULAR],
         compiler_params=pltpu.CompilerParams(collective_id=0, has_side_effects=True, vmem_limit_bytes=VMEM_LIMIT),
         name="layer",

time: 155 us -> 153 us (0.987)
  Pallas kernels: 154 us -> 152 us
    pallas_call x1, Pallas kernels: 150 us -> 148 us  [layer(): pl.pallas_call(functools.partial(layer_kernel, xs, yzs, gp), out_shape=(j...]
where the time goes in v9:
time: 153 us
  Pallas kernels  152 us (99%)
    pallas_call x1, Pallas kernels, layer(): pl.pallas_call(functools.partial(layer_kernel, xs, yzs, gp), out_shape=(j...  148 us
    pallas_call x1, Pallas kernels, results(): pl.pallas_call(functools.partial(results_kernel, chunks), out_shape=tuple...  4.41 us

profile of v9, /device:TPU:1, one launch (start us, length us, event | category | flops | bytes accessed | tf_op | source)
XLA Modules:
  0.0 152.6 jit_solution(10961196615681137792)
XLA Ops:
  0.6 147.6 %layer.1 = (bf16[24,8192]{1,0:T(8,128)(2,1)}, bf16[64,128,128]{2,1,0:T(8,128)(2,1)}, bf16[64,128,128]{2,1,0:T(8,128)(2,1)}) custom-call(s32[64]{0:T(128)} %len_ref.1, bf16[22,8192]{1,0:T(8,128)(2,1)} %bitcast.4, bf16[1,22]{1,0:T(2,128)(2,1)} %bitcast.6, bf16[192,352]{1,0:T(8,128)(2,1)} %bitcast.5, bf16[352,704]{1,0:T(8,128)(2,1)} %wg_ref.1, ...), custom_call_target="tpu_custom_call" | custom-call | tf_op jit(solution)/shard_map/layer/pallas_call | solution.py:708
  148.2 4.4 %results.1 = (bf16[22,8192]{1,0:T(8,128)(2,1)}, bf16[64,128,128]{2,1,0:T(8,128)(2,1)}, bf16[64,128,128]{2,1,0:T(8,128)(2,1)}) custom-call(bf16[24,8192]{1,0:T(8,128)(2,1)} %get-tuple-element.9.y_ref, bf16[64,128,128]{2,1,0:T(8,128)(2,1)} %get-tuple-element.10.k_ref, bf16[64,128,128]{2,1,0:T(8,128)(2,1)} %get-tuple-element.11.v_ref), custom_call_target="tpu_custom_call" | custom-call | tf_op jit(solution)/shard_map/results/pallas_call | solution.py:758

commit v10 on v9

--- a/solution.py
+++ b/solution.py
@@ -111,8 +111,7 @@
     any_peer = at.on_yz(at.block(0, UP))
 
     def w2_at(x, k=None):
-        n2 = w2v.shape[0]
-        return w2v.at[:, x] if k is None else w2v.at[pl.ds(k * (n2 // 2), n2 // 2), x]
+        return w2v.at[x, pl.ds(0, k_loc)] if k is None else w2v.at[x, pl.ds(k * (k_loc // 2), k_loc // 2)]
 
     def o_rows(j, k):
         return ob.at[pl.ds(pl.multiple_of(j * dev_rows + k * part, part), part)]
@@ -187,7 +186,7 @@
         vmem((2, 2, big, rows), f32),
         vmem((2, 2, 2, big, rows), f32),
         vmem((xs, gp, rows), bf16),
-        vmem((block, w2v.shape[3]), f32),
+        vmem((block, w2v.shape[2]), f32),
     )
 
 
@@ -340,8 +339,7 @@
     narrow[:c_f, :] = wm_ref[:].astype(f32)
     narrow[c_f:, :] = wa_ref[:].astype(f32)
     tall[:k_loc, :] = narrow[:].T
-    for j in range(yzs):
-        w2v[j, at.x] = tall[j * grp:j * grp + gp, :].astype(bf16)
+    w2v[at.x, :k_loc] = tall[:k_loc, :].astype(bf16)
     head_dim = k_s.shape[2]
     request = lax.broadcasted_iota(jnp.int32, (dev_rows, head_dim), 0)
     lane = lax.broadcasted_iota(jnp.int32, (dev_rows, head_dim), 1)
@@ -571,9 +569,12 @@
         return zb.at[dz, dy, pl.ds(h * hr, hr)]
 
     def compute(dz, dy):
-        w = w2v[at.block(dz, dy)].astype(jnp.float32)
+        start = at.block(dz, dy) * grp
+        base = start // 16 * 16
+        span = 48
         for x in range(xs):
-            ws[pl.ds(x * grp, grp), :] = w[x, :grp]
+            w = w2v[x, pl.ds(pl.multiple_of(base, 16), span), :].astype(jnp.float32)
+            ws[pl.ds(x * grp, grp), :] = pltpu.roll(w, span - (start - base), 0)[:grp]
         zb[dz, dy] = jnp.dot(ws[:].astype(jnp.bfloat16), act[:], preferred_element_type=jnp.float32)
 
     def send1(h, dg):
@@ -700,6 +701,7 @@
     dev_rows = k_cache.shape[0]
     c_a, c_f = weights[3].shape[0], weights[4].shape[0]
     n2 = c_a + c_f
+    grp = x_t.shape[0]
     dma, vmem = pltpu.SemaphoreType.DMA, pltpu.VMEM
     bf16 = jnp.bfloat16
     aspec = pl.BlockSpec(memory_space=pl.ANY)
@@ -712,7 +714,7 @@
         out_specs=(aspec, aspec, aspec),
         scratch_shapes=[
             vmem((n2, rows), bf16),
-            vmem((yzs, xs, gp, n2), bf16),
+            vmem((xs, yzs * grp + 16, n2), bf16),
             vmem((xs, gp, rows), bf16),
             vmem(k_cache.shape, bf16),
             vmem(k_cache.shape, bf16),

time: 153 us -> 153 us (level)
  no operation moved by 1% of the time
where the time goes in v10:
time: 153 us
  Pallas kernels  153 us (100%)
    pallas_call x1, Pallas kernels, layer(): pl.pallas_call(functools.partial(layer_kernel, xs, yzs, gp), out_shape=(j...  148 us
    pallas_call x1, Pallas kernels, results(): pl.pallas_call(functools.partial(results_kernel, chunks), out_shape=tuple...  4.41 us

profile of v10, /device:TPU:1, one launch (start us, length us, event | category | flops | bytes accessed | tf_op | source)
XLA Modules:
  0.0 153.3 jit_solution(7089583902572814759)
XLA Ops:
  0.6 148.2 %layer.1 = (bf16[24,8192]{1,0:T(8,128)(2,1)}, bf16[64,128,128]{2,1,0:T(8,128)(2,1)}, bf16[64,128,128]{2,1,0:T(8,128)(2,1)}) custom-call(s32[64]{0:T(128)} %len_ref.1, bf16[22,8192]{1,0:T(8,128)(2,1)} %bitcast.4, bf16[1,22]{1,0:T(2,128)(2,1)} %bitcast.6, bf16[192,352]{1,0:T(8,128)(2,1)} %bitcast.5, bf16[352,704]{1,0:T(8,128)(2,1)} %wg_ref.1, ...), custom_call_target="tpu_custom_call" | custom-call | tf_op jit(solution)/shard_map/layer/pallas_call | solution.py:710
  148.9 4.4 %results.1 = (bf16[22,8192]{1,0:T(8,128)(2,1)}, bf16[64,128,128]{2,1,0:T(8,128)(2,1)}, bf16[64,128,128]{2,1,0:T(8,128)(2,1)}) custom-call(bf16[24,8192]{1,0:T(8,128)(2,1)} %get-tuple-element.9.y_ref, bf16[64,128,128]{2,1,0:T(8,128)(2,1)} %get-tuple-element.10.k_ref, bf16[64,128,128]{2,1,0:T(8,128)(2,1)} %get-tuple-element.11.v_ref), custom_call_target="tpu_custom_call" | custom-call | tf_op jit(solution)/shard_map/results/pallas_call | solution.py:760
